TPU v7x, 32 devices: a whole 2x2x4 slice. The times are simulated.
32 devices in a mesh: gx: 4 (over y, x), gy: 4 (over z), gz: 2 (over core).
Axes of the slice: x: 2, y: 2, z: 4, core: 2. Of those that a mesh axis runs over, the one named last changes fastest.
Arguments:
- offsets: float32 [3, 4, 16, 16, 128], P(None, 'gx', 'gy', 'gz'), may hold values from 0 to 10
- history: float32 [6, 4, 16, 16, 128], P(None, 'gx', 'gy', 'gz'), may hold values from -0.6 to 0.6
- occupied: int32 [4, 16, 16, 128], P('gx', 'gy', 'gz'), may hold values from 0 to 1, as said below
- species: int32 [4, 16, 16, 128], P('gx', 'gy', 'gz'), may hold values from 0 to 3
- chi_table: float32 [4], replicated, may hold values from 3 to 8
- eta_table: float32 [4], replicated, may hold values from 6 to 16
- gamma_table: float32 [4], replicated, may hold values from 0.5 to 1
Outputs:
- charge: float32 [4, 16, 16, 128], P('gx', 'gy', 'gz')
- residual: float32 [4, 16, 16, 128], P('gx', 'gy', 'gz')
Inputs may be any that keep to these rules, and one draw needn't show every extreme that they name: `occupied`: slot 0 of every cell holds an atom.
All inputs are finite; a program needn't handle non-finite values.
Results may differ from a plain program's by a relative error of at most 0.0003.
Values sent between devices are 32-bit elements; how exact they have to be, the bound alone decides.
No kernel may reach another device: no remote copies, remote signals or barrier semaphores. Data moves between devices by JAX's collectives and lax.ppermute only.
A program may use at most 64 MiB of HBM per device.

v0:
```python
import jax
import jax.numpy as jnp
from jax import lax
from jax.sharding import PartitionSpec as P

EDGE = 10.0
CUTOFF = 10.0
COULOMB = 14.4
extrapolate_weights = (22.0 / 7.0, -55.0 / 14.0, 55.0 / 21.0, -22.0 / 21.0, 5.0 / 21.0, -1.0 / 42.0)


def with_halo(block, sides, width):
    for axis, dim in sides:
        count = lax.axis_size(axis)
        forward = [(i, i + 1) for i in range(count - 1)]
        forward.append((count - 1, 0))
        backward = [(target, source) for source, target in forward]
        low = lax.ppermute(
            lax.slice_in_dim(block, block.shape[dim] - width, None, axis=dim), axis, forward
        )
        high = lax.ppermute(lax.slice_in_dim(block, 0, width, axis=dim), axis, backward)
        block = jnp.concatenate([low, block, high], axis=dim)
    return block


def lookup(species, values_table):
    match = species[..., None] == jnp.arange(values_table.shape[0], dtype=jnp.int32)
    return jnp.sum(jnp.where(match, values_table, jnp.float32(0.0)), axis=-1)


def pair_kernel(target, source, shifts):
    delta_x = source[0][..., None, :] + shifts[0] - target[0][..., :, None]
    delta_y = source[1][..., None, :] + shifts[1] - target[1][..., :, None]
    delta_z = source[2][..., None, :] + shifts[2] - target[2][..., :, None]
    square = delta_x * delta_x + delta_y * delta_y + delta_z * delta_z
    radius = jnp.sqrt(square)
    ratio = radius / CUTOFF
    fourth = ratio * ratio * ratio * ratio
    polynom = 1.0 + fourth * (-35.0 + ratio * (84.0 + ratio * (-70.0 + 20.0 * ratio)))
    tapered = jnp.where(ratio < 1.0, polynom, 0.0)
    return tapered * (square * radius + target[4][..., :, None] * source[4][..., None, :]) ** (
        -1.0 / 3.0
    )


def pair_sum(target, source, shifts):
    kernel = pair_kernel(target, source, shifts)
    return jnp.sum(kernel * source[3][..., None, :], axis=-1)


def coulomb(padded, fields):
    layers, cells_x, cells_y, cells_z, slots_per = fields.shape

    def one_offset(offset_index, summed):
        step_x = offset_index // 9 - 1
        step_y = offset_index // 3 % 3 - 1
        step_z = offset_index % 3 - 1
        zero_start = jnp.int32(0)
        source = lax.dynamic_slice(
            padded,
            (zero_start, 1 + step_x, 1 + step_y, 1 + step_z, zero_start),
            (layers, cells_x, cells_y, cells_z, slots_per),
        )
        shifts = (
            step_x.astype(jnp.float32) * EDGE,
            step_y.astype(jnp.float32) * EDGE,
            step_z.astype(jnp.float32) * EDGE,
        )
        return summed + pair_sum(fields, source, shifts)

    start_sum = jnp.zeros((cells_x, cells_y, cells_z, slots_per), jnp.float32)
    return lax.fori_loop(0, 27, one_offset, start_sum)


def body(offsets, history, occupied, species, chi_table, eta_table, gamma_table):
    weight = occupied.astype(jnp.float32)
    predicted = extrapolate_weights[0] * history[0]
    for level in range(1, 6):
        predicted = predicted + extrapolate_weights[level] * history[level]
    predicted = weight * predicted
    chi = lookup(species, chi_table)
    eta = lookup(species, eta_table)
    gam = lookup(species, gamma_table)
    shield = gam ** (-1.5)
    fields = jnp.concatenate([offsets, predicted[None], shield[None]], axis=0)
    padded = with_halo(fields, (("gx", 1), ("gy", 2), ("gz", 3)), 1)
    summed = coulomb(padded, fields)
    potential = COULOMB * (summed - (shield * shield) ** (-1.0 / 3.0) * predicted)
    electroneg = chi + eta * predicted + potential
    atom_count, elec_sum, charge_sum, scaled_sum, inverse_sum = lax.psum(
        (
            jnp.sum(weight),
            jnp.sum(weight * electroneg),
            jnp.sum(predicted),
            jnp.sum(weight * electroneg / eta),
            jnp.sum(weight / eta),
        ),
        ("gx", "gy", "gz"),
    )
    chem_potential = elec_sum / atom_count
    stepped = weight * (predicted - (electroneg - chem_potential) / eta)
    stepped_total = charge_sum - scaled_sum + chem_potential * inverse_sum
    charge = weight * (stepped - stepped_total / atom_count)
    residual = weight * (electroneg - chem_potential)
    return (charge, residual)


def solution(mesh):
    return jax.shard_map(
        body,
        mesh=mesh,
        in_specs=(
            P(None, "gx", "gy", "gz", None),
            P(None, "gx", "gy", "gz", None),
            P("gx", "gy", "gz", None),
            P("gx", "gy", "gz", None),
            P(),
            P(),
            P(),
        ),
        out_specs=(P("gx", "gy", "gz", None), P("gx", "gy", "gz", None)),
        check_vma=False,
    )
```

profile of v0, /device:TPU:0, one launch (start us, length us, event | category | flops | bytes accessed | tf_op | source)
XLA Modules:
  0.0 243.8 jit_solution(8535333007638683315)
XLA Ops:
  0.6 0.8 select_reduce_fusion
  1.5 1.4 fusion.27
  2.9 0.8 pad_maximum_fusion.1
  3.7 3.0 %collective-permute-start = (f32[5,1,4,8,128]{4,3,2,1,0:T(8,128)S(1)}, f32[5,1,4,8,128]{4,3,2,1,0:T(8,128)S(1)}, u32[]{:S(2)}, u32[]{:S(2)}) collective-permute-start(f32[5,1,4,8,128]{4,3,2,1,0:T(8,128)S(1)} %pad_maximum_fusion.1), channel_id=1, source_target_pairs={{0,8},{8,16},{16,24},{24,0},{1,9},{9,17},{17,25},{25,1},{2,10},{10... | collective-permute-start | bytes 245768 | tf_op jit(solution)/shard_map/ppermute | solution.py:18
  6.7 1.0 collective-permute-start.1
  7.7 2.7 %collective-permute-done = f32[5,1,4,8,128]{4,3,2,1,0:T(8,128)S(1)} collective-permute-done((f32[5,1,4,8,128]{4,3,2,1,0:T(8,128)S(1)}, f32[5,1,4,8,128]{4,3,2,1,0:T(8,128)S(1)}, u32[]{:S(2)}, u32[]{:S(2)}) %collective-permute-start) | collective-permute-done | bytes 81952 | tf_op jit(solution)/shard_map/ppermute | solution.py:18
  10.4 1.7 collective-permute-done.1
  12.1 0.7 pad_maximum_fusion.6
  12.8 1.6 collective-permute-start.2
  14.5 2.2 collective-permute-start.3
  16.7 2.5 %collective-permute-done.2 = f32[5,3,1,8,128]{4,3,2,1,0:T(8,128)S(1)} collective-permute-done((f32[5,3,1,8,128]{4,3,2,1,0:T(8,128)S(1)}, f32[5,3,1,8,128]{4,3,2,1,0:T(8,128)S(1)}, u32[]{:S(2)}, u32[]{:S(2)}) %collective-permute-start.2) | collective-permute-done | bytes 61472 | tf_op jit(solution)/shard_map/ppermute | solution.py:18
  19.2 0.1 collective-permute-done.3
  19.4 0.1 collective-permute-start.4
  19.5 0.5 collective-permute-start.5
  20.0 0.7 collective-permute-done.4
  20.7 0.2 collective-permute-done.5
  20.9 0.2 pad_maximum_fusion
  21.0 178.2 %while.19 = (s32[]{:T(128)}, f32[1,4,8,128]{3,2,1,0:T(8,128)S(1)}, f32[5,3,6,10,128]{4,3,2,1,0:T(8,128)S(1)}, f32[3,1,4,8,128]{4,3,2,1,0:T(8,128)S(1)}, f32[1,4,...) while((s32[]{:T(128)}, f32[1,4,8,128]{3,2,1,0:T(8,128)S(1)}, ...), condition=%wide.region_5.6_spmd.clone, body=%wide.region_3.5_spmd.clone.sunk | while | flops 14696497 | bytes 475823 | solution.py:72
  21.2 6.4 %fusion.31 = f32[4,8,128]{2,1,0:T(8,128)S(1)} fusion(f32[4,8,128]{2,1,0:T(8,128)S(1)} %get-tuple-element.328, f32[4,8,128]{2,1,0:T(8,128)S(1)} %get-tuple-element.329, f32[4,8,128]{2,1,0:T(8,128)S(1)} %bitcast.66, f32[4,8,128]{2,1,0:T(8,128)S(1)} %get-tuple-element.330, f32[4,8,128]{2,1,0:T(8,128)S(1)} %get-tuple-element.331, ...), kind=kLoop, calls=%fused_computation.18.clone.1 | loop fusion | flops 14675968 | bytes 163840 | tf_op jit(solution)/shard_map/while/body/eval_jaxpr/reduce_sum | solution.py:48
  27.8 6.4 %fusion.31 = f32[4,8,128]{2,1,0:T(8,128)S(1)} fusion(f32[4,8,128]{2,1,0:T(8,128)S(1)} %get-tuple-element.328, f32[4,8,128]{2,1,0:T(8,128)S(1)} %get-tuple-element.329, f32[4,8,128]{2,1,0:T(8,128)S(1)} %bitcast.66, f32[4,8,128]{2,1,0:T(8,128)S(1)} %get-tuple-element.330, f32[4,8,128]{2,1,0:T(8,128)S(1)} %get-tuple-element.331, ...), kind=kLoop, calls=%fused_computation.18.clone.1 | loop fusion | flops 14675968 | bytes 163840 | tf_op jit(solution)/shard_map/while/body/eval_jaxpr/reduce_sum | solution.py:48
  34.4 6.4 %fusion.31 = f32[4,8,128]{2,1,0:T(8,128)S(1)} fusion(f32[4,8,128]{2,1,0:T(8,128)S(1)} %get-tuple-element.328, f32[4,8,128]{2,1,0:T(8,128)S(1)} %get-tuple-element.329, f32[4,8,128]{2,1,0:T(8,128)S(1)} %bitcast.66, f32[4,8,128]{2,1,0:T(8,128)S(1)} %get-tuple-element.330, f32[4,8,128]{2,1,0:T(8,128)S(1)} %get-tuple-element.331, ...), kind=kLoop, calls=%fused_computation.18.clone.1 | loop fusion | flops 14675968 | bytes 163840 | tf_op jit(solution)/shard_map/while/body/eval_jaxpr/reduce_sum | solution.py:48
  41.0 6.4 %fusion.31 = f32[4,8,128]{2,1,0:T(8,128)S(1)} fusion(f32[4,8,128]{2,1,0:T(8,128)S(1)} %get-tuple-element.328, f32[4,8,128]{2,1,0:T(8,128)S(1)} %get-tuple-element.329, f32[4,8,128]{2,1,0:T(8,128)S(1)} %bitcast.66, f32[4,8,128]{2,1,0:T(8,128)S(1)} %get-tuple-element.330, f32[4,8,128]{2,1,0:T(8,128)S(1)} %get-tuple-element.331, ...), kind=kLoop, calls=%fused_computation.18.clone.1 | loop fusion | flops 14675968 | bytes 163840 | tf_op jit(solution)/shard_map/while/body/eval_jaxpr/reduce_sum | solution.py:48
  47.6 6.4 %fusion.31 = f32[4,8,128]{2,1,0:T(8,128)S(1)} fusion(f32[4,8,128]{2,1,0:T(8,128)S(1)} %get-tuple-element.328, f32[4,8,128]{2,1,0:T(8,128)S(1)} %get-tuple-element.329, f32[4,8,128]{2,1,0:T(8,128)S(1)} %bitcast.66, f32[4,8,128]{2,1,0:T(8,128)S(1)} %get-tuple-element.330, f32[4,8,128]{2,1,0:T(8,128)S(1)} %get-tuple-element.331, ...), kind=kLoop, calls=%fused_computation.18.clone.1 | loop fusion | flops 14675968 | bytes 163840 | tf_op jit(solution)/shard_map/while/body/eval_jaxpr/reduce_sum | solution.py:48
  54.2 6.4 %fusion.31 = f32[4,8,128]{2,1,0:T(8,128)S(1)} fusion(f32[4,8,128]{2,1,0:T(8,128)S(1)} %get-tuple-element.328, f32[4,8,128]{2,1,0:T(8,128)S(1)} %get-tuple-element.329, f32[4,8,128]{2,1,0:T(8,128)S(1)} %bitcast.66, f32[4,8,128]{2,1,0:T(8,128)S(1)} %get-tuple-element.330, f32[4,8,128]{2,1,0:T(8,128)S(1)} %get-tuple-element.331, ...), kind=kLoop, calls=%fused_computation.18.clone.1 | loop fusion | flops 14675968 | bytes 163840 | tf_op jit(solution)/shard_map/while/body/eval_jaxpr/reduce_sum | solution.py:48
  60.8 6.4 %fusion.31 = f32[4,8,128]{2,1,0:T(8,128)S(1)} fusion(f32[4,8,128]{2,1,0:T(8,128)S(1)} %get-tuple-element.328, f32[4,8,128]{2,1,0:T(8,128)S(1)} %get-tuple-element.329, f32[4,8,128]{2,1,0:T(8,128)S(1)} %bitcast.66, f32[4,8,128]{2,1,0:T(8,128)S(1)} %get-tuple-element.330, f32[4,8,128]{2,1,0:T(8,128)S(1)} %get-tuple-element.331, ...), kind=kLoop, calls=%fused_computation.18.clone.1 | loop fusion | flops 14675968 | bytes 163840 | tf_op jit(solution)/shard_map/while/body/eval_jaxpr/reduce_sum | solution.py:48
  67.4 6.4 %fusion.31 = f32[4,8,128]{2,1,0:T(8,128)S(1)} fusion(f32[4,8,128]{2,1,0:T(8,128)S(1)} %get-tuple-element.328, f32[4,8,128]{2,1,0:T(8,128)S(1)} %get-tuple-element.329, f32[4,8,128]{2,1,0:T(8,128)S(1)} %bitcast.66, f32[4,8,128]{2,1,0:T(8,128)S(1)} %get-tuple-element.330, f32[4,8,128]{2,1,0:T(8,128)S(1)} %get-tuple-element.331, ...), kind=kLoop, calls=%fused_computation.18.clone.1 | loop fusion | flops 14675968 | bytes 163840 | tf_op jit(solution)/shard_map/while/body/eval_jaxpr/reduce_sum | solution.py:48
  74.0 6.4 %fusion.31 = f32[4,8,128]{2,1,0:T(8,128)S(1)} fusion(f32[4,8,128]{2,1,0:T(8,128)S(1)} %get-tuple-element.328, f32[4,8,128]{2,1,0:T(8,128)S(1)} %get-tuple-element.329, f32[4,8,128]{2,1,0:T(8,128)S(1)} %bitcast.66, f32[4,8,128]{2,1,0:T(8,128)S(1)} %get-tuple-element.330, f32[4,8,128]{2,1,0:T(8,128)S(1)} %get-tuple-element.331, ...), kind=kLoop, calls=%fused_computation.18.clone.1 | loop fusion | flops 14675968 | bytes 163840 | tf_op jit(solution)/shard_map/while/body/eval_jaxpr/reduce_sum | solution.py:48
  80.6 6.4 %fusion.31 = f32[4,8,128]{2,1,0:T(8,128)S(1)} fusion(f32[4,8,128]{2,1,0:T(8,128)S(1)} %get-tuple-element.328, f32[4,8,128]{2,1,0:T(8,128)S(1)} %get-tuple-element.329, f32[4,8,128]{2,1,0:T(8,128)S(1)} %bitcast.66, f32[4,8,128]{2,1,0:T(8,128)S(1)} %get-tuple-element.330, f32[4,8,128]{2,1,0:T(8,128)S(1)} %get-tuple-element.331, ...), kind=kLoop, calls=%fused_computation.18.clone.1 | loop fusion | flops 14675968 | bytes 163840 | tf_op jit(solution)/shard_map/while/body/eval_jaxpr/reduce_sum | solution.py:48
  87.2 6.4 %fusion.31 = f32[4,8,128]{2,1,0:T(8,128)S(1)} fusion(f32[4,8,128]{2,1,0:T(8,128)S(1)} %get-tuple-element.328, f32[4,8,128]{2,1,0:T(8,128)S(1)} %get-tuple-element.329, f32[4,8,128]{2,1,0:T(8,128)S(1)} %bitcast.66, f32[4,8,128]{2,1,0:T(8,128)S(1)} %get-tuple-element.330, f32[4,8,128]{2,1,0:T(8,128)S(1)} %get-tuple-element.331, ...), kind=kLoop, calls=%fused_computation.18.clone.1 | loop fusion | flops 14675968 | bytes 163840 | tf_op jit(solution)/shard_map/while/body/eval_jaxpr/reduce_sum | solution.py:48
  93.8 6.4 %fusion.31 = f32[4,8,128]{2,1,0:T(8,128)S(1)} fusion(f32[4,8,128]{2,1,0:T(8,128)S(1)} %get-tuple-element.328, f32[4,8,128]{2,1,0:T(8,128)S(1)} %get-tuple-element.329, f32[4,8,128]{2,1,0:T(8,128)S(1)} %bitcast.66, f32[4,8,128]{2,1,0:T(8,128)S(1)} %get-tuple-element.330, f32[4,8,128]{2,1,0:T(8,128)S(1)} %get-tuple-element.331, ...), kind=kLoop, calls=%fused_computation.18.clone.1 | loop fusion | flops 14675968 | bytes 163840 | tf_op jit(solution)/shard_map/while/body/eval_jaxpr/reduce_sum | solution.py:48
  100.4 6.4 %fusion.31 = f32[4,8,128]{2,1,0:T(8,128)S(1)} fusion(f32[4,8,128]{2,1,0:T(8,128)S(1)} %get-tuple-element.328, f32[4,8,128]{2,1,0:T(8,128)S(1)} %get-tuple-element.329, f32[4,8,128]{2,1,0:T(8,128)S(1)} %bitcast.66, f32[4,8,128]{2,1,0:T(8,128)S(1)} %get-tuple-element.330, f32[4,8,128]{2,1,0:T(8,128)S(1)} %get-tuple-element.331, ...), kind=kLoop, calls=%fused_computation.18.clone.1 | loop fusion | flops 14675968 | bytes 163840 | tf_op jit(solution)/shard_map/while/body/eval_jaxpr/reduce_sum | solution.py:48
  107.0 6.4 %fusion.31 = f32[4,8,128]{2,1,0:T(8,128)S(1)} fusion(f32[4,8,128]{2,1,0:T(8,128)S(1)} %get-tuple-element.328, f32[4,8,128]{2,1,0:T(8,128)S(1)} %get-tuple-element.329, f32[4,8,128]{2,1,0:T(8,128)S(1)} %bitcast.66, f32[4,8,128]{2,1,0:T(8,128)S(1)} %get-tuple-element.330, f32[4,8,128]{2,1,0:T(8,128)S(1)} %get-tuple-element.331, ...), kind=kLoop, calls=%fused_computation.18.clone.1 | loop fusion | flops 14675968 | bytes 163840 | tf_op jit(solution)/shard_map/while/body/eval_jaxpr/reduce_sum | solution.py:48
  113.6 6.4 %fusion.31 = f32[4,8,128]{2,1,0:T(8,128)S(1)} fusion(f32[4,8,128]{2,1,0:T(8,128)S(1)} %get-tuple-element.328, f32[4,8,128]{2,1,0:T(8,128)S(1)} %get-tuple-element.329, f32[4,8,128]{2,1,0:T(8,128)S(1)} %bitcast.66, f32[4,8,128]{2,1,0:T(8,128)S(1)} %get-tuple-element.330, f32[4,8,128]{2,1,0:T(8,128)S(1)} %get-tuple-element.331, ...), kind=kLoop, calls=%fused_computation.18.clone.1 | loop fusion | flops 14675968 | bytes 163840 | tf_op jit(solution)/shard_map/while/body/eval_jaxpr/reduce_sum | solution.py:48
  120.2 6.4 %fusion.31 = f32[4,8,128]{2,1,0:T(8,128)S(1)} fusion(f32[4,8,128]{2,1,0:T(8,128)S(1)} %get-tuple-element.328, f32[4,8,128]{2,1,0:T(8,128)S(1)} %get-tuple-element.329, f32[4,8,128]{2,1,0:T(8,128)S(1)} %bitcast.66, f32[4,8,128]{2,1,0:T(8,128)S(1)} %get-tuple-element.330, f32[4,8,128]{2,1,0:T(8,128)S(1)} %get-tuple-element.331, ...), kind=kLoop, calls=%fused_computation.18.clone.1 | loop fusion | flops 14675968 | bytes 163840 | tf_op jit(solution)/shard_map/while/body/eval_jaxpr/reduce_sum | solution.py:48
  126.8 6.4 %fusion.31 = f32[4,8,128]{2,1,0:T(8,128)S(1)} fusion(f32[4,8,128]{2,1,0:T(8,128)S(1)} %get-tuple-element.328, f32[4,8,128]{2,1,0:T(8,128)S(1)} %get-tuple-element.329, f32[4,8,128]{2,1,0:T(8,128)S(1)} %bitcast.66, f32[4,8,128]{2,1,0:T(8,128)S(1)} %get-tuple-element.330, f32[4,8,128]{2,1,0:T(8,128)S(1)} %get-tuple-element.331, ...), kind=kLoop, calls=%fused_computation.18.clone.1 | loop fusion | flops 14675968 | bytes 163840 | tf_op jit(solution)/shard_map/while/body/eval_jaxpr/reduce_sum | solution.py:48
  133.4 6.4 %fusion.31 = f32[4,8,128]{2,1,0:T(8,128)S(1)} fusion(f32[4,8,128]{2,1,0:T(8,128)S(1)} %get-tuple-element.328, f32[4,8,128]{2,1,0:T(8,128)S(1)} %get-tuple-element.329, f32[4,8,128]{2,1,0:T(8,128)S(1)} %bitcast.66, f32[4,8,128]{2,1,0:T(8,128)S(1)} %get-tuple-element.330, f32[4,8,128]{2,1,0:T(8,128)S(1)} %get-tuple-element.331, ...), kind=kLoop, calls=%fused_computation.18.clone.1 | loop fusion | flops 14675968 | bytes 163840 | tf_op jit(solution)/shard_map/while/body/eval_jaxpr/reduce_sum | solution.py:48
  140.0 6.4 %fusion.31 = f32[4,8,128]{2,1,0:T(8,128)S(1)} fusion(f32[4,8,128]{2,1,0:T(8,128)S(1)} %get-tuple-element.328, f32[4,8,128]{2,1,0:T(8,128)S(1)} %get-tuple-element.329, f32[4,8,128]{2,1,0:T(8,128)S(1)} %bitcast.66, f32[4,8,128]{2,1,0:T(8,128)S(1)} %get-tuple-element.330, f32[4,8,128]{2,1,0:T(8,128)S(1)} %get-tuple-element.331, ...), kind=kLoop, calls=%fused_computation.18.clone.1 | loop fusion | flops 14675968 | bytes 163840 | tf_op jit(solution)/shard_map/while/body/eval_jaxpr/reduce_sum | solution.py:48
  146.6 6.4 %fusion.31 = f32[4,8,128]{2,1,0:T(8,128)S(1)} fusion(f32[4,8,128]{2,1,0:T(8,128)S(1)} %get-tuple-element.328, f32[4,8,128]{2,1,0:T(8,128)S(1)} %get-tuple-element.329, f32[4,8,128]{2,1,0:T(8,128)S(1)} %bitcast.66, f32[4,8,128]{2,1,0:T(8,128)S(1)} %get-tuple-element.330, f32[4,8,128]{2,1,0:T(8,128)S(1)} %get-tuple-element.331, ...), kind=kLoop, calls=%fused_computation.18.clone.1 | loop fusion | flops 14675968 | bytes 163840 | tf_op jit(solution)/shard_map/while/body/eval_jaxpr/reduce_sum | solution.py:48
  153.2 6.4 %fusion.31 = f32[4,8,128]{2,1,0:T(8,128)S(1)} fusion(f32[4,8,128]{2,1,0:T(8,128)S(1)} %get-tuple-element.328, f32[4,8,128]{2,1,0:T(8,128)S(1)} %get-tuple-element.329, f32[4,8,128]{2,1,0:T(8,128)S(1)} %bitcast.66, f32[4,8,128]{2,1,0:T(8,128)S(1)} %get-tuple-element.330, f32[4,8,128]{2,1,0:T(8,128)S(1)} %get-tuple-element.331, ...), kind=kLoop, calls=%fused_computation.18.clone.1 | loop fusion | flops 14675968 | bytes 163840 | tf_op jit(solution)/shard_map/while/body/eval_jaxpr/reduce_sum | solution.py:48
  159.8 6.4 %fusion.31 = f32[4,8,128]{2,1,0:T(8,128)S(1)} fusion(f32[4,8,128]{2,1,0:T(8,128)S(1)} %get-tuple-element.328, f32[4,8,128]{2,1,0:T(8,128)S(1)} %get-tuple-element.329, f32[4,8,128]{2,1,0:T(8,128)S(1)} %bitcast.66, f32[4,8,128]{2,1,0:T(8,128)S(1)} %get-tuple-element.330, f32[4,8,128]{2,1,0:T(8,128)S(1)} %get-tuple-element.331, ...), kind=kLoop, calls=%fused_computation.18.clone.1 | loop fusion | flops 14675968 | bytes 163840 | tf_op jit(solution)/shard_map/while/body/eval_jaxpr/reduce_sum | solution.py:48
  166.4 6.4 %fusion.31 = f32[4,8,128]{2,1,0:T(8,128)S(1)} fusion(f32[4,8,128]{2,1,0:T(8,128)S(1)} %get-tuple-element.328, f32[4,8,128]{2,1,0:T(8,128)S(1)} %get-tuple-element.329, f32[4,8,128]{2,1,0:T(8,128)S(1)} %bitcast.66, f32[4,8,128]{2,1,0:T(8,128)S(1)} %get-tuple-element.330, f32[4,8,128]{2,1,0:T(8,128)S(1)} %get-tuple-element.331, ...), kind=kLoop, calls=%fused_computation.18.clone.1 | loop fusion | flops 14675968 | bytes 163840 | tf_op jit(solution)/shard_map/while/body/eval_jaxpr/reduce_sum | solution.py:48
  172.9 6.4 %fusion.31 = f32[4,8,128]{2,1,0:T(8,128)S(1)} fusion(f32[4,8,128]{2,1,0:T(8,128)S(1)} %get-tuple-element.328, f32[4,8,128]{2,1,0:T(8,128)S(1)} %get-tuple-element.329, f32[4,8,128]{2,1,0:T(8,128)S(1)} %bitcast.66, f32[4,8,128]{2,1,0:T(8,128)S(1)} %get-tuple-element.330, f32[4,8,128]{2,1,0:T(8,128)S(1)} %get-tuple-element.331, ...), kind=kLoop, calls=%fused_computation.18.clone.1 | loop fusion | flops 14675968 | bytes 163840 | tf_op jit(solution)/shard_map/while/body/eval_jaxpr/reduce_sum | solution.py:48
  179.5 6.4 %fusion.31 = f32[4,8,128]{2,1,0:T(8,128)S(1)} fusion(f32[4,8,128]{2,1,0:T(8,128)S(1)} %get-tuple-element.328, f32[4,8,128]{2,1,0:T(8,128)S(1)} %get-tuple-element.329, f32[4,8,128]{2,1,0:T(8,128)S(1)} %bitcast.66, f32[4,8,128]{2,1,0:T(8,128)S(1)} %get-tuple-element.330, f32[4,8,128]{2,1,0:T(8,128)S(1)} %get-tuple-element.331, ...), kind=kLoop, calls=%fused_computation.18.clone.1 | loop fusion | flops 14675968 | bytes 163840 | tf_op jit(solution)/shard_map/while/body/eval_jaxpr/reduce_sum | solution.py:48
  186.1 6.4 %fusion.31 = f32[4,8,128]{2,1,0:T(8,128)S(1)} fusion(f32[4,8,128]{2,1,0:T(8,128)S(1)} %get-tuple-element.328, f32[4,8,128]{2,1,0:T(8,128)S(1)} %get-tuple-element.329, f32[4,8,128]{2,1,0:T(8,128)S(1)} %bitcast.66, f32[4,8,128]{2,1,0:T(8,128)S(1)} %get-tuple-element.330, f32[4,8,128]{2,1,0:T(8,128)S(1)} %get-tuple-element.331, ...), kind=kLoop, calls=%fused_computation.18.clone.1 | loop fusion | flops 14675968 | bytes 163840 | tf_op jit(solution)/shard_map/while/body/eval_jaxpr/reduce_sum | solution.py:48
  192.7 6.4 %fusion.31 = f32[4,8,128]{2,1,0:T(8,128)S(1)} fusion(f32[4,8,128]{2,1,0:T(8,128)S(1)} %get-tuple-element.328, f32[4,8,128]{2,1,0:T(8,128)S(1)} %get-tuple-element.329, f32[4,8,128]{2,1,0:T(8,128)S(1)} %bitcast.66, f32[4,8,128]{2,1,0:T(8,128)S(1)} %get-tuple-element.330, f32[4,8,128]{2,1,0:T(8,128)S(1)} %get-tuple-element.331, ...), kind=kLoop, calls=%fused_computation.18.clone.1 | loop fusion | flops 14675968 | bytes 163840 | tf_op jit(solution)/shard_map/while/body/eval_jaxpr/reduce_sum | solution.py:48
  199.2 0.7 fusion.24
  200.0 39.4 %all-reduce = (f32[]{:T(128)}, f32[]{:T(128)}, f32[]{:T(128)}, f32[]{:T(128)}, f32[]{:T(128)}) all-reduce(f32[]{:T(128)} %get-tuple-element.268, f32[]{:T(128)} %get-tuple-element.246, f32[]{:T(128)} %get-tuple-element.247, f32[]{:T(128)} %get-tuple-element.248, ...), channel_id=1, replica_groups=mesh['gx'=4,'gy'=4,'gz'=2] {'gx','gy','gz'}, use_global_device_ids=true, to_apply=%region_11.12 | all-reduce | flops 5 | bytes 40 | tf_op jit(solution)/shard_map/psum | solution.py:90
  243.2 0.6 convert_multiply_fusion
  (61 shorter events, 1.3 us)
Async XLA Ops:
  0.6 18.7 %copy-start = (f32[3,1,4,8,128]{4,3,2,1,0:T(8,128)S(1)}, f32[3,1,4,8,128]{4,3,2,1,0:T(8,128)}, u32[]{:S(2)}) copy-start(f32[3,1,4,8,128]{4,3,2,1,0:T(8,128)} %param.9) | copy-start | bytes 147460
  3.7 6.7 %collective-permute-start = (f32[5,1,4,8,128]{4,3,2,1,0:T(8,128)S(1)}, f32[5,1,4,8,128]{4,3,2,1,0:T(8,128)S(1)}, u32[]{:S(2)}, u32[]{:S(2)}) collective-permute-start(f32[5,1,4,8,128]{4,3,2,1,0:T(8,128)S(1)} %pad_maximum_fusion.1), channel_id=1, source_target_pairs={{0,8},{8,16},{16,24},{24,0},{1,9},{9,17},{17,25},{25,1},{2,10},{10... | collective-permute-start | bytes 245768 | tf_op jit(solution)/shard_map/ppermute | solution.py:18
  6.7 5.4 %collective-permute-start.1 = (f32[5,1,4,8,128]{4,3,2,1,0:T(8,128)S(1)}, f32[5,1,4,8,128]{4,3,2,1,0:T(8,128)S(1)}, u32[]{:S(2)}, u32[]{:S(2)}) collective-permute-start(f32[5,1,4,8,128]{4,3,2,1,0:T(8,128)S(1)} %pad_maximum_fusion.1), channel_id=1, source_target_pairs={{8,0},{16,8},{24,16},{0,24},{9,1},{17,9},{25,17},{1,25},{10,2},{18... | collective-permute-start | bytes 245768 | tf_op jit(solution)/shard_map/ppermute | solution.py:21
  12.8 6.4 %collective-permute-start.2 = (f32[5,3,1,8,128]{4,3,2,1,0:T(8,128)S(1)}, f32[5,3,1,8,128]{4,3,2,1,0:T(8,128)S(1)}, u32[]{:S(2)}, u32[]{:S(2)}) collective-permute-start(f32[5,3,1,8,128]{4,3,2,1,0:T(8,128)S(1)} %get-tuple-element.283), channel_id=1, source_target_pairs={{0,2},{2,4},{4,6},{6,0},{1,3},{3,5},{5,7},{7,1},{8,10},{10,12},{12... | collective-permute-start | bytes 184328 | tf_op jit(solution)/shard_map/ppermute | solution.py:18
  14.5 4.9 %collective-permute-start.3 = (f32[5,3,1,8,128]{4,3,2,1,0:T(8,128)S(1)}, f32[5,3,1,8,128]{4,3,2,1,0:T(8,128)S(1)}, u32[]{:S(2)}, u32[]{:S(2)}) collective-permute-start(f32[5,3,1,8,128]{4,3,2,1,0:T(8,128)S(1)} %get-tuple-element.284), channel_id=1, source_target_pairs={{2,0},{4,2},{6,4},{0,6},{3,1},{5,3},{7,5},{1,7},{10,8},{12,10},{14... | collective-permute-start | bytes 184328 | tf_op jit(solution)/shard_map/ppermute | solution.py:21
  19.4 1.3 collective-permute-start.4
  19.5 1.4 collective-permute-start.5
  21.0 178.2 %copy-start.1 = (s32[1,4,8,128]{3,2,1,0:T(8,128)S(1)}, s32[1,4,8,128]{3,2,1,0:T(8,128)}, u32[]{:S(2)}) copy-start(s32[1,4,8,128]{3,2,1,0:T(8,128)} %param.11) | copy-start | bytes 49156
where the time goes:
time: 244 us
  other arithmetic  180 us (74%)
  blocking collectives  39.4 us (16%)
  starting transfers between devices  8.42 us (3%)
  waiting for transfers between devices  7.9 us (3%)
  between operations  4.56 us (2%)
  loops' own time  3.4 us (1%)
    reduce_sum x27, other arithmetic, pair_sum(): return jnp.sum(kernel * source[3][..., None, :], axis=-1)  174 us
    psum x1, blocking collectives, body(): lax.psum((jnp.sum(weight), jnp.sum(weight * electroneg), jnp.sum(predicte...  39.4 us
    ppermute x3, waiting for transfers between devices, with_halo(): lax.ppermute(lax.slice_in_dim(block, block.shape[dim] - width, None, axis...  5.88 us
  transfers between devices with their start and end apart: 6, of which 6 were waited for; matrix products, arithmetic and copies ran while one was open for 0% of the time, Pallas kernels for 0%

commit v1 on v0

v1 whole, which is shorter than its diff:
```python
import math

import jax
import jax.numpy as jnp
import numpy as np
from jax import lax
from jax.experimental import pallas as pl
from jax.experimental.pallas import tpu as pltpu
from jax.sharding import PartitionSpec as P

EDGE = 10.0
COULOMB = 14.4
WEIGHTS = (22.0 / 7.0, -55.0 / 14.0, 55.0 / 21.0, -22.0 / 21.0, 5.0 / 21.0, -1.0 / 42.0)
FIELDS = 8
SHELL = [(a, 1, c) for a in (-1, 0, 1) for c in (-1, 0, 1)]
SHELL += [(a, 0, 1) for a in (-1, 0, 1)] + [(1, 0, 0)]
NP = len(SHELL)
F32 = jnp.float32
BF16 = jnp.bfloat16


def ring(n, k):
    return [(i, (i + k) % n) for i in range(n)]


def pieces_of(x):
    hi = x.astype(BF16)
    rest = x - hi.astype(F32)
    mid = rest.astype(BF16)
    low = (rest - mid.astype(F32)).astype(BF16)
    return hi, mid, low


def pick(species, table_ref):
    out = jnp.full(species.shape, table_ref[0], F32)
    for t in range(1, table_ref.shape[0]):
        out = jnp.where(species == t, table_ref[t], out)
    return out


def pack_kernel(off_ref, hist_ref, occ_ref, spec_ref, chi_ref, eta_ref, gam_ref, cell_ref, aux_ref, part_ref):
    cells, slots = occ_ref.shape
    weight = occ_ref[...].astype(F32)
    species = spec_ref[...]
    predicted = WEIGHTS[0] * hist_ref[0]
    for level in range(1, len(WEIGHTS)):
        predicted = predicted + WEIGHTS[level] * hist_ref[level]
    predicted = weight * predicted
    chi = pick(species, chi_ref)
    eta = pick(species, eta_ref)
    gam = pick(species, gam_ref)
    root = lax.rsqrt(gam)
    shield = root * root * root * (EDGE**-1.5)
    inverse = 1.0 / eta
    base = chi + eta * predicted - COULOMB * gam * predicted
    winv = weight * inverse
    zero = jnp.zeros((1, slots), F32)
    rows = [weight, weight * base, predicted, winv * base, winv]
    rows = [jnp.sum(r, axis=0, keepdims=True) for r in rows] + [zero] * 3
    part_ref[...] = jnp.concatenate(rows, axis=0)
    tri = lax.broadcasted_iota(jnp.int32, (slots, slots), 0) <= lax.broadcasted_iota(jnp.int32, (slots, slots), 1)
    wb = weight.astype(BF16)
    rank = jnp.dot(wb, tri.astype(F32).astype(BF16), preferred_element_type=F32)
    count = jnp.dot(wb, jnp.ones((slots, slots), BF16), preferred_element_type=F32)
    pos = jnp.where(weight > 0, rank - 1.0, -1.0)
    aux_ref[0] = base
    aux_ref[1] = predicted
    aux_ref[2] = inverse
    aux_ref[3] = pos
    fields = [off_ref[d] * (1.0 / EDGE) for d in range(3)] + [predicted, shield, winv, weight, weight]
    row_id = lax.broadcasted_iota(jnp.int32, (slots, slots), 0).astype(F32)
    lane = lax.broadcasted_iota(jnp.int32, (FIELDS, slots), 1).astype(F32)
    sub = lax.broadcasted_iota(jnp.int32, (FIELDS, slots), 0)
    for c in range(cells):
        feat = jnp.concatenate([f[c : c + 1] for f in fields], axis=0)
        hot = jnp.where(row_id == pos[c : c + 1], 1.0, 0.0).astype(BF16)
        parts = jnp.concatenate(pieces_of(feat), axis=0)
        out = lax.dot_general(parts, hot, (((1,), (1,)), ((), ())), preferred_element_type=F32)
        out = out[:FIELDS] + out[FIELDS : 2 * FIELDS] + out[2 * FIELDS :]
        number = jnp.broadcast_to(count[c : c + 1], (FIELDS, slots))
        out = jnp.where((sub == 4) & (lane >= number), 1.0, out)
        cell_ref[c] = jnp.where(sub == 7, number, out)


def pair_kernel(nb, z2, slots, chunk_ref, table_ref, part_ref, *refs):
    planes = refs[:-5]
    out_ref, abc, bbc, acca, accb = refs[-5:]
    nx = len(planes)
    r2 = planes[0].shape[0]
    per = r2 * z2
    nck = slots // 8
    nb1 = nb + 1
    ty, tz = r2 - 1, z2 - 2
    own = [(p, r, z) for p in range(nx) for r in range(ty) for z in range(tz)]
    cell_of = lambda p, r, z: p * per + r * z2 + z
    order = (0, 1, 2, 4, 3)
    for p in range(nx):
        for r in range(r2):
            for z in range(z2):
                cell = planes[p][r, z]
                for k, f in enumerate(order):
                    abc[cell_of(p, r, z), k] = jnp.broadcast_to(cell[f : f + 1], (8, slots))
    for b, (p, r, z) in enumerate(own):
        cell = planes[p][r, z + 1]
        turned = cell.T
        for k, f in enumerate(order):
            wide = jnp.broadcast_to(turned[:, f : f + 1], (slots, slots))
            bbc[b * nck : (b + 1) * nck, k] = wide.reshape(nck, 8, slots)
    blank = jnp.zeros((8, slots), F32)
    for k in range(5):
        bbc[nb * nck, k] = jnp.full((8, slots), 1.0 if k == 3 else 0.0, F32)
    for b in range(nb1):
        for s in range(2):
            for q in range(NP):
                acca[s, b, q] = blank
    for i in range(nb * nck):
        accb[i] = blank

    def value(ai, shift, bf):
        a, y, c = shift
        dx = abc[ai, 0] - bf[0][a]
        dy = abc[ai, 1] - bf[1][y]
        dz = abc[ai, 2] - bf[2][c]
        s = dx * dx + dy * dy + dz * dz
        s = jnp.minimum(jnp.maximum(s, 1e-12), 1.0)
        u = s * lax.rsqrt(s)
        v = 1.0 - u
        v = v * v
        v = v * v
        poly = ((u + 0.5) * u + 0.2) * u + 0.05
        x = s * u + abc[ai, 3] * bf[3]
        return (v * poly) * jnp.exp2(jnp.log2(x) * (-1.0 / 3.0))

    def item(slot, b, c):
        be = jnp.minimum(b, nb - 1)
        bases = [table_ref[a * nb1 + be] for a in range(3)]
        ci = jnp.where(b < nb, b * nck + c, nb * nck)
        raw = [bbc[ci, k] for k in range(5)]
        bf = [{o: (raw[k] - float(o) if o else raw[k]) for o in (-1, 0, 1)} for k in range(3)] + [raw[3]]
        qb = raw[4]
        k = value(bases[1], (0, 0, 0), bf)
        total = k * abc[bases[1], 4]
        for q, (a, y, z) in enumerate(SHELL):
            ai = bases[a + 1] + (y * z2 + z)
            k = value(ai, (a, y, z), bf)
            total = total + k * abc[ai, 4]
            acca[slot, b, q] = acca[slot, b, q] + k * qb
        accb[ci] = total

    def advance(b, c):
        more = c + 1 < chunk_ref[b]
        return jnp.where(more, b, jnp.minimum(b + 1, nb)), jnp.where(more, c + 1, 0)

    def step(_, carry):
        b, c = carry
        item(0, b, c)
        b, c = advance(b, c)
        item(1, b, c)
        return advance(b, c)

    lax.fori_loop(0, chunk_ref[nb1], step, (jnp.int32(0), jnp.int32(0)))

    sums = {}
    for b, (p, r, z) in enumerate(own):
        rows = accb[b * nck : (b + 1) * nck].reshape(slots, slots).T
        folded = rows[:8]
        for i in range(1, nck):
            folded = folded + rows[8 * i : 8 * i + 8]
        key = cell_of(p, r, z + 1)
        sums[key] = sums[key] + folded if key in sums else folded
        for q, (a, y, c) in enumerate(SHELL):
            key = cell_of((p + a) % nx, r + y, z + 1 + c)
            term = acca[0, b, q] + acca[1, b, q]
            sums[key] = sums[key] + term if key in sums else term
    one = jnp.zeros((1, slots), F32)
    two = jnp.zeros((1, slots), F32)
    for p in range(nx):
        for r in range(r2):
            for z in range(z2):
                key = cell_of(p, r, z)
                if key in sums:
                    row = jnp.sum(sums[key], axis=0, keepdims=True)
                    cell = planes[p][r, z]
                    one = one + cell[6:7] * row
                    two = two + cell[5:6] * row
                else:
                    row = jnp.zeros((1, slots), F32)
                out_ref[p, r * z2 + z : r * z2 + z + 1, :] = row
    scale = 2.0 * COULOMB
    part = part_ref[...]
    tail = jnp.concatenate([part[0:1], part[1:2] + scale * one, part[2:3], part[3:4] + scale * two, part[4:8]], axis=0)
    for p in range(nx):
        out_ref[p, per : per + 8, :] = tail


def finish_kernel(sum_ref, aux_ref, occ_ref, part_ref, charge_ref, resid_ref):
    cells, slots = occ_ref.shape
    weight = occ_ref[...].astype(F32)
    row_id = lax.broadcasted_iota(jnp.int32, (slots, slots), 0).astype(F32)
    packed = sum_ref[...]
    pos = aux_ref[3]
    hi, mid, low = [t.astype(F32) for t in pieces_of(packed)]
    lines = []
    for c in range(cells):
        hot = jnp.where(row_id == pos[c : c + 1], 1.0, 0.0).astype(BF16)
        parts = jnp.concatenate([hi[c : c + 1], mid[c : c + 1], low[c : c + 1]] + [jnp.zeros((5, slots), F32)], axis=0)
        out = jnp.dot(parts.astype(BF16), hot, preferred_element_type=F32)
        lines.append(out[0:1] + out[1:2] + out[2:3])
    summed = jnp.concatenate(lines, axis=0)
    totals = jnp.sum(part_ref[...], axis=1, keepdims=True)
    number, elec, charge_sum, scaled, inv_sum = [totals[i : i + 1] for i in range(5)]
    chem = elec / number
    stepped_total = charge_sum - scaled + chem * inv_sum
    delta = aux_ref[0] + (2.0 * COULOMB) * summed - chem
    stepped = weight * (aux_ref[1] - delta * aux_ref[2])
    charge_ref[...] = weight * (stepped - stepped_total / number)
    resid_ref[...] = weight * delta


def body(offsets, history, occupied, species, chi_table, eta_table, gamma_table):
    _, ny, nz, slots = occupied.shape
    cells = ny * nz
    nx, gy, gz = lax.axis_size("gx"), lax.axis_size("gy"), lax.axis_size("gz")
    py = math.gcd(nx, ny)
    pz = nx // py
    ty, tz = ny // py, nz // pz
    r2, z2 = ty + 1, tz + 2
    per = r2 * z2
    nb = nx * ty * tz
    nck = slots // 8
    vmem = pl.BlockSpec(memory_space=pltpu.VMEM)
    smem = pl.BlockSpec(memory_space=pltpu.SMEM)
    shape = lambda *s: jax.ShapeDtypeStruct(s, F32)
    occ = occupied.reshape(cells, slots)
    packed, aux, part = pl.pallas_call(
        pack_kernel,
        out_shape=(shape(cells, FIELDS, slots), shape(4, cells, slots), shape(8, slots)),
        in_specs=[vmem] * 4 + [smem] * 3,
        out_specs=(vmem, vmem, vmem),
        name="pack",
    )(
        offsets.reshape(3, cells, slots),
        history.reshape(-1, cells, slots),
        occ,
        species.reshape(cells, slots),
        chi_table,
        eta_table,
        gamma_table,
    )
    plane = packed.reshape(ny, nz, FIELDS, slots)
    low = lax.ppermute(plane[:, nz - 1 :], "gz", ring(gz, 1))
    high = lax.ppermute(plane[:, :1], "gz", ring(gz, -1))
    plane = jnp.concatenate([low, plane, high], axis=1)
    above = lax.ppermute(plane[:1], "gy", ring(gy, -1))
    plane = jnp.concatenate([plane, above], axis=0)
    me = lax.axis_index("gx")

    def tile(owner):
        return lax.dynamic_slice(plane, ((owner // pz) * ty, (owner % pz) * tz, 0, 0), (r2, z2, FIELDS, slots))

    planes = [tile(me)]
    for k in range(1, nx):
        planes.append(lax.ppermute(tile((me - k) % nx), "gx", ring(nx, -k)))
    number = jnp.stack([p[:ty, 1 : tz + 1, 7, 0] for p in planes]).reshape(nb).astype(jnp.int32)
    chunks = (number + 7) // 8
    steps = (jnp.sum(chunks) + 1) // 2
    chunks = jnp.concatenate([chunks, jnp.zeros((1,), jnp.int32), steps[None]])
    table = np.zeros((3, nb + 1), np.int32)
    for b in range(nb):
        p, r, z = b // (ty * tz), b // tz % ty, b % tz
        for a in range(3):
            table[a, b] = ((p + a - 1) % nx) * per + r * z2 + z + 1
    ncell = nx * per
    out = pl.pallas_call(
        lambda *refs: pair_kernel(nb, z2, slots, *refs),
        out_shape=shape(nx, per + 8, slots),
        in_specs=[smem, smem, vmem] + [vmem] * nx,
        out_specs=vmem,
        scratch_shapes=[
            pltpu.VMEM((ncell, 5, 8, slots), F32),
            pltpu.VMEM((nb * nck + 1, 5, 8, slots), F32),
            pltpu.VMEM((2, nb + 1, NP, 8, slots), F32),
            pltpu.VMEM((nb * nck + 1, 8, slots), F32),
        ],
        compiler_params=pltpu.CompilerParams(vmem_limit_bytes=40 * 1024 * 1024),
        name="pairs",
    )(chunks, jnp.asarray(table.reshape(-1)), part, *planes)
    gathered = [out[0]]
    for k in range(1, nx):
        gathered.append(lax.ppermute(out[k], "gx", ring(nx, k)))
    total = sum(g[per:] for g in gathered[1:]) + gathered[0][per:]
    wide = jnp.zeros((ny + 1, nz + 2, slots), F32)
    for k in range(nx):
        owner = (me - k) % nx
        at = ((owner // pz) * ty, (owner % pz) * tz, 0)
        piece = gathered[k][:per].reshape(r2, z2, slots)
        wide = wide + lax.dynamic_update_slice(jnp.zeros_like(wide), piece, at)
    total = total + lax.ppermute(total, "gz", ring(gz, 1)) if gz == 2 else lax.psum(total, "gz")
    back = lax.ppermute(wide[ny:], "gy", ring(gy, 1))
    if gy == 4:
        total = total + lax.ppermute(total, "gy", [(i, i ^ 1) for i in range(gy)])
        total = total + lax.ppermute(total, "gy", [(i, i ^ 2) for i in range(gy)])
    else:
        total = lax.psum(total, "gy")
    wide = jnp.concatenate([wide[:1] + back, wide[1:ny]], axis=0)
    from_high = lax.ppermute(wide[:, :1], "gz", ring(gz, -1))
    from_low = lax.ppermute(wide[:, nz + 1 :], "gz", ring(gz, 1))
    inner = wide[:, 1 : nz + 1]
    inner = jnp.concatenate([inner[:, :1] + from_low, inner[:, 1 : nz - 1], inner[:, nz - 1 :] + from_high], axis=1)
    charge, residual = pl.pallas_call(
        finish_kernel,
        out_shape=(shape(cells, slots), shape(cells, slots)),
        in_specs=[vmem] * 4,
        out_specs=(vmem, vmem),
        name="finish",
    )(inner.reshape(cells, slots), aux, occ, total)
    return charge.reshape(occupied.shape), residual.reshape(occupied.shape)


def solution(mesh):
    return jax.shard_map(
        body,
        mesh=mesh,
        in_specs=(
            P(None, "gx", "gy", "gz", None),
            P(None, "gx", "gy", "gz", None),
            P("gx", "gy", "gz", None),
            P("gx", "gy", "gz", None),
            P(),
            P(),
            P(),
        ),
        out_specs=(P("gx", "gy", "gz", None), P("gx", "gy", "gz", None)),
        check_vma=False,
    )
```

time: 244 us -> 76.2 us (0.31)
  other arithmetic: 180 us -> 3.44 us
  blocking collectives: 39.4 us -> 0 us
  Pallas kernels: 0 us -> 32.6 us
  waiting for transfers between devices: 7.9 us -> 21.7 us
  starting transfers between devices: 8.42 us -> 14.1 us
  loops' own time: 3.4 us -> 0 us
  between operations: 4.56 us -> 1.45 us
  local copies, waits for them, and re-layouts: 0.03 us -> 2.66 us
    reduce_sum x30 -> x0, other arithmetic: 177 us -> none  [the longest x27 174 us: pair_sum(): return jnp.sum(kernel * source[3][..., None, :], axis=-1)]
    psum x1 -> x0, blocking collectives: 39.4 us -> none  [body(): lax.psum((jnp.sum(weight), jnp.sum(weight * electroneg), jnp.sum(predicte...]
    pallas_call x0 -> x3, Pallas kernels: none -> 32.6 us  [the longest x1 28.4 us: body(): pl.pallas_call(lambda *refs: pair_kernel(nb, z2, slots, *refs), out_shape...]
    ppermute x6 -> x15, waiting for transfers between devices: 7.9 us -> 21.7 us  [the longest x1 5.23 us: body(): back = lax.ppermute(wide[ny:], 'gy', ring(gy, 1))]
    ppermute x6 -> x15, starting transfers between devices: 8.42 us -> 14.1 us  [the longest x1 4.75 us: body(): above = lax.ppermute(plane[:1], 'gy', ring(gy, -1))]
    another operation x1 -> x0, loops' own time: 3.4 us -> none  [coulomb(): return lax.fori_loop(0, 27, one_offset, start_sum)]
  transfers between devices with their start and end apart: 6 -> 15, of which waited for: 6 -> 13; matrix products, arithmetic and copies ran while one was open for 0% -> 1% of each run, Pallas kernels for 0% -> 0%
where the time goes in v1:
time: 76.2 us; the launch traced here: 75.9 us
  Pallas kernels  32.6 us (43%)
  waiting for transfers between devices  21.7 us (28%)
  starting transfers between devices  14.1 us (19%)
  other arithmetic  3.44 us (5%)
  local copies, waits for them, and re-layouts  2.66 us (3%)
  between operations  1.45 us (2%)
    pallas_call x1, Pallas kernels, body(): pl.pallas_call(lambda *refs: pair_kernel(nb, z2, slots, *refs), out_shape...  28.4 us
    ppermute x1, waiting for transfers between devices, body(): back = lax.ppermute(wide[ny:], 'gy', ring(gy, 1))  5.23 us
    ppermute x1, starting transfers between devices, body(): above = lax.ppermute(plane[:1], 'gy', ring(gy, -1))  4.75 us
    ppermute x3, starting transfers between devices, body(): planes.append(lax.ppermute(tile((me - k) % nx), 'gx', ring(nx, -k)))  4.5 us
    ppermute x3, waiting for transfers between devices, body(): gathered.append(lax.ppermute(out[k], 'gx', ring(nx, k)))  4.34 us
    ppermute x1, waiting for transfers between devices, body(): total = total + lax.ppermute(total, 'gy', [(i, i ^ 2) for i in range(gy)])  3.32 us
    ppermute x3, starting transfers between devices, body(): gathered.append(lax.ppermute(out[k], 'gx', ring(nx, k)))  3.03 us
    ppermute x3, waiting for transfers between devices, body(): planes.append(lax.ppermute(tile((me - k) % nx), 'gx', ring(nx, -k)))  2.57 us
  transfers between devices with their start and end apart: 15, of which 13 were waited for; matrix products, arithmetic and copies ran while one was open for 1% of the time, Pallas kernels for 0%

profile of v1, /device:TPU:0, one launch (start us, length us, event | category | flops | bytes accessed | tf_op | source)
XLA Modules:
  0.0 75.9 jit_solution(11395693209296154682)
XLA Ops:
  0.6 2.4 %pack.1 = (f32[32,8,128]{2,1,0:T(8,128)}, f32[4,32,128]{2,1,0:T(8,128)}, f32[8,128]{1,0:T(8,128)}) custom-call(f32[3,32,128]{2,1,0:T(8,128)} %bitcast.30, f32[6,32,128]{2,1,0:T(8,128)} %bitcast.27, s32[32,128]{1,0:T(8,128)} %bitcast.28, s32[32,128]{1,0:T(8,128)} %bitcast.31, f32[4]{0:T(128)} %chi_ref.1, f32[4]{0:T(128)} %eta_ref.1, f32[4]{0:T(128)} %gam_ref.1), custom_call_target="tpu_custom_call" | custom-call | tf_op jit(solution)/shard_map/pack/pallas_call | solution.py:235
  3.0 0.7 fusion.7
  3.7 0.5 collective-permute-start
  4.2 0.1 collective-permute-start.1
  4.3 0.8 %collective-permute-done = f32[4,1,8,128]{3,2,1,0:T(8,128)S(1)} collective-permute-done((f32[4,1,8,128]{3,2,1,0:T(8,128)S(1)}, f32[4,1,8,128]{3,2,1,0:T(8,128)S(1)}, u32[]{:S(2)}, u32[]{:S(2)}) %collective-permute-start) | collective-permute-done | bytes 16416 | tf_op jit(solution)/shard_map/ppermute | solution.py:251
  5.1 0.3 collective-permute-done.1
  5.4 0.8 %pad_maximum_fusion.1 = f32[1,10,8,128]{3,2,1,0:T(8,128)S(1)} fusion(f32[4,1,8,128]{3,2,1,0:T(8,128)S(1)} %collective-permute-done.1, f32[4,8,8,128]{3,2,1,0:T(8,128)} %bitcast.25, f32[4,1,8,128]{3,2,1,0:T(8,128)S(1)} %collective-permute-done), kind=kLoop, calls=%fused_computation.3 | loop fusion | flops 20480 | bytes 204800 | tf_op jit(solution)/shard_map/concatenate | solution.py:253
  6.2 4.7 %collective-permute-start.2 = (f32[1,10,8,128]{3,2,1,0:T(8,128)S(1)}, f32[1,10,8,128]{3,2,1,0:T(8,128)S(1)}, u32[]{:S(2)}, u32[]{:S(2)}) collective-permute-start(f32[1,10,8,128]{3,2,1,0:T(8,128)S(1)} %pad_maximum_fusion.1), channel_id=1, source_target_pairs={{0,6},{2,0},{4,2},{6,4},{1,7},{3,1},{5,3},{7,5},{8,14},{10,8},{12,... | collective-permute-start | bytes 122888 | tf_op jit(solution)/shard_map/ppermute | solution.py:254
  10.9 1.7 %collective-permute-done.2 = f32[1,10,8,128]{3,2,1,0:T(8,128)S(1)} collective-permute-done((f32[1,10,8,128]{3,2,1,0:T(8,128)S(1)}, f32[1,10,8,128]{3,2,1,0:T(8,128)S(1)}, u32[]{:S(2)}, u32[]{:S(2)}) %collective-permute-start.2) | collective-permute-done | bytes 40992 | tf_op jit(solution)/shard_map/ppermute | solution.py:254
  12.7 1.5 %collective-permute-start.5 = (f32[2,10,8,128]{3,2,1,0:T(8,128)S(1)}, f32[2,10,8,128]{3,2,1,0:T(8,128)S(1)}, u32[]{:S(2)}, u32[]{:S(2)}) collective-permute-start(f32[2,10,8,128]{3,2,1,0:T(8,128)S(1)} %get-tuple-element.15), channel_id=1, source_target_pairs={{0,8},{8,16},{16,24},{24,0},{1,9},{9,17},{17,25},{25,1},{2,10},{10... | collective-permute-start | bytes 245768 | tf_op jit(solution)/shard_map/ppermute | solution.py:263
  14.2 1.5 %collective-permute-start.4 = (f32[2,10,8,128]{3,2,1,0:T(8,128)S(1)}, f32[2,10,8,128]{3,2,1,0:T(8,128)S(1)}, u32[]{:S(2)}, u32[]{:S(2)}) collective-permute-start(f32[2,10,8,128]{3,2,1,0:T(8,128)S(1)} %get-tuple-element.16), channel_id=1, source_target_pairs={{0,16},{8,24},{16,0},{24,8},{1,17},{9,25},{17,1},{25,9},{2,18},{10... | collective-permute-start | bytes 245768 | tf_op jit(solution)/shard_map/ppermute | solution.py:263
  15.7 1.4 %collective-permute-start.3 = (f32[2,10,8,128]{3,2,1,0:T(8,128)S(1)}, f32[2,10,8,128]{3,2,1,0:T(8,128)S(1)}, u32[]{:S(2)}, u32[]{:S(2)}) collective-permute-start(f32[2,10,8,128]{3,2,1,0:T(8,128)S(1)} %get-tuple-element.17), channel_id=1, source_target_pairs={{0,24},{8,0},{16,8},{24,16},{1,25},{9,1},{17,9},{25,17},{2,26},{10... | collective-permute-start | bytes 245768 | tf_op jit(solution)/shard_map/ppermute | solution.py:263
  17.2 0.1 dynamic-slice_reduce_fusion
  17.3 1.6 %collective-permute-done.5.refs_6_ = f32[2,10,8,128]{3,2,1,0:T(8,128)S(1)} collective-permute-done((f32[2,10,8,128]{3,2,1,0:T(8,128)S(1)}, f32[2,10,8,128]{3,2,1,0:T(8,128)S(1)}, u32[]{:S(2)}, u32[]{:S(2)}) %collective-permute-start.5) | collective-permute-done | bytes 81952 | tf_op jit(solution)/shard_map/ppermute | solution.py:263
  18.9 0.1 slice_reduce_fusion
  19.1 0.2 collective-permute-done.4.refs_5_
  19.2 0.1 slice_reduce_fusion.1
  19.4 0.8 %collective-permute-done.3.refs_4_ = f32[2,10,8,128]{3,2,1,0:T(8,128)S(1)} collective-permute-done((f32[2,10,8,128]{3,2,1,0:T(8,128)S(1)}, f32[2,10,8,128]{3,2,1,0:T(8,128)S(1)}, u32[]{:S(2)}, u32[]{:S(2)}) %collective-permute-start.3) | collective-permute-done | bytes 81952 | tf_op jit(solution)/shard_map/ppermute | solution.py:263
  20.2 0.1 slice_reduce_fusion.2
  20.3 0.5 broadcast.91
  20.8 1.3 %fusion.6 = (s32[4,8]{1,0:T(4,128)S(1)}, s32[]{:T(128)}) fusion(s32[]{:T(128)} %broadcast.91, f32[1,1,8]{2,1,0:T(1,128)S(1)} %bitcast.33, f32[1,1,8]{2,1,0:T(1,128)S(1)} %bitcast.34, f32[1,1,8]{2,1,0:T(1,128)S(1)} %bitcast.35, f32[1,1,8]{2,1,0:T(1,128)S(1)} %bitcast.32), kind=kLoop, calls=%fused_computation.46 | loop fusion | flops 671 | bytes 264 | tf_op jit(solution)/shard_map/add | solution.py:265
  22.8 0.1 add.140
  22.9 0.0 copy-start
  22.9 0.1 pad_add_fusion.refs_0_
  23.0 0.6 copy-done
  23.6 0.1 copy-done.1
  23.6 28.4 %pairs.1 = f32[4,28,128]{2,1,0:T(8,128)S(1)} custom-call(s32[34]{0:T(128)S(1)} %pad_add_fusion.refs_0_, s32[99]{0:T(128)S(1)} %copy-done.1, f32[8,128]{1,0:T(8,128)S(1)} %copy-done, f32[2,10,8,128]{3,2,1,0:T(8,128)S(1)} %get-tuple-element.14.refs_3_, f32[2,10,8,128]{3,2,1,0:T(8,128)S(1)} %collective-permute-done.3.refs_4_, ...), custom_call_target="tpu_custom_call" | custom-call | tf_op jit(solution)/shard_map/pairs/pallas_call | solution.py:274
  52.1 2.4 %collective-permute-start.8 = (f32[28,128]{1,0:T(8,128)S(1)}, f32[28,128]{1,0:T(8,128)S(1)}, u32[]{:S(2)}, u32[]{:S(2)}) collective-permute-start(f32[28,128]{1,0:T(8,128)S(1)} %get-tuple-element.20), channel_id=1, source_target_pairs={{0,24},{8,0},{16,8},{24,16},{1,25},{9,1},{17,9},{25,17},{2,26},{10... | collective-permute-start | bytes 43016 | tf_op jit(solution)/shard_map/ppermute | solution.py:290
  54.4 0.4 collective-permute-start.7
  54.8 0.3 collective-permute-start.6
  55.1 0.8 %collective-permute-done.8 = f32[28,128]{1,0:T(8,128)S(1)} collective-permute-done((f32[28,128]{1,0:T(8,128)S(1)}, f32[28,128]{1,0:T(8,128)S(1)}, u32[]{:S(2)}, u32[]{:S(2)}) %collective-permute-start.8) | collective-permute-done | bytes 14368 | tf_op jit(solution)/shard_map/ppermute | solution.py:290
  55.9 2.3 %collective-permute-done.7 = f32[28,128]{1,0:T(8,128)S(1)} collective-permute-done((f32[28,128]{1,0:T(8,128)S(1)}, f32[28,128]{1,0:T(8,128)S(1)}, u32[]{:S(2)}, u32[]{:S(2)}) %collective-permute-start.7) | collective-permute-done | bytes 14368 | tf_op jit(solution)/shard_map/ppermute | solution.py:290
  58.2 1.3 %collective-permute-done.6 = f32[28,128]{1,0:T(8,128)S(1)} collective-permute-done((f32[28,128]{1,0:T(8,128)S(1)}, f32[28,128]{1,0:T(8,128)S(1)}, u32[]{:S(2)}, u32[]{:S(2)}) %collective-permute-start.6) | collective-permute-done | bytes 14368 | tf_op jit(solution)/shard_map/ppermute | solution.py:290
  59.5 0.4 collective-permute-start.9
  59.9 0.1 collective-permute-start.12
  60.0 5.2 %collective-permute-done.9 = f32[1,10,128]{2,1,0:T(8,128)S(1)} collective-permute-done((f32[1,10,128]{2,1,0:T(8,128)S(1)}, f32[1,10,128]{2,1,0:T(8,128)S(1)}, u32[]{:S(2)}, u32[]{:S(2)}) %collective-permute-start.9) | collective-permute-done | bytes 5152 | tf_op jit(solution)/shard_map/ppermute | solution.py:299
  65.2 0.1 collective-permute-start.10
  65.3 0.0 collective-permute-done.12
  65.3 0.1 collective-permute-start.13
  65.4 1.0 %collective-permute-done.10 = f32[4,1,128]{2,1,0:T(1,128)S(1)} collective-permute-done((f32[4,1,128]{2,1,0:T(1,128)S(1)}, f32[4,1,128]{2,1,0:T(1,128)S(1)}, u32[]{:S(2)}, u32[]{:S(2)}) %collective-permute-start.10) | collective-permute-done | bytes 2080 | tf_op jit(solution)/shard_map/ppermute | solution.py:307
  66.4 0.2 collective-permute-start.11
  66.6 2.4 %collective-permute-done.13 = f32[8,128]{1,0:T(8,128)S(1)} collective-permute-done((f32[8,128]{1,0:T(8,128)S(1)}, f32[8,128]{1,0:T(8,128)S(1)}, u32[]{:S(2)}, u32[]{:S(2)}) %collective-permute-start.13) | collective-permute-done | bytes 4128 | tf_op jit(solution)/shard_map/ppermute | solution.py:301
  69.0 0.6 collective-permute-start.14
  69.5 0.0 collective-permute-done.11
  69.6 0.6 maximum_bitcast_fusion.sum_ref
  70.2 3.3 %collective-permute-done.14 = f32[8,128]{1,0:T(8,128)S(1)} collective-permute-done((f32[8,128]{1,0:T(8,128)S(1)}, f32[8,128]{1,0:T(8,128)S(1)}, u32[]{:S(2)}, u32[]{:S(2)}) %collective-permute-start.14) | collective-permute-done | bytes 4128 | tf_op jit(solution)/shard_map/ppermute | solution.py:302
  73.5 0.6 add.158.part_ref
  74.1 1.9 %finish.1 = (f32[32,128]{1,0:T(8,128)}, f32[32,128]{1,0:T(8,128)}) custom-call(f32[32,128]{1,0:T(8,128)} %maximum_bitcast_fusion.sum_ref, f32[4,32,128]{2,1,0:T(8,128)} %get-tuple-element.9.aux_ref, s32[32,128]{1,0:T(8,128)} %bitcast.29, f32[8,128]{1,0:T(8,128)} %add.158.part_ref), custom_call_target="tpu_custom_call" | custom-call | tf_op jit(solution)/shard_map/finish/pallas_call | solution.py:310
  (30 shorter events, 0.2 us)
Async XLA Ops:
  3.7 1.3 %collective-permute-start = (f32[4,1,8,128]{3,2,1,0:T(8,128)S(1)}, f32[4,1,8,128]{3,2,1,0:T(8,128)S(1)}, u32[]{:S(2)}, u32[]{:S(2)}) collective-permute-start(f32[4,1,8,128]{3,2,1,0:T(8,128)S(1)} %get-tuple-element.18), channel_id=1, source_target_pairs={{0,1},{1,0},{2,3},{3,2},{4,5},{5,4},{6,7},{7,6},{8,9},{9,8},{10,11... | collective-permute-start | bytes 49160 | tf_op jit(solution)/shard_map/ppermute | solution.py:251
  4.2 8.4 %copy-start.2 = (f32[32,8,128]{2,1,0:T(8,128)S(1)}, f32[32,8,128]{2,1,0:T(8,128)}, u32[]{:S(2)}) copy-start(f32[32,8,128]{2,1,0:T(8,128)} %get-tuple-element.7) | copy-start | bytes 393220
  4.2 1.2 %collective-permute-start.1 = (f32[4,1,8,128]{3,2,1,0:T(8,128)S(1)}, f32[4,1,8,128]{3,2,1,0:T(8,128)S(1)}, u32[]{:S(2)}, u32[]{:S(2)}) collective-permute-start(f32[4,1,8,128]{3,2,1,0:T(8,128)S(1)} %get-tuple-element.19), channel_id=1, source_target_pairs={{0,1},{1,0},{2,3},{3,2},{4,5},{5,4},{6,7},{7,6},{8,9},{9,8},{10,11... | collective-permute-start | bytes 49160 | tf_op jit(solution)/shard_map/ppermute | solution.py:252
  6.2 6.4 %collective-permute-start.2 = (f32[1,10,8,128]{3,2,1,0:T(8,128)S(1)}, f32[1,10,8,128]{3,2,1,0:T(8,128)S(1)}, u32[]{:S(2)}, u32[]{:S(2)}) collective-permute-start(f32[1,10,8,128]{3,2,1,0:T(8,128)S(1)} %pad_maximum_fusion.1), channel_id=1, source_target_pairs={{0,6},{2,0},{4,2},{6,4},{1,7},{3,1},{5,3},{7,5},{8,14},{10,8},{12,... | collective-permute-start | bytes 122888 | tf_op jit(solution)/shard_map/ppermute | solution.py:254
  12.7 6.2 %collective-permute-start.5 = (f32[2,10,8,128]{3,2,1,0:T(8,128)S(1)}, f32[2,10,8,128]{3,2,1,0:T(8,128)S(1)}, u32[]{:S(2)}, u32[]{:S(2)}) collective-permute-start(f32[2,10,8,128]{3,2,1,0:T(8,128)S(1)} %get-tuple-element.15), channel_id=1, source_target_pairs={{0,8},{8,16},{16,24},{24,0},{1,9},{9,17},{17,25},{25,1},{2,10},{10... | collective-permute-start | bytes 245768 | tf_op jit(solution)/shard_map/ppermute | solution.py:263
  14.2 5.0 %collective-permute-start.4 = (f32[2,10,8,128]{3,2,1,0:T(8,128)S(1)}, f32[2,10,8,128]{3,2,1,0:T(8,128)S(1)}, u32[]{:S(2)}, u32[]{:S(2)}) collective-permute-start(f32[2,10,8,128]{3,2,1,0:T(8,128)S(1)} %get-tuple-element.16), channel_id=1, source_target_pairs={{0,16},{8,24},{16,0},{24,8},{1,17},{9,25},{17,1},{25,9},{2,18},{10... | collective-permute-start | bytes 245768 | tf_op jit(solution)/shard_map/ppermute | solution.py:263
  15.7 4.4 %collective-permute-start.3 = (f32[2,10,8,128]{3,2,1,0:T(8,128)S(1)}, f32[2,10,8,128]{3,2,1,0:T(8,128)S(1)}, u32[]{:S(2)}, u32[]{:S(2)}) collective-permute-start(f32[2,10,8,128]{3,2,1,0:T(8,128)S(1)} %get-tuple-element.17), channel_id=1, source_target_pairs={{0,24},{8,0},{16,8},{24,16},{1,25},{9,1},{17,9},{25,17},{2,26},{10... | collective-permute-start | bytes 245768 | tf_op jit(solution)/shard_map/ppermute | solution.py:263
  22.9 0.7 copy-start
  23.0 0.7 copy-start.1
  52.1 3.8 %collective-permute-start.8 = (f32[28,128]{1,0:T(8,128)S(1)}, f32[28,128]{1,0:T(8,128)S(1)}, u32[]{:S(2)}, u32[]{:S(2)}) collective-permute-start(f32[28,128]{1,0:T(8,128)S(1)} %get-tuple-element.20), channel_id=1, source_target_pairs={{0,24},{8,0},{16,8},{24,16},{1,25},{9,1},{17,9},{25,17},{2,26},{10... | collective-permute-start | bytes 43016 | tf_op jit(solution)/shard_map/ppermute | solution.py:290
  54.4 3.7 %collective-permute-start.7 = (f32[28,128]{1,0:T(8,128)S(1)}, f32[28,128]{1,0:T(8,128)S(1)}, u32[]{:S(2)}, u32[]{:S(2)}) collective-permute-start(f32[28,128]{1,0:T(8,128)S(1)} %get-tuple-element.21), channel_id=1, source_target_pairs={{0,16},{8,24},{16,0},{24,8},{1,17},{9,25},{17,1},{25,9},{2,18},{10... | collective-permute-start | bytes 43016 | tf_op jit(solution)/shard_map/ppermute | solution.py:290
  54.8 4.6 %collective-permute-start.6 = (f32[28,128]{1,0:T(8,128)S(1)}, f32[28,128]{1,0:T(8,128)S(1)}, u32[]{:S(2)}, u32[]{:S(2)}) collective-permute-start(f32[28,128]{1,0:T(8,128)S(1)} %get-tuple-element.22), channel_id=1, source_target_pairs={{0,8},{8,16},{16,24},{24,0},{1,9},{9,17},{17,25},{25,1},{2,10},{10... | collective-permute-start | bytes 43016 | tf_op jit(solution)/shard_map/ppermute | solution.py:290
  59.5 5.7 %collective-permute-start.9 = (f32[1,10,128]{2,1,0:T(8,128)S(1)}, f32[1,10,128]{2,1,0:T(8,128)S(1)}, u32[]{:S(2)}, u32[]{:S(2)}) collective-permute-start(f32[1,10,128]{2,1,0:T(8,128)S(1)} %slice.129), channel_id=1, source_target_pairs={{0,2},{2,4},{4,6},{6,0},{1,3},{3,5},{5,7},{7,1},{8,10},{10,12},{12... | collective-permute-start | bytes 15368 | tf_op jit(solution)/shard_map/ppermute | solution.py:299
  59.9 5.4 %collective-permute-start.12 = (f32[8,128]{1,0:T(8,128)S(1)}, f32[8,128]{1,0:T(8,128)S(1)}, u32[]{:S(2)}, u32[]{:S(2)}) collective-permute-start(f32[8,128]{1,0:T(8,128)S(1)} %fusion.1), channel_id=1, source_target_pairs={{0,1},{1,0},{2,3},{3,2},{4,5},{5,4},{6,7},{7,6},{8,9},{9,8},{10,11... | collective-permute-start | bytes 12296 | tf_op jit(solution)/shard_map/ppermute | solution.py:298
  65.2 1.2 %collective-permute-start.10 = (f32[4,1,128]{2,1,0:T(1,128)S(1)}, f32[4,1,128]{2,1,0:T(1,128)S(1)}, u32[]{:S(2)}, u32[]{:S(2)}) collective-permute-start(f32[4,1,128]{2,1,0:T(1,128)S(1)} %pad_maximum_fusion.4), channel_id=1, source_target_pairs={{0,1},{1,0},{2,3},{3,2},{4,5},{5,4},{6,7},{7,6},{8,9},{9,8},{10,11... | collective-permute-start | bytes 6152 | tf_op jit(solution)/shard_map/ppermute | solution.py:307
  65.3 3.7 %collective-permute-start.13 = (f32[8,128]{1,0:T(8,128)S(1)}, f32[8,128]{1,0:T(8,128)S(1)}, u32[]{:S(2)}, u32[]{:S(2)}) collective-permute-start(f32[8,128]{1,0:T(8,128)S(1)} %add.156), channel_id=1, source_target_pairs={{0,2},{2,0},{4,6},{6,4},{1,3},{3,1},{5,7},{7,5},{8,10},{10,8},{12,... | collective-permute-start | bytes 12296 | tf_op jit(solution)/shard_map/ppermute | solution.py:301
  66.4 3.1 %collective-permute-start.11 = (f32[4,1,128]{2,1,0:T(1,128)S(1)}, f32[4,1,128]{2,1,0:T(1,128)S(1)}, u32[]{:S(2)}, u32[]{:S(2)}) collective-permute-start(f32[4,1,128]{2,1,0:T(1,128)S(1)} %get-tuple-element.24), channel_id=1, source_target_pairs={{0,1},{1,0},{2,3},{3,2},{4,5},{5,4},{6,7},{7,6},{8,9},{9,8},{10,11... | collective-permute-start | bytes 6152 | tf_op jit(solution)/shard_map/ppermute | solution.py:306
  69.0 4.5 %collective-permute-start.14 = (f32[8,128]{1,0:T(8,128)S(1)}, f32[8,128]{1,0:T(8,128)S(1)}, u32[]{:S(2)}, u32[]{:S(2)}) collective-permute-start(f32[8,128]{1,0:T(8,128)S(1)} %add.157), channel_id=1, source_target_pairs={{0,4},{2,6},{4,0},{6,2},{1,5},{3,7},{5,1},{7,3},{8,12},{10,14},{12... | collective-permute-start | bytes 12296 | tf_op jit(solution)/shard_map/ppermute | solution.py:302

commit v2 on v1

v2 whole, which is shorter than its diff:
```python
import math

import jax
import jax.numpy as jnp
from jax import lax
from jax.experimental import pallas as pl
from jax.experimental.pallas import tpu as pltpu
from jax.sharding import PartitionSpec as P

EDGE = 10.0
COULOMB = 14.4
WEIGHTS = (22.0 / 7.0, -55.0 / 14.0, 55.0 / 21.0, -22.0 / 21.0, 5.0 / 21.0, -1.0 / 42.0)
FIELDS = 8
SHELL_UP = [(a, 1, c) for a in (-1, 0, 1) for c in (-1, 0, 1)]
SHELL_ROW = [(a, 0, 1) for a in (-1, 0, 1)] + [(1, 0, 0)]
UP_GROUP, ROW_GROUP = 3, 5
VMEM_LIMIT = 24 * 1024 * 1024
F32 = jnp.float32
BF16 = jnp.bfloat16


def ring(n, k):
    return [(i, (i + k) % n) for i in range(n)]


def pieces_of(x):
    hi = x.astype(BF16)
    rest = x - hi.astype(F32)
    mid = rest.astype(BF16)
    low = (rest - mid.astype(F32)).astype(BF16)
    return hi, mid, low


def pick(species, table_ref):
    out = jnp.full(species.shape, table_ref[0], F32)
    for t in range(1, table_ref.shape[0]):
        out = jnp.where(species == t, table_ref[t], out)
    return out


def pack_kernel(pz, tz, off_ref, hist_ref, occ_ref, spec_ref, chi_ref, eta_ref, gam_ref, aux_ref, part_ref, *refs):
    tiles, cell_ref = refs[:-1], refs[-1]
    cells, slots = occ_ref.shape
    weight = occ_ref[...].astype(F32)
    species = spec_ref[...]
    predicted = WEIGHTS[0] * hist_ref[0]
    for level in range(1, len(WEIGHTS)):
        predicted = predicted + WEIGHTS[level] * hist_ref[level]
    predicted = weight * predicted
    chi = pick(species, chi_ref)
    eta = pick(species, eta_ref)
    gam = pick(species, gam_ref)
    root = lax.rsqrt(gam)
    shield = root * root * root * (EDGE**-1.5)
    inverse = 1.0 / eta
    base = chi + eta * predicted - COULOMB * gam * predicted
    winv = weight * inverse
    zero = jnp.zeros((1, slots), F32)
    rows = [weight, weight * base, predicted, winv * base, winv]
    rows = [jnp.sum(r, axis=0, keepdims=True) for r in rows] + [zero] * 3
    part_ref[...] = jnp.concatenate(rows, axis=0)
    tri = lax.broadcasted_iota(jnp.int32, (slots, slots), 0) <= lax.broadcasted_iota(jnp.int32, (slots, slots), 1)
    wb = weight.astype(BF16)
    rank = jnp.dot(wb, tri.astype(F32).astype(BF16), preferred_element_type=F32)
    count = jnp.dot(wb, jnp.ones((slots, slots), BF16), preferred_element_type=F32)
    pos = jnp.where(weight > 0, rank - 1.0, -1.0)
    aux_ref[0] = base
    aux_ref[1] = predicted
    aux_ref[2] = inverse
    aux_ref[3] = pos
    fields = [off_ref[d] * (1.0 / EDGE) for d in range(3)] + [predicted, shield, winv, weight, weight]
    row_id = lax.broadcasted_iota(jnp.int32, (slots, slots), 0).astype(F32)
    lane = lax.broadcasted_iota(jnp.int32, (FIELDS, slots), 1).astype(F32)
    sub = lax.broadcasted_iota(jnp.int32, (FIELDS, slots), 0)
    for c in range(cells):
        feat = jnp.concatenate([f[c : c + 1] for f in fields], axis=0)
        hot = jnp.where(row_id == pos[c : c + 1], 1.0, 0.0).astype(BF16)
        parts = jnp.concatenate(pieces_of(feat), axis=0)
        out = lax.dot_general(parts, hot, (((1,), (1,)), ((), ())), preferred_element_type=F32)
        out = out[:FIELDS] + out[FIELDS : 2 * FIELDS] + out[2 * FIELDS :]
        number = jnp.broadcast_to(count[c : c + 1], (FIELDS, slots))
        out = jnp.where((sub == 4) & (lane >= number), 1.0, out)
        cell_ref[c] = jnp.where(sub == 7, number, out)
    nx = len(tiles)
    me = lax.axis_index("gx")
    ty = tiles[0].shape[0]
    nz = tz * pz
    for k in range(nx):
        owner = lax.rem(me + (nx - k), nx)
        corner = (owner // pz) * (ty * nz) + (owner % pz) * tz
        for r in range(ty):
            for z in range(tz):
                tiles[k][r, z] = cell_ref[corner + (r * nz + z)]


def pair_kernel(cfg, *refs):
    nx, ty, tz, slots = cfg["nx"], cfg["ty"], cfg["tz"], cfg["slots"]
    shell, alone, group = cfg["shell"], cfg["alone"], cfg["group"]
    side, up, first = cfg["side"], cfg["up"], cfg["first"]
    refs = list(refs)
    planes = [refs.pop(0) for _ in range(nx)]
    edge_low, edge_high = (refs.pop(0), refs.pop(0)) if side else (None, None)
    above = refs.pop(0) if up else None
    before = None if first else refs.pop(0)
    part_ref = refs.pop(0)
    out_ref, part_out = refs.pop(0), refs.pop(0)
    up_ref = refs.pop(0) if up else None
    abc, turned_ref, wide_ref, acca, accb, base_s, chunk_s, itemb_s, itemc_s = refs
    nck = slots // 8
    nb = nx * ty * len(cfg["mine"])
    z2 = tz + 2
    per = (ty + 1) * z2
    own = [(p, r, z) for p in range(nx) for r in range(ty) for z in cfg["mine"]]

    def cell_of(p, r, z):
        return (p % nx) * per + r * z2 + z + 1

    def load(p, r, z):
        if r < ty:
            return planes[p][r, z] if 0 <= z < tz else (edge_low[p, r] if z < 0 else edge_high[p, r])
        return above[(p - cfg["turn"]) % nx, z + 1]

    order = (0, 1, 2, 4, 3)
    total_chunks = jnp.int32(0)
    for b, (p, r, z) in enumerate(own):
        cell = load(p, r, z)
        turned_ref[b * nck : (b + 1) * nck] = cell.T.reshape(nck, 8, FIELDS)
        number = (jnp.max(cell[7:8]).astype(jnp.int32) + 7) // 8
        chunk_s[b] = number
        total_chunks = total_chunks + number
        for a in range(3):
            base_s[a * (nb + 1) + b] = cell_of(p + a - 1, r, z)
    chunk_s[nb] = 0
    for a in range(3):
        base_s[a * (nb + 1) + nb] = cell_of(0, 0, own[0][2])
    sub = lax.broadcasted_iota(jnp.int32, (8, slots), 0)
    slant = lax.broadcasted_iota(jnp.int32, (8, slots), 1) - sub
    blank = jnp.zeros((8, slots), F32)
    turned_ref[nb * nck] = jnp.where(lax.broadcasted_iota(jnp.int32, (8, FIELDS), 1) == 4, 1.0, 0.0)
    touched = {}
    for b, (p, r, z) in enumerate(own):
        for a, y, c in shell + ([(0, 0, 0)] if alone else []):
            touched[cell_of(p + a, r + y, z + c)] = ((p + a) % nx, r + y, z + c)
    for key, where in touched.items():
        cell = load(*where)
        for k, f in enumerate(order):
            abc[key, k] = jnp.broadcast_to(cell[f : f + 1], (8, slots))
    for b in range(nb + 1):
        for g in range(group):
            for q in range(len(shell)):
                acca[g, b, q] = blank

    def extend(t, b, c):
        for g in range(group):
            itemb_s[t * group + g] = b
            itemc_s[t * group + g] = c
            more = c + 1 < chunk_s[b]
            b, c = jnp.where(more, b, jnp.minimum(b + 1, nb)), jnp.where(more, c + 1, 0)
        return b, c

    def listed(t, g):
        return itemb_s[t * group + g], itemc_s[t * group + g]

    def prepare(t, g):
        b, c = listed(t, g)
        block = turned_ref[b * nck + c]
        for k, f in enumerate(order):
            wide_ref[g, k] = jnp.broadcast_to(block[:, f : f + 1], (8, slots))

    def value(ai, shift, bf):
        dx, dy, dz = [abc[ai, k] - bf[k][o] for k, o in enumerate(shift)]
        s = dx * dx + dy * dy + dz * dz
        s = jnp.minimum(jnp.maximum(s, 1e-12), 1.0)
        u = s * lax.rsqrt(s)
        v = 1.0 - u
        v = v * v
        v = v * v
        poly = ((u + 0.5) * u + 0.2) * u + 0.05
        x = s * u + abc[ai, 3] * bf[3]
        return (v * poly) * jnp.exp2(jnp.log2(x) * (-1.0 / 3.0))

    def item(t, g):
        b, c = listed(t, g)
        bases = [base_s[a * (nb + 1) + b] for a in range(3)]
        raw = [wide_ref[g, k] for k in range(5)]
        bf = [{o: (raw[k] - float(o) if o else raw[k]) for o in (-1, 0, 1)} for k in range(3)] + [raw[3]]
        qb = raw[4]
        total = None
        if alone:
            total = value(bases[1], (0, 0, 0), bf) * abc[bases[1], 4]
        for q, (a, y, z) in enumerate(shell):
            ai = bases[a + 1] + (y * z2 + z)
            k = value(ai, (a, y, z), bf)
            term = k * abc[ai, 4]
            total = term if total is None else total + term
            acca[g, b, q] = acca[g, b, q] + k * qb
        accb[b * nck + c] = total

    def step(t, carry):
        for g in range(group):
            item(t, g)
        for g in range(group):
            prepare(t + 1, g)
        return extend(t + 2, *carry)

    ahead = extend(1, *extend(0, jnp.int32(0), jnp.int32(0)))
    for g in range(group):
        prepare(0, g)
    steps = (total_chunks + (group - 1)) // group
    lax.fori_loop(0, steps, step, ahead)

    sums = {}

    def add(key, term):
        sums[key] = sums[key] + term if key in sums else term

    for b, (p, r, z) in enumerate(own):
        rows = accb[b * nck : (b + 1) * nck].reshape(slots, slots).T
        folded = rows[:8]
        for i in range(1, nck):
            folded = folded + rows[8 * i : 8 * i + 8]
        filled = jnp.broadcast_to(load(p, r, z)[6:7], (8, slots)) > 0.0
        add(cell_of(p, r, z), jnp.where(filled, folded, 0.0))
        for g in range(group):
            for q, (a, y, c) in enumerate(shell):
                add(cell_of(p + a, r + y, z + c), acca[g, b, q])
    one = jnp.zeros((1, slots), F32)
    two = jnp.zeros((1, slots), F32)
    for p in range(nx):
        for r in range(ty + 1):
            for z in range(-1, tz + 1):
                key = cell_of(p, r, z)
                row = jnp.zeros((1, slots), F32)
                if key in sums:
                    row = jnp.sum(sums[key], axis=0, keepdims=True)
                    cell = load(p, r, z)
                    one = one + cell[6:7] * row
                    two = two + cell[5:6] * row
                i = r * z2 + z + 1
                if r == ty:
                    if up:
                        up_ref[(p - cfg["turn"]) % nx, z + 1 : z + 2, :] = row
                elif first:
                    out_ref[p, i : i + 1, :] = row
                else:
                    out_ref[p, i : i + 1, :] = before[p, i : i + 1, :] + row
    scale = 2.0 * COULOMB
    part = part_ref[...]
    rows = [part[0:1], part[1:2] + scale * one, part[2:3], part[3:4] + scale * two, part[4:8]]
    rows = jnp.concatenate(rows, axis=0)
    if cfg["last"]:
        rows = jnp.broadcast_to(jnp.sum(rows, axis=1, keepdims=True), rows.shape)
    part_out[...] = rows


def pair_call(cfg, *args):
    nx, ty, tz, slots = cfg["nx"], cfg["ty"], cfg["tz"], cfg["slots"]
    nb = nx * ty * len(cfg["mine"])
    nck = slots // 8
    shape = lambda *s: jax.ShapeDtypeStruct(s, F32)
    vmem = pl.BlockSpec(memory_space=pltpu.VMEM)
    outs = [shape(nx, ty * (tz + 2), slots), shape(8, slots)]
    if cfg["up"]:
        outs.append(shape(nx, tz + 2, slots))
    return pl.pallas_call(
        lambda *refs: pair_kernel(cfg, *refs),
        out_shape=tuple(outs),
        in_specs=[vmem] * len(args),
        out_specs=(vmem,) * len(outs),
        scratch_shapes=[
            pltpu.VMEM((nx * (ty + 1) * (tz + 2), 5, 8, slots), F32),
            pltpu.VMEM((nb * nck + 1, 8, FIELDS), F32),
            pltpu.VMEM((cfg["group"], 5, 8, slots), F32),
            pltpu.VMEM((cfg["group"], nb + 1, len(cfg["shell"]), 8, slots), F32),
            pltpu.VMEM((nb * nck + 1, 8, slots), F32),
            pltpu.SMEM((3 * (nb + 1),), jnp.int32),
            pltpu.SMEM((nb + 1,), jnp.int32),
            pltpu.SMEM((nb * nck + 4 * cfg["group"],), jnp.int32),
            pltpu.SMEM((nb * nck + 4 * cfg["group"],), jnp.int32),
        ],
        compiler_params=pltpu.CompilerParams(vmem_limit_bytes=VMEM_LIMIT),
        name=cfg["name"],
    )(*args)


def unpack_kernel(sum_ref, aux_ref, out_ref):
    cells, slots = out_ref.shape
    row_id = lax.broadcasted_iota(jnp.int32, (slots, slots), 0).astype(F32)
    pos = aux_ref[3]
    hi, mid, low = [t.astype(F32) for t in pieces_of(sum_ref[...])]
    lines = []
    for c in range(cells):
        hot = jnp.where(row_id == pos[c : c + 1], 1.0, 0.0).astype(BF16)
        parts = jnp.concatenate([hi[c : c + 1], mid[c : c + 1], low[c : c + 1]] + [jnp.zeros((5, slots), F32)], axis=0)
        out = jnp.dot(parts.astype(BF16), hot, preferred_element_type=F32)
        lines.append(out[0:1] + out[1:2] + out[2:3])
    out_ref[...] = jnp.concatenate(lines, axis=0)


def body(offsets, history, occupied, species, chi_table, eta_table, gamma_table):
    _, ny, nz, slots = occupied.shape
    cells = ny * nz
    axes = ("gx", "gy", "gz")
    nx, gy, gz = [lax.axis_size(a) for a in axes]
    py = math.gcd(nx, ny)
    pz = nx // py
    ty, tz = ny // py, nz // pz
    z2 = tz + 2
    vmem = pl.BlockSpec(memory_space=pltpu.VMEM)
    shape = lambda *s: jax.ShapeDtypeStruct(s, F32)
    occ = occupied.reshape(cells, slots)
    aux, part, *tiles = pl.pallas_call(
        lambda *refs: pack_kernel(pz, tz, *refs),
        out_shape=(shape(4, cells, slots), shape(8, slots)) + (shape(ty, tz, FIELDS, slots),) * nx,
        in_specs=[vmem] * 4 + [pl.BlockSpec(memory_space=pltpu.SMEM)] * 3,
        out_specs=(vmem,) * (2 + nx),
        scratch_shapes=[pltpu.VMEM((cells, FIELDS, slots), F32)],
        name="pack",
    )(
        offsets.reshape(3, cells, slots),
        history.reshape(-1, cells, slots),
        occ,
        species.reshape(cells, slots),
        chi_table,
        eta_table,
        gamma_table,
    )
    me = lax.axis_index("gx")
    planes = [tiles[0]] + [lax.ppermute(tiles[k], "gx", ring(nx, -k)) for k in range(1, nx)]

    def number_of(x, y, z):
        return (x * gy + y) * gz + z

    def towards(up, side):
        pairs = []
        for x in range(nx):
            for y in range(gy):
                for z in range(gz):
                    row = (y * py + x // pz + up) % (gy * py)
                    col = (z * pz + x % pz + side) % (gz * pz)
                    pairs.append((number_of(row % py * pz + col % pz, row // py, col // pz), number_of(x, y, z)))
        return pairs

    def turned(array, side):
        if pz == 1:
            return array
        col = me % pz
        return jnp.roll(array, (col + side) % pz - col, axis=0)

    first = jnp.stack([p[:, 0] for p in planes])
    last = jnp.stack([p[:, tz - 1] for p in planes])
    if gz * pz == 2:
        both = lax.ppermute(jnp.stack([first, last]), axes, towards(0, 1))
        edge_low, edge_high = turned(both[1], -1), turned(both[0], 1)
    else:
        edge_low = turned(lax.ppermute(last, axes, towards(0, -1)), -1)
        edge_high = turned(lax.ppermute(first, axes, towards(0, 1)), 1)
    bottom = jnp.concatenate([edge_low[:, :1], jnp.stack([p[0] for p in planes]), edge_high[:, :1]], axis=1)
    above = lax.ppermute(bottom, axes, towards(1, 0))

    common = dict(nx=nx, ty=ty, tz=tz, slots=slots, turn=pz % nx)
    half = tz // 2
    row = dict(common, shell=SHELL_ROW, alone=True, group=ROW_GROUP, side=True, up=False)
    early = dict(row, name="early", mine=range(half), first=True, last=False)
    late = dict(row, name="late", mine=range(half, tz), first=False, last=True)
    upper = dict(common, name="upper", mine=range(tz), shell=SHELL_UP, alone=False, group=UP_GROUP, side=ty > 1, up=True, first=False, last=False)
    sums, part = pair_call(early, *planes, edge_low, edge_high, part)
    inner_edges = (edge_low, edge_high) if ty > 1 else ()
    sums, part, up_sums = pair_call(upper, *planes, *inner_edges, above, sums, part)
    back = lax.ppermute(up_sums, axes, [(t, s) for s, t in towards(1, 0)])
    sums, part = pair_call(late, *planes, edge_low, edge_high, sums, part)

    sums = jnp.concatenate([sums[:, :z2] + back, sums[:, z2:], jnp.broadcast_to(part, (nx,) + part.shape)], axis=1)
    rows = ty * z2
    gathered = [sums[0]] + [lax.ppermute(sums[k], "gx", ring(nx, k)) for k in range(1, nx)]
    total = gathered[0][rows:]
    for g in gathered[1:]:
        total = total + g[rows:]
    for axis, count in (("gz", gz), ("gy", gy)):
        if count & (count - 1):
            total = lax.psum(total, axis)
        else:
            for bit in range(count.bit_length() - 1):
                total = total + lax.ppermute(total, axis, [(i, i ^ (1 << bit)) for i in range(count)])
    wide = jnp.zeros((ny, nz + 2, slots), F32)
    for k in range(nx):
        owner = (me - k) % nx
        at = ((owner // pz) * ty, (owner % pz) * tz, 0)
        piece = gathered[k][:rows].reshape(ty, z2, slots)
        wide = wide + lax.dynamic_update_slice(jnp.zeros_like(wide), piece, at)
    if gz == 2:
        both = lax.ppermute(jnp.stack([wide[:, 0], wide[:, nz + 1]]), "gz", ring(gz, 1))
        from_high, from_low = both[0], both[1]
    else:
        from_high = lax.ppermute(wide[:, 0], "gz", ring(gz, -1))
        from_low = lax.ppermute(wide[:, nz + 1], "gz", ring(gz, 1))
    inner = wide[:, 1 : nz + 1]
    inner = jnp.concatenate(
        [inner[:, :1] + from_low[:, None], inner[:, 1 : nz - 1], inner[:, nz - 1 :] + from_high[:, None]], axis=1
    )
    summed = pl.pallas_call(
        unpack_kernel,
        out_shape=shape(cells, slots),
        in_specs=[vmem] * 2,
        out_specs=vmem,
        compiler_params=pltpu.CompilerParams(vmem_limit_bytes=VMEM_LIMIT),
        name="unpack",
    )(inner.reshape(cells, slots), aux)
    weight = occ.astype(F32)
    number, elec, charge_sum, scaled, inv_sum = [total[i : i + 1] for i in range(5)]
    chem = elec / number
    stepped_total = charge_sum - scaled + chem * inv_sum
    delta = aux[0] + (2.0 * COULOMB) * summed - chem
    stepped = weight * (aux[1] - delta * aux[2])
    charge = weight * (stepped - stepped_total / number)
    residual = weight * delta
    return charge.reshape(occupied.shape), residual.reshape(occupied.shape)


def solution(mesh):
    return jax.shard_map(
        body,
        mesh=mesh,
        in_specs=(
            P(None, "gx", "gy", "gz", None),
            P(None, "gx", "gy", "gz", None),
            P("gx", "gy", "gz", None),
            P("gx", "gy", "gz", None),
            P(),
            P(),
            P(),
        ),
        out_specs=(P("gx", "gy", "gz", None), P("gx", "gy", "gz", None)),
        check_vma=False,
    )
```

time: 76.2 us -> 64.6 us (0.85)
  waiting for transfers between devices: 21.7 us -> 14.5 us
  other arithmetic: 3.44 us -> 0.76 us
  local copies, waits for them, and re-layouts: 2.66 us -> 1.42 us
    ppermute x15 -> x13, waiting for transfers between devices: 21.7 us -> 14.5 us  [the longest x3 5.08 us: body(): lax.ppermute(total, axis, [(i, i ^ 1 << bit) for i in range(count)])]
    add x8 -> x7, other arithmetic: 1.92 us -> 0.03 us  [the longest x3 0.01 us: body(): total + lax.ppermute(total, axis, [(i, i ^ 1 << bit) for i in range(count)])]
    concatenate x4 -> x1, other arithmetic: 0.86 us -> 0.02 us  [body(): jnp.concatenate([edge_low[:, :1], jnp.stack([p[0] for p in planes]), edge...]
    pallas_call x3 -> x5, Pallas kernels: 32.6 us -> 32.8 us  [the longest x3 30 us: pair_call(): pl.pallas_call(lambda *refs: pair_kernel(cfg, *refs), out_shape=tuple(out...]
    ppermute x15 -> x13, starting transfers between devices: 14.1 us -> 14 us  [the longest x3 5.02 us: body(): lax.ppermute(tiles[k], 'gx', ring(nx, -k))]
  transfers between devices with their start and end apart: 15 -> 13, of which waited for: 13 -> 9; matrix products, arithmetic and copies ran while one was open for 1% -> 1% of each run, Pallas kernels for 0% -> 19%
where the time goes in v2:
time: 64.6 us; the launch traced here: 64.4 us
  Pallas kernels  32.8 us (51%)
  waiting for transfers between devices  14.5 us (22%)
  starting transfers between devices  14 us (22%)
  local copies, waits for them, and re-layouts  1.42 us (2%)
  between operations  0.92 us (1%)
  other arithmetic  0.76 us (1%)
    pallas_call x3, Pallas kernels, pair_call(): pl.pallas_call(lambda *refs: pair_kernel(cfg, *refs), out_shape=tuple(out...  30 us
    ppermute x3, waiting for transfers between devices, body(): lax.ppermute(total, axis, [(i, i ^ 1 << bit) for i in range(count)])  5.08 us
    ppermute x3, starting transfers between devices, body(): lax.ppermute(tiles[k], 'gx', ring(nx, -k))  5.02 us
    ppermute x3, waiting for transfers between devices, body(): lax.ppermute(tiles[k], 'gx', ring(nx, -k))  3.76 us
    ppermute x1, starting transfers between devices, body(): above = lax.ppermute(bottom, axes, towards(1, 0))  3.15 us
    ppermute x3, waiting for transfers between devices, body(): lax.ppermute(sums[k], 'gx', ring(nx, k))  3.12 us
    ppermute x3, starting transfers between devices, body(): lax.ppermute(total, axis, [(i, i ^ 1 << bit) for i in range(count)])  3.12 us
    pallas_call x1, Pallas kernels, body(): pl.pallas_call(lambda *refs: pack_kernel(pz, tz, *refs), out_shape=(shape...  2.36 us
  transfers between devices with their start and end apart: 13, of which 9 were waited for; matrix products, arithmetic and copies ran while one was open for 1% of the time, Pallas kernels for 19%

profile of v2, /device:TPU:0, one launch (start us, length us, event | category | flops | bytes accessed | tf_op | source)
XLA Modules:
  0.0 64.4 jit_solution(5229769471655039117)
XLA Ops:
  0.6 2.4 %pack.1 = (f32[4,32,128]{2,1,0:T(8,128)}, f32[8,128]{1,0:T(8,128)}, f32[1,8,8,128]{3,2,1,0:T(8,128)}, f32[1,8,8,128]{3,2,1,0:T(8,128)}, f32[1,8,8,128]{3,2,1,0:T(8,128)}, /*index=5*/f32[1,8,8,128]{3,2,1,0:T(8,128)}) custom-call(f32[3,32,128]{2,1,0:T(8,128)} %bitcast.108, f32[6,32,128]{2,1,0:T(8,128)} %bitcast.106, s32[32,128]{1,0:T(8,128)} %bitcast.107, ...), custom_call_target="tpu_custom_call" | custom-call | tf_op jit(solution)/shard_map/pack/pallas_call | solution.py:312
  3.0 3.9 %collective-permute-start = (f32[1,8,8,128]{3,2,0,1:T(8,128)}, f32[1,8,8,128]{3,2,0,1:T(8,128)S(1)}, u32[]{:S(2)}, u32[]{:S(2)}) collective-permute-start(f32[1,8,8,128]{3,2,0,1:T(8,128)} %bitcast.116), channel_id=1, source_target_pairs={{0,24},{8,0},{16,8},{24,16},{1,25},{9,1},{17,9},{25,17},{2,26},{10... | collective-permute-start | bytes 98312 | tf_op jit(solution)/shard_map/ppermute | solution.py:329
  6.9 0.5 collective-permute-start.1
  7.4 0.6 collective-permute-start.2
  8.0 0.7 %fusion.16 = (f32[1,1,8,128]{3,2,0,1:T(8,128)S(1)}, f32[1,1,8,128]{3,2,0,1:T(8,128)S(1)}) fusion(f32[1,8,8,128]{3,2,0,1:T(8,128)} %bitcast.95), kind=kLoop, calls=%fused_computation.43 | loop fusion | bytes 16384 | tf_op jit(solution)/shard_map/slice | solution.py:350
  8.7 3.8 %collective-permute-done.2 = f32[1,8,8,128]{3,2,0,1:T(8,128)S(1)} collective-permute-done((f32[1,8,8,128]{3,2,0,1:T(8,128)}, f32[1,8,8,128]{3,2,0,1:T(8,128)S(1)}, u32[]{:S(2)}, u32[]{:S(2)}) %collective-permute-start.2) | collective-permute-done | bytes 32800 | tf_op jit(solution)/shard_map/ppermute | solution.py:329
  12.4 0.0 collective-permute-done.1
  12.5 0.0 collective-permute-done
  12.5 0.0 copy-start
  12.5 0.1 collective-permute-start.3
  12.6 1.2 %collective-permute-done.3 = f32[2,4,1,8,128]{4,3,1,2,0:T(8,128)S(1)} collective-permute-done((f32[2,4,1,8,128]{4,3,1,2,0:T(8,128)S(1)}, f32[2,4,1,8,128]{4,3,1,2,0:T(8,128)S(1)}, u32[]{:S(2)}, u32[]{:S(2)}) %collective-permute-start.3) | collective-permute-done | bytes 32800 | tf_op jit(solution)/shard_map/ppermute | solution.py:353
  13.8 0.0 copy-done
  13.8 3.2 %collective-permute-start.4 = (f32[4,10,8,128]{3,2,0,1:T(8,128)S(1)}, f32[4,10,8,128]{3,2,0,1:T(8,128)S(1)}, u32[]{:S(2)}, u32[]{:S(2)}) collective-permute-start(f32[4,10,8,128]{3,2,0,1:T(8,128)S(1)} %pad_maximum_fusion), channel_id=1, source_target_pairs={{8,0},{9,1},{10,2},{11,3},{12,4},{13,5},{14,6},{15,7},{16,8},{17,9... | collective-permute-start | bytes 491528 | tf_op jit(solution)/shard_map/ppermute | solution.py:359
  17.0 0.0 copy-start.2
  17.0 0.7 %copy-done.2 = f32[8,128]{1,0:T(8,128)S(1)} copy-done((f32[8,128]{1,0:T(8,128)S(1)}, f32[8,128]{1,0:T(8,128)}, u32[]{:S(2)}) %copy-start.2) | copy-done | bytes 4120
  17.7 5.8 %early.1 = (f32[4,10,128]{2,1,0:T(8,128)S(1)}, f32[8,128]{1,0:T(8,128)S(1)}) custom-call(f32[1,8,8,128]{3,2,1,0:T(8,128)S(1)} %copy-done, f32[1,8,8,128]{3,2,1,0:T(8,128)S(1)} %bitcast.97, f32[1,8,8,128]{3,2,1,0:T(8,128)S(1)} %bitcast.100, f32[1,8,8,128]{3,2,1,0:T(8,128)S(1)} %bitcast.103, f32[4,1,8,128]{3,2,1,0:T(8,128)S(1)} %get-tuple-element.39.refs_4_, ...), custom_call_target="tpu_custom_call" | custom-call | tf_op jit(solution)/shard_map/early/pallas_call | solution.py:265
  23.5 0.0 collective-permute-done.4
  23.5 18.1 %upper.1 = (f32[4,10,128]{2,1,0:T(8,128)S(1)}, f32[8,128]{1,0:T(8,128)S(1)}, f32[4,10,128]{2,1,0:T(8,128)S(1)}) custom-call(f32[1,8,8,128]{3,2,1,0:T(8,128)S(1)} %copy-done, f32[1,8,8,128]{3,2,1,0:T(8,128)S(1)} %bitcast.98, f32[1,8,8,128]{3,2,1,0:T(8,128)S(1)} %bitcast.101, f32[1,8,8,128]{3,2,1,0:T(8,128)S(1)} %bitcast.104, ...), custom_call_target="tpu_custom_call" | custom-call | tf_op jit(solution)/shard_map/upper/pallas_call | solution.py:265
  41.7 0.1 collective-permute-start.5
  41.8 6.1 %late.1 = (f32[4,10,128]{2,1,0:T(8,128)S(1)}, f32[8,128]{1,0:T(8,128)S(1)}) custom-call(f32[1,8,8,128]{3,2,1,0:T(8,128)S(1)} %copy-done, f32[1,8,8,128]{3,2,1,0:T(8,128)S(1)} %bitcast.99, f32[1,8,8,128]{3,2,1,0:T(8,128)S(1)} %bitcast.102, f32[1,8,8,128]{3,2,1,0:T(8,128)S(1)} %bitcast.105, f32[4,1,8,128]{3,2,1,0:T(8,128)S(1)} %get-tuple-element.39.refs_4_, ...), custom_call_target="tpu_custom_call" | custom-call | tf_op jit(solution)/shard_map/late/pallas_call | solution.py:265
  47.9 1.3 %collective-permute-done.5 = f32[4,10,128]{2,1,0:T(8,128)S(1)} collective-permute-done((f32[4,10,128]{2,1,0:T(8,128)S(1)}, f32[4,10,128]{2,1,0:T(8,128)S(1)}, u32[]{:S(2)}, u32[]{:S(2)}) %collective-permute-start.5) | collective-permute-done | bytes 20512 | tf_op jit(solution)/shard_map/ppermute | solution.py:370
  49.3 0.1 collective-permute-start.8
  49.3 0.1 collective-permute-start.7
  49.4 1.9 %collective-permute-start.6 = (f32[18,128]{1,0:T(8,128)S(1)}, f32[18,128]{1,0:T(8,128)S(1)}, u32[]{:S(2)}, u32[]{:S(2)}) collective-permute-start(f32[18,128]{1,0:T(8,128)S(1)} %get-tuple-element.32), channel_id=1, source_target_pairs={{0,8},{8,16},{16,24},{24,0},{1,9},{9,17},{17,25},{25,1},{2,10},{10... | collective-permute-start | bytes 27656 | tf_op jit(solution)/shard_map/ppermute | solution.py:375
  51.3 1.7 %collective-permute-done.8 = f32[18,128]{1,0:T(8,128)S(1)} collective-permute-done((f32[18,128]{1,0:T(8,128)S(1)}, f32[18,128]{1,0:T(8,128)S(1)}, u32[]{:S(2)}, u32[]{:S(2)}) %collective-permute-start.8) | collective-permute-done | bytes 9248 | tf_op jit(solution)/shard_map/ppermute | solution.py:375
  53.0 0.1 collective-permute-done.7
  53.1 1.4 %collective-permute-done.6 = f32[18,128]{1,0:T(8,128)S(1)} collective-permute-done((f32[18,128]{1,0:T(8,128)S(1)}, f32[18,128]{1,0:T(8,128)S(1)}, u32[]{:S(2)}, u32[]{:S(2)}) %collective-permute-start.6) | collective-permute-done | bytes 9248 | tf_op jit(solution)/shard_map/ppermute | solution.py:375
  54.5 0.0 collective-permute-start.10
  54.6 0.0 copy-start.1
  54.6 0.5 collective-permute-start.9
  55.1 0.5 collective-permute-done.10
  55.6 0.5 collective-permute-start.11
  56.2 0.0 collective-permute-done.9
  56.2 3.1 %collective-permute-done.11 = f32[8,128]{1,0:T(8,128)S(1)} collective-permute-done((f32[8,128]{1,0:T(8,128)S(1)}, f32[8,128]{1,0:T(8,128)S(1)}, u32[]{:S(2)}, u32[]{:S(2)}) %collective-permute-start.11) | collective-permute-done | bytes 4128 | tf_op jit(solution)/shard_map/ppermute | solution.py:384
  59.3 2.6 %collective-permute-start.12 = (f32[8,128]{1,0:T(8,128)S(1)}, f32[8,128]{1,0:T(8,128)S(1)}, u32[]{:S(2)}, u32[]{:S(2)}) collective-permute-start(f32[8,128]{1,0:T(8,128)S(1)} %add.110), channel_id=1, source_target_pairs={{0,4},{2,6},{4,0},{6,2},{1,5},{3,7},{5,1},{7,3},{8,12},{10,14},{12... | collective-permute-start | bytes 12296 | tf_op jit(solution)/shard_map/ppermute | solution.py:384
  61.9 0.0 copy-done.1
  61.9 0.4 unpack.1
  62.3 0.0 copy-start.3
  62.3 1.5 %collective-permute-done.12 = f32[8,128]{1,0:T(8,128)S(1)} collective-permute-done((f32[8,128]{1,0:T(8,128)S(1)}, f32[8,128]{1,0:T(8,128)S(1)}, u32[]{:S(2)}, u32[]{:S(2)}) %collective-permute-start.12) | collective-permute-done | bytes 4128 | tf_op jit(solution)/shard_map/ppermute | solution.py:384
  63.8 0.0 copy-done.3
  63.8 0.6 multiply_bitcast_fusion
  (28 shorter events, 0.2 us)
Async XLA Ops:
  3.0 9.5 %collective-permute-start = (f32[1,8,8,128]{3,2,0,1:T(8,128)}, f32[1,8,8,128]{3,2,0,1:T(8,128)S(1)}, u32[]{:S(2)}, u32[]{:S(2)}) collective-permute-start(f32[1,8,8,128]{3,2,0,1:T(8,128)} %bitcast.116), channel_id=1, source_target_pairs={{0,24},{8,0},{16,8},{24,16},{1,25},{9,1},{17,9},{25,17},{2,26},{10... | collective-permute-start | bytes 98312 | tf_op jit(solution)/shard_map/ppermute | solution.py:329
  6.9 5.5 %collective-permute-start.1 = (f32[1,8,8,128]{3,2,0,1:T(8,128)}, f32[1,8,8,128]{3,2,0,1:T(8,128)S(1)}, u32[]{:S(2)}, u32[]{:S(2)}) collective-permute-start(f32[1,8,8,128]{3,2,0,1:T(8,128)} %bitcast.117), channel_id=1, source_target_pairs={{0,16},{8,24},{16,0},{24,8},{1,17},{9,25},{17,1},{25,9},{2,18},{10... | collective-permute-start | bytes 98312 | tf_op jit(solution)/shard_map/ppermute | solution.py:329
  7.4 5.0 %collective-permute-start.2 = (f32[1,8,8,128]{3,2,0,1:T(8,128)}, f32[1,8,8,128]{3,2,0,1:T(8,128)S(1)}, u32[]{:S(2)}, u32[]{:S(2)}) collective-permute-start(f32[1,8,8,128]{3,2,0,1:T(8,128)} %bitcast.118), channel_id=1, source_target_pairs={{0,8},{8,16},{16,24},{24,0},{1,9},{9,17},{17,25},{25,1},{2,10},{10... | collective-permute-start | bytes 98312 | tf_op jit(solution)/shard_map/ppermute | solution.py:329
  12.5 1.3 %copy-start = (f32[1,8,8,128]{3,2,1,0:T(8,128)S(1)}, f32[1,8,8,128]{3,2,1,0:T(8,128)}, u32[]{:S(2)}) copy-start(f32[1,8,8,128]{3,2,1,0:T(8,128)} %get-tuple-element.16.refs_0_) | copy-start | bytes 98308
  12.5 1.3 %collective-permute-start.3 = (f32[2,4,1,8,128]{4,3,1,2,0:T(8,128)S(1)}, f32[2,4,1,8,128]{4,3,1,2,0:T(8,128)S(1)}, u32[]{:S(2)}, u32[]{:S(2)}) collective-permute-start(f32[2,4,1,8,128]{4,3,1,2,0:T(8,128)S(1)} %pad_maximum_fusion.1), channel_id=1, source_target_pairs={{1,0},{0,1},{3,2},{2,3},{5,4},{4,5},{7,6},{6,7},{9,8},{8,9},{11,10... | collective-permute-start | bytes 98312 | tf_op jit(solution)/shard_map/ppermute | solution.py:353
  13.8 9.7 %collective-permute-start.4 = (f32[4,10,8,128]{3,2,0,1:T(8,128)S(1)}, f32[4,10,8,128]{3,2,0,1:T(8,128)S(1)}, u32[]{:S(2)}, u32[]{:S(2)}) collective-permute-start(f32[4,10,8,128]{3,2,0,1:T(8,128)S(1)} %pad_maximum_fusion), channel_id=1, source_target_pairs={{8,0},{9,1},{10,2},{11,3},{12,4},{13,5},{14,6},{15,7},{16,8},{17,9... | collective-permute-start | bytes 491528 | tf_op jit(solution)/shard_map/ppermute | solution.py:359
  17.0 0.7 %copy-start.2 = (f32[8,128]{1,0:T(8,128)S(1)}, f32[8,128]{1,0:T(8,128)}, u32[]{:S(2)}) copy-start(f32[8,128]{1,0:T(8,128)} %get-tuple-element.20.refs_6_) | copy-start | bytes 12292
  41.7 7.6 %collective-permute-start.5 = (f32[4,10,128]{2,1,0:T(8,128)S(1)}, f32[4,10,128]{2,1,0:T(8,128)S(1)}, u32[]{:S(2)}, u32[]{:S(2)}) collective-permute-start(f32[4,10,128]{2,1,0:T(8,128)S(1)} %get-tuple-element.26), channel_id=1, source_target_pairs={{0,8},{1,9},{2,10},{3,11},{4,12},{5,13},{6,14},{7,15},{8,16},{9,17... | collective-permute-start | bytes 61448 | tf_op jit(solution)/shard_map/ppermute | solution.py:370
  49.3 3.7 %collective-permute-start.8 = (f32[18,128]{1,0:T(8,128)S(1)}, f32[18,128]{1,0:T(8,128)S(1)}, u32[]{:S(2)}, u32[]{:S(2)}) collective-permute-start(f32[18,128]{1,0:T(8,128)S(1)} %get-tuple-element.34), channel_id=1, source_target_pairs={{0,24},{8,0},{16,8},{24,16},{1,25},{9,1},{17,9},{25,17},{2,26},{10... | collective-permute-start | bytes 27656 | tf_op jit(solution)/shard_map/ppermute | solution.py:375
  49.3 3.8 %collective-permute-start.7 = (f32[18,128]{1,0:T(8,128)S(1)}, f32[18,128]{1,0:T(8,128)S(1)}, u32[]{:S(2)}, u32[]{:S(2)}) collective-permute-start(f32[18,128]{1,0:T(8,128)S(1)} %get-tuple-element.33), channel_id=1, source_target_pairs={{0,16},{8,24},{16,0},{24,8},{1,17},{9,25},{17,1},{25,9},{2,18},{10... | collective-permute-start | bytes 27656 | tf_op jit(solution)/shard_map/ppermute | solution.py:375
  49.4 5.1 %collective-permute-start.6 = (f32[18,128]{1,0:T(8,128)S(1)}, f32[18,128]{1,0:T(8,128)S(1)}, u32[]{:S(2)}, u32[]{:S(2)}) collective-permute-start(f32[18,128]{1,0:T(8,128)S(1)} %get-tuple-element.32), channel_id=1, source_target_pairs={{0,8},{8,16},{16,24},{24,0},{1,9},{9,17},{17,25},{25,1},{2,10},{10... | collective-permute-start | bytes 27656 | tf_op jit(solution)/shard_map/ppermute | solution.py:375
  54.5 1.2 %collective-permute-start.10 = (f32[8,128]{1,0:T(8,128)S(1)}, f32[8,128]{1,0:T(8,128)S(1)}, u32[]{:S(2)}, u32[]{:S(2)}) collective-permute-start(f32[8,128]{1,0:T(8,128)S(1)} %slice_add_fusion), channel_id=1, source_target_pairs={{0,1},{1,0},{2,3},{3,2},{4,5},{5,4},{6,7},{7,6},{8,9},{9,8},{10,11... | collective-permute-start | bytes 12296 | tf_op jit(solution)/shard_map/ppermute | solution.py:384
  54.6 7.3 %copy-start.1 = (f32[4,32,128]{2,1,0:T(8,128)S(1)}, f32[4,32,128]{2,1,0:T(8,128)}, u32[]{:S(2)}) copy-start(f32[4,32,128]{2,1,0:T(8,128)} %get-tuple-element.15.aux_ref) | copy-start | bytes 196612
  54.6 1.6 %collective-permute-start.9 = (f32[2,4,128]{2,1,0:T(4,128)S(1)}, f32[2,4,128]{2,1,0:T(4,128)S(1)}, u32[]{:S(2)}, u32[]{:S(2)}) collective-permute-start(f32[2,4,128]{2,1,0:T(4,128)S(1)} %pad_maximum_fusion.3), channel_id=1, source_target_pairs={{0,1},{1,0},{2,3},{3,2},{4,5},{5,4},{6,7},{7,6},{8,9},{9,8},{10,11... | collective-permute-start | bytes 12296 | tf_op jit(solution)/shard_map/ppermute | solution.py:392
  55.6 3.6 %collective-permute-start.11 = (f32[8,128]{1,0:T(8,128)S(1)}, f32[8,128]{1,0:T(8,128)S(1)}, u32[]{:S(2)}, u32[]{:S(2)}) collective-permute-start(f32[8,128]{1,0:T(8,128)S(1)} %add.109), channel_id=1, source_target_pairs={{0,2},{2,0},{4,6},{6,4},{1,3},{3,1},{5,7},{7,5},{8,10},{10,8},{12,... | collective-permute-start | bytes 12296 | tf_op jit(solution)/shard_map/ppermute | solution.py:384
  59.3 4.5 %collective-permute-start.12 = (f32[8,128]{1,0:T(8,128)S(1)}, f32[8,128]{1,0:T(8,128)S(1)}, u32[]{:S(2)}, u32[]{:S(2)}) collective-permute-start(f32[8,128]{1,0:T(8,128)S(1)} %add.110), channel_id=1, source_target_pairs={{0,4},{2,6},{4,0},{6,2},{1,5},{3,7},{5,1},{7,3},{8,12},{10,14},{12... | collective-permute-start | bytes 12296 | tf_op jit(solution)/shard_map/ppermute | solution.py:384
  62.3 1.5 %copy-start.3 = (s32[1,4,8,128]{3,2,1,0:T(8,128)S(1)}, s32[1,4,8,128]{3,2,1,0:T(8,128)}, u32[]{:S(2)}) copy-start(s32[1,4,8,128]{3,2,1,0:T(8,128)} %param.9) | copy-start | bytes 49156

commit v3 on v2

--- a/solution.py
+++ b/solution.py
@@ -14,9 +14,43 @@
 SHELL_UP = [(a, 1, c) for a in (-1, 0, 1) for c in (-1, 0, 1)]
 SHELL_ROW = [(a, 0, 1) for a in (-1, 0, 1)] + [(1, 0, 0)]
 UP_GROUP, ROW_GROUP = 3, 5
+
+
+def real_root():
+    u = -0.34
+    for _ in range(8):
+        u -= (((u + 0.5) * u + 0.2) * u + 0.05) / ((3.0 * u + 1.0) * u + 0.2)
+    return -u
+
+
+ROOT = real_root()
+LINEAR = 0.5 - ROOT
+FREE = 0.2 - ROOT * LINEAR
+REACH = 1.0 / LINEAR
+SCALE = 2.0 * COULOMB / REACH**6
 VMEM_LIMIT = 24 * 1024 * 1024
 F32 = jnp.float32
 BF16 = jnp.bfloat16
+
+
+def fold(g, n):
+    if n % 2:
+        return g
+    half = n // 2
+    return (3 * half - 1 - g if g >= half else g) if isinstance(g, int) else jnp.where(g < half, g, 3 * half - 1 - g)
+
+
+def tile_of(g, y, n):
+    t = fold(g, n)
+    if isinstance(y, int):
+        return n - 1 - t if y % 2 else t
+    return jnp.where(lax.rem(y, 2) == 1, n - 1 - t, t)
+
+
+def device_of(t, y, n):
+    if isinstance(y, int):
+        return fold(n - 1 - t if y % 2 else t, n)
+    return fold(jnp.where(lax.rem(y, 2) == 1, n - 1 - t, t), n)
 
 
 def ring(n, k):
@@ -51,14 +85,14 @@
     eta = pick(species, eta_ref)
     gam = pick(species, gam_ref)
     root = lax.rsqrt(gam)
-    shield = root * root * root * (EDGE**-1.5)
+    shield = root * root * root * ((REACH / EDGE) ** 1.5)
     inverse = 1.0 / eta
     base = chi + eta * predicted - COULOMB * gam * predicted
     winv = weight * inverse
     zero = jnp.zeros((1, slots), F32)
     rows = [weight, weight * base, predicted, winv * base, winv]
     rows = [jnp.sum(r, axis=0, keepdims=True) for r in rows] + [zero] * 3
-    part_ref[...] = jnp.concatenate(rows, axis=0)
+    part_ref[...] = jnp.broadcast_to(jnp.sum(jnp.concatenate(rows, axis=0), axis=1, keepdims=True), part_ref.shape)
     tri = lax.broadcasted_iota(jnp.int32, (slots, slots), 0) <= lax.broadcasted_iota(jnp.int32, (slots, slots), 1)
     wb = weight.astype(BF16)
     rank = jnp.dot(wb, tri.astype(F32).astype(BF16), preferred_element_type=F32)
@@ -68,7 +102,7 @@
     aux_ref[1] = predicted
     aux_ref[2] = inverse
     aux_ref[3] = pos
-    fields = [off_ref[d] * (1.0 / EDGE) for d in range(3)] + [predicted, shield, winv, weight, weight]
+    fields = [off_ref[d] * (REACH / EDGE) for d in range(3)] + [predicted, shield, winv, weight, weight]
     row_id = lax.broadcasted_iota(jnp.int32, (slots, slots), 0).astype(F32)
     lane = lax.broadcasted_iota(jnp.int32, (FIELDS, slots), 1).astype(F32)
     sub = lax.broadcasted_iota(jnp.int32, (FIELDS, slots), 0)
@@ -86,7 +120,7 @@
     ty = tiles[0].shape[0]
     nz = tz * pz
     for k in range(nx):
-        owner = lax.rem(me + (nx - k), nx)
+        owner = tile_of(lax.rem(me + (nx - k), nx), lax.axis_index("gy"), nx)
         corner = (owner // pz) * (ty * nz) + (owner % pz) * tz
         for r in range(ty):
             for z in range(tz):
@@ -101,12 +135,17 @@
     planes = [refs.pop(0) for _ in range(nx)]
     edge_low, edge_high = (refs.pop(0), refs.pop(0)) if side else (None, None)
     above = refs.pop(0) if up else None
-    before = None if first else refs.pop(0)
-    part_ref = refs.pop(0)
+    before, part_ref = (None, None) if first else (refs.pop(0), refs.pop(0))
     out_ref, part_out = refs.pop(0), refs.pop(0)
     up_ref = refs.pop(0) if up else None
     abc, turned_ref, wide_ref, acca, accb, base_s, chunk_s, itemb_s, itemc_s = refs
     nck = slots // 8
+    if up:
+        me, y = lax.axis_index("gx"), lax.axis_index("gy")
+        t = tile_of(me, y, nx) + cfg["pz"]
+        y = lax.rem(y + jnp.where(t < nx, 0, 1), cfg["gy"])
+        turn = device_of(lax.rem(t, nx), y, nx) - me
+        there = [lax.rem(p - turn + 2 * nx, nx) for p in range(nx)]
     nb = nx * ty * len(cfg["mine"])
     z2 = tz + 2
     per = (ty + 1) * z2
@@ -118,7 +157,7 @@
     def load(p, r, z):
         if r < ty:
             return planes[p][r, z] if 0 <= z < tz else (edge_low[p, r] if z < 0 else edge_high[p, r])
-        return above[(p - cfg["turn"]) % nx, z + 1]
+        return above[there[p], z + 1]
 
     order = (0, 1, 2, 4, 3)
     total_chunks = jnp.int32(0)
@@ -170,12 +209,12 @@
     def value(ai, shift, bf):
         dx, dy, dz = [abc[ai, k] - bf[k][o] for k, o in enumerate(shift)]
         s = dx * dx + dy * dy + dz * dz
-        s = jnp.minimum(jnp.maximum(s, 1e-12), 1.0)
+        s = jnp.minimum(jnp.maximum(s, 1e-12), REACH * REACH)
         u = s * lax.rsqrt(s)
-        v = 1.0 - u
+        v = REACH - u
         v = v * v
         v = v * v
-        poly = ((u + 0.5) * u + 0.2) * u + 0.05
+        poly = (u + ROOT * REACH) * ((s + u) + FREE * REACH * REACH)
         x = s * u + abc[ai, 3] * bf[3]
         return (v * poly) * jnp.exp2(jnp.log2(x) * (-1.0 / 3.0))
 
@@ -183,7 +222,7 @@
         b, c = listed(t, g)
         bases = [base_s[a * (nb + 1) + b] for a in range(3)]
         raw = [wide_ref[g, k] for k in range(5)]
-        bf = [{o: (raw[k] - float(o) if o else raw[k]) for o in (-1, 0, 1)} for k in range(3)] + [raw[3]]
+        bf = [{o: (raw[k] - o * REACH if o else raw[k]) for o in (-1, 0, 1)} for k in range(3)] + [raw[3]]
         qb = raw[4]
         total = None
         if alone:
@@ -239,15 +278,16 @@
                 i = r * z2 + z + 1
                 if r == ty:
                     if up:
-                        up_ref[(p - cfg["turn"]) % nx, z + 1 : z + 2, :] = row
+                        up_ref[there[p], z + 1 : z + 2, :] = row
                 elif first:
                     out_ref[p, i : i + 1, :] = row
                 else:
                     out_ref[p, i : i + 1, :] = before[p, i : i + 1, :] + row
-    scale = 2.0 * COULOMB
-    part = part_ref[...]
-    rows = [part[0:1], part[1:2] + scale * one, part[2:3], part[3:4] + scale * two, part[4:8]]
-    rows = jnp.concatenate(rows, axis=0)
+    scale = SCALE
+    none = jnp.zeros((1, slots), F32)
+    rows = jnp.concatenate([none, scale * one, none, scale * two] + [none] * 4, axis=0)
+    if not first:
+        rows = rows + part_ref[...]
     if cfg["last"]:
         rows = jnp.broadcast_to(jnp.sum(rows, axis=1, keepdims=True), rows.shape)
     part_out[...] = rows
@@ -325,7 +365,7 @@
         eta_table,
         gamma_table,
     )
-    me = lax.axis_index("gx")
+    me, column = lax.axis_index("gx"), lax.axis_index("gy")
     planes = [tiles[0]] + [lax.ppermute(tiles[k], "gx", ring(nx, -k)) for k in range(1, nx)]
 
     def number_of(x, y, z):
@@ -336,16 +376,19 @@
         for x in range(nx):
             for y in range(gy):
                 for z in range(gz):
-                    row = (y * py + x // pz + up) % (gy * py)
-                    col = (z * pz + x % pz + side) % (gz * pz)
-                    pairs.append((number_of(row % py * pz + col % pz, row // py, col // pz), number_of(x, y, z)))
+                    t = tile_of(x, y, nx)
+                    row = (y * py + t // pz + up) % (gy * py)
+                    col = (z * pz + t % pz + side) % (gz * pz)
+                    source = device_of(row % py * pz + col % pz, row // py, nx)
+                    pairs.append((number_of(source, row // py, col // pz), number_of(x, y, z)))
         return pairs
 
     def turned(array, side):
         if pz == 1:
             return array
-        col = me % pz
-        return jnp.roll(array, (col + side) % pz - col, axis=0)
+        t = tile_of(me, column, nx)
+        t = t - t % pz + (t + side) % pz
+        return jnp.roll(array, device_of(t, column, nx) - me, axis=0)
 
     first = jnp.stack([p[:, 0] for p in planes])
     last = jnp.stack([p[:, tz - 1] for p in planes])
@@ -358,17 +401,18 @@
     bottom = jnp.concatenate([edge_low[:, :1], jnp.stack([p[0] for p in planes]), edge_high[:, :1]], axis=1)
     above = lax.ppermute(bottom, axes, towards(1, 0))
 
-    common = dict(nx=nx, ty=ty, tz=tz, slots=slots, turn=pz % nx)
+    common = dict(nx=nx, ty=ty, tz=tz, slots=slots, pz=pz, gy=gy)
     half = tz // 2
     row = dict(common, shell=SHELL_ROW, alone=True, group=ROW_GROUP, side=True, up=False)
     early = dict(row, name="early", mine=range(half), first=True, last=False)
     late = dict(row, name="late", mine=range(half, tz), first=False, last=True)
     upper = dict(common, name="upper", mine=range(tz), shell=SHELL_UP, alone=False, group=UP_GROUP, side=ty > 1, up=True, first=False, last=False)
-    sums, part = pair_call(early, *planes, edge_low, edge_high, part)
+    sums, found = pair_call(early, *planes, edge_low, edge_high)
     inner_edges = (edge_low, edge_high) if ty > 1 else ()
-    sums, part, up_sums = pair_call(upper, *planes, *inner_edges, above, sums, part)
+    sums, found, up_sums = pair_call(upper, *planes, *inner_edges, above, sums, found)
     back = lax.ppermute(up_sums, axes, [(t, s) for s, t in towards(1, 0)])
-    sums, part = pair_call(late, *planes, edge_low, edge_high, sums, part)
+    sums, found = pair_call(late, *planes, edge_low, edge_high, sums, found)
+    part = part + found
 
     sums = jnp.concatenate([sums[:, :z2] + back, sums[:, z2:], jnp.broadcast_to(part, (nx,) + part.shape)], axis=1)
     rows = ty * z2
@@ -384,7 +428,7 @@
                 total = total + lax.ppermute(total, axis, [(i, i ^ (1 << bit)) for i in range(count)])
     wide = jnp.zeros((ny, nz + 2, slots), F32)
     for k in range(nx):
-        owner = (me - k) % nx
+        owner = tile_of((me - k) % nx, column, nx)
         at = ((owner // pz) * ty, (owner % pz) * tz, 0)
         piece = gathered[k][:rows].reshape(ty, z2, slots)
         wide = wide + lax.dynamic_update_slice(jnp.zeros_like(wide), piece, at)
@@ -410,7 +454,7 @@
     number, elec, charge_sum, scaled, inv_sum = [total[i : i + 1] for i in range(5)]
     chem = elec / number
     stepped_total = charge_sum - scaled + chem * inv_sum
-    delta = aux[0] + (2.0 * COULOMB) * summed - chem
+    delta = aux[0] + SCALE * summed - chem
     stepped = weight * (aux[1] - delta * aux[2])
     charge = weight * (stepped - stepped_total / number)
     residual = weight * delta

time: 64.6 us -> 63.2 us (0.978)
  waiting for transfers between devices: 14.5 us -> 12 us
  starting transfers between devices: 14 us -> 16 us
  Pallas kernels: 32.8 us -> 32 us
  local copies, waits for them, and re-layouts: 1.42 us -> 0.75 us
    ppermute x3, starting transfers between devices: 3.12 us -> 4.6 us  [body(): lax.ppermute(total, axis, [(i, i ^ 1 << bit) for i in range(count)])]
    ppermute x1, waiting for transfers between devices: 1.35 us -> 0.01 us  [body(): back = lax.ppermute(up_sums, axes, [(t, s) for s, t in towards(1, 0)])]
    ppermute x3, waiting for transfers between devices: 5.08 us -> 3.95 us  [body(): lax.ppermute(total, axis, [(i, i ^ 1 << bit) for i in range(count)])]
    pallas_call x3, Pallas kernels: 30 us -> 29.3 us  [pair_call(): pl.pallas_call(lambda *refs: pair_kernel(cfg, *refs), out_shape=tuple(out...]
    unnamed x8, local copies, waits for them, and re-layouts: 0.7 us -> 0.02 us
  transfers between devices with their start and end apart: 13 -> 13, of which waited for: 9 -> 8; matrix products, arithmetic and copies ran while one was open for 1% -> 1% of each run, Pallas kernels for 19% -> 19%
where the time goes in v3:
time: 63.2 us; the launch traced here: 62.6 us
  Pallas kernels  32 us (51%)
  starting transfers between devices  16 us (25%)
  waiting for transfers between devices  12 us (19%)
  between operations  0.96 us (2%)
  other arithmetic  0.76 us (1%)
  local copies, waits for them, and re-layouts  0.75 us (1%)
    pallas_call x3, Pallas kernels, pair_call(): pl.pallas_call(lambda *refs: pair_kernel(cfg, *refs), out_shape=tuple(out...  29.3 us
    ppermute x3, starting transfers between devices, body(): lax.ppermute(tiles[k], 'gx', ring(nx, -k))  5.02 us
    ppermute x3, starting transfers between devices, body(): lax.ppermute(total, axis, [(i, i ^ 1 << bit) for i in range(count)])  4.6 us
    ppermute x3, waiting for transfers between devices, body(): lax.ppermute(total, axis, [(i, i ^ 1 << bit) for i in range(count)])  3.95 us
    ppermute x3, waiting for transfers between devices, body(): lax.ppermute(tiles[k], 'gx', ring(nx, -k))  3.76 us
    ppermute x1, starting transfers between devices, body(): above = lax.ppermute(bottom, axes, towards(1, 0))  3.66 us
    ppermute x3, waiting for transfers between devices, body(): lax.ppermute(sums[k], 'gx', ring(nx, k))  3.12 us
    pallas_call x1, Pallas kernels, body(): pl.pallas_call(lambda *refs: pack_kernel(pz, tz, *refs), out_shape=(shape...  2.35 us
  transfers between devices with their start and end apart: 13, of which 8 were waited for; matrix products, arithmetic and copies ran while one was open for 1% of the time, Pallas kernels for 19%

profile of v3, /device:TPU:0, one launch (start us, length us, event | category | flops | bytes accessed | tf_op | source)
XLA Modules:
  0.0 62.6 jit_solution(6592291552742510789)
XLA Ops:
  0.6 2.4 %pack.1 = (f32[4,32,128]{2,1,0:T(8,128)}, f32[8,128]{1,0:T(8,128)}, f32[1,8,8,128]{3,2,1,0:T(8,128)}, f32[1,8,8,128]{3,2,1,0:T(8,128)}, f32[1,8,8,128]{3,2,1,0:T(8,128)}, /*index=5*/f32[1,8,8,128]{3,2,1,0:T(8,128)}) custom-call(f32[3,32,128]{2,1,0:T(8,128)} %bitcast.108, f32[6,32,128]{2,1,0:T(8,128)} %bitcast.106, s32[32,128]{1,0:T(8,128)} %bitcast.107, ...), custom_call_target="tpu_custom_call" | custom-call | tf_op jit(solution)/shard_map/pack/pallas_call | solution.py:352
  3.0 3.9 %collective-permute-start = (f32[1,8,8,128]{3,2,0,1:T(8,128)}, f32[1,8,8,128]{3,2,0,1:T(8,128)S(1)}, u32[]{:S(2)}, u32[]{:S(2)}) collective-permute-start(f32[1,8,8,128]{3,2,0,1:T(8,128)} %bitcast.116), channel_id=1, source_target_pairs={{0,24},{8,0},{16,8},{24,16},{1,25},{9,1},{17,9},{25,17},{2,26},{10... | collective-permute-start | bytes 98312 | tf_op jit(solution)/shard_map/ppermute | solution.py:369
  6.9 0.5 collective-permute-start.1
  7.4 0.6 collective-permute-start.2
  8.0 0.7 %fusion.16 = (f32[1,1,8,128]{3,2,0,1:T(8,128)S(1)}, f32[1,1,8,128]{3,2,0,1:T(8,128)S(1)}) fusion(f32[1,8,8,128]{3,2,0,1:T(8,128)} %bitcast.95), kind=kLoop, calls=%fused_computation.43 | loop fusion | bytes 16384 | tf_op jit(solution)/shard_map/slice | solution.py:393
  8.7 3.8 %collective-permute-done.2 = f32[1,8,8,128]{3,2,0,1:T(8,128)S(1)} collective-permute-done((f32[1,8,8,128]{3,2,0,1:T(8,128)}, f32[1,8,8,128]{3,2,0,1:T(8,128)S(1)}, u32[]{:S(2)}, u32[]{:S(2)}) %collective-permute-start.2) | collective-permute-done | bytes 32800 | tf_op jit(solution)/shard_map/ppermute | solution.py:369
  12.4 0.0 collective-permute-done.1
  12.4 0.0 collective-permute-done
  12.5 0.0 copy-start
  12.5 0.1 collective-permute-start.3
  12.6 1.2 %collective-permute-done.3 = f32[2,4,1,8,128]{4,3,1,2,0:T(8,128)S(1)} collective-permute-done((f32[2,4,1,8,128]{4,3,1,2,0:T(8,128)S(1)}, f32[2,4,1,8,128]{4,3,1,2,0:T(8,128)S(1)}, u32[]{:S(2)}, u32[]{:S(2)}) %collective-permute-start.3) | collective-permute-done | bytes 32800 | tf_op jit(solution)/shard_map/ppermute | solution.py:396
  13.8 0.0 copy-done
  13.8 3.7 %collective-permute-start.4 = (f32[4,10,8,128]{3,2,0,1:T(8,128)S(1)}, f32[4,10,8,128]{3,2,0,1:T(8,128)S(1)}, u32[]{:S(2)}, u32[]{:S(2)}) collective-permute-start(f32[4,10,8,128]{3,2,0,1:T(8,128)S(1)} %pad_maximum_fusion), channel_id=1, source_target_pairs={{8,0},{9,1},{4,2},{5,3},{12,4},{13,5},{0,6},{1,7},{24,8},{25,9},{2... | collective-permute-start | bytes 491528 | tf_op jit(solution)/shard_map/ppermute | solution.py:402
  17.5 5.8 %early.1 = (f32[4,10,128]{2,1,0:T(8,128)S(1)}, f32[8,128]{1,0:T(8,128)S(1)}) custom-call(f32[1,8,8,128]{3,2,1,0:T(8,128)S(1)} %copy-done, f32[1,8,8,128]{3,2,1,0:T(8,128)S(1)} %bitcast.97, f32[1,8,8,128]{3,2,1,0:T(8,128)S(1)} %bitcast.100, f32[1,8,8,128]{3,2,1,0:T(8,128)S(1)} %bitcast.103, f32[4,1,8,128]{3,2,1,0:T(8,128)S(1)} %get-tuple-element.39.refs_4_, ...), custom_call_target="tpu_custom_call" | custom-call | tf_op jit(solution)/shard_map/early/pallas_call | solution.py:305
  23.3 0.0 collective-permute-done.4
  23.3 17.6 %upper.1 = (f32[4,10,128]{2,1,0:T(8,128)S(1)}, f32[8,128]{1,0:T(8,128)S(1)}, f32[4,10,128]{2,1,0:T(8,128)S(1)}) custom-call(f32[1,8,8,128]{3,2,1,0:T(8,128)S(1)} %copy-done, f32[1,8,8,128]{3,2,1,0:T(8,128)S(1)} %bitcast.98, f32[1,8,8,128]{3,2,1,0:T(8,128)S(1)} %bitcast.101, f32[1,8,8,128]{3,2,1,0:T(8,128)S(1)} %bitcast.104, ...), custom_call_target="tpu_custom_call" | custom-call | tf_op jit(solution)/shard_map/upper/pallas_call | solution.py:305
  40.9 0.1 collective-permute-start.5
  41.1 0.0 copy-start.3
  41.1 5.9 %late.1 = (f32[4,10,128]{2,1,0:T(8,128)S(1)}, f32[8,128]{1,0:T(8,128)S(1)}) custom-call(f32[1,8,8,128]{3,2,1,0:T(8,128)S(1)} %copy-done, f32[1,8,8,128]{3,2,1,0:T(8,128)S(1)} %bitcast.99, f32[1,8,8,128]{3,2,1,0:T(8,128)S(1)} %bitcast.102, f32[1,8,8,128]{3,2,1,0:T(8,128)S(1)} %bitcast.105, f32[4,1,8,128]{3,2,1,0:T(8,128)S(1)} %get-tuple-element.39.refs_4_, ...), custom_call_target="tpu_custom_call" | custom-call | tf_op jit(solution)/shard_map/late/pallas_call | solution.py:305
  47.0 0.0 copy-done.3
  47.0 0.0 collective-permute-done.5
  47.0 0.2 collective-permute-start.8
  47.2 0.4 collective-permute-start.7
  47.6 1.5 %collective-permute-start.6 = (f32[18,128]{1,0:T(8,128)S(1)}, f32[18,128]{1,0:T(8,128)S(1)}, u32[]{:S(2)}, u32[]{:S(2)}) collective-permute-start(f32[18,128]{1,0:T(8,128)S(1)} %get-tuple-element.32), channel_id=1, source_target_pairs={{0,8},{8,16},{16,24},{24,0},{1,9},{9,17},{17,25},{25,1},{2,10},{10... | collective-permute-start | bytes 27656 | tf_op jit(solution)/shard_map/ppermute | solution.py:419
  49.1 1.7 %collective-permute-done.8 = f32[18,128]{1,0:T(8,128)S(1)} collective-permute-done((f32[18,128]{1,0:T(8,128)S(1)}, f32[18,128]{1,0:T(8,128)S(1)}, u32[]{:S(2)}, u32[]{:S(2)}) %collective-permute-start.8) | collective-permute-done | bytes 9248 | tf_op jit(solution)/shard_map/ppermute | solution.py:419
  50.8 0.1 collective-permute-done.7
  50.9 1.4 %collective-permute-done.6 = f32[18,128]{1,0:T(8,128)S(1)} collective-permute-done((f32[18,128]{1,0:T(8,128)S(1)}, f32[18,128]{1,0:T(8,128)S(1)}, u32[]{:S(2)}, u32[]{:S(2)}) %collective-permute-start.6) | collective-permute-done | bytes 9248 | tf_op jit(solution)/shard_map/ppermute | solution.py:419
  52.3 0.0 collective-permute-start.10
  52.3 0.0 copy-start.1
  52.4 0.5 collective-permute-start.9
  52.9 0.5 collective-permute-done.10
  53.4 1.3 %collective-permute-start.11 = (f32[8,128]{1,0:T(8,128)S(1)}, f32[8,128]{1,0:T(8,128)S(1)}, u32[]{:S(2)}, u32[]{:S(2)}) collective-permute-start(f32[8,128]{1,0:T(8,128)S(1)} %add.113), channel_id=1, source_target_pairs={{0,2},{2,0},{4,6},{6,4},{1,3},{3,1},{5,7},{7,5},{8,10},{10,8},{12,... | collective-permute-start | bytes 12296 | tf_op jit(solution)/shard_map/ppermute | solution.py:428
  54.8 0.0 collective-permute-done.9
  54.8 2.3 %collective-permute-done.11 = f32[8,128]{1,0:T(8,128)S(1)} collective-permute-done((f32[8,128]{1,0:T(8,128)S(1)}, f32[8,128]{1,0:T(8,128)S(1)}, u32[]{:S(2)}, u32[]{:S(2)}) %collective-permute-start.11) | collective-permute-done | bytes 4128 | tf_op jit(solution)/shard_map/ppermute | solution.py:428
  57.1 3.3 %collective-permute-start.12 = (f32[8,128]{1,0:T(8,128)S(1)}, f32[8,128]{1,0:T(8,128)S(1)}, u32[]{:S(2)}, u32[]{:S(2)}) collective-permute-start(f32[8,128]{1,0:T(8,128)S(1)} %add.114), channel_id=1, source_target_pairs={{0,4},{2,6},{4,0},{6,2},{1,5},{3,7},{5,1},{7,3},{8,12},{10,14},{12... | collective-permute-start | bytes 12296 | tf_op jit(solution)/shard_map/ppermute | solution.py:428
  60.3 0.0 copy-done.1
  60.3 0.4 unpack.1
  60.7 0.0 copy-start.2
  60.7 1.2 %collective-permute-done.12 = f32[8,128]{1,0:T(8,128)S(1)} collective-permute-done((f32[8,128]{1,0:T(8,128)S(1)}, f32[8,128]{1,0:T(8,128)S(1)}, u32[]{:S(2)}, u32[]{:S(2)}) %collective-permute-start.12) | collective-permute-done | bytes 4128 | tf_op jit(solution)/shard_map/ppermute | solution.py:428
  61.9 0.0 copy-done.2
  61.9 0.6 multiply_bitcast_fusion
  (29 shorter events, 0.2 us)
Async XLA Ops:
  3.0 9.5 %collective-permute-start = (f32[1,8,8,128]{3,2,0,1:T(8,128)}, f32[1,8,8,128]{3,2,0,1:T(8,128)S(1)}, u32[]{:S(2)}, u32[]{:S(2)}) collective-permute-start(f32[1,8,8,128]{3,2,0,1:T(8,128)} %bitcast.116), channel_id=1, source_target_pairs={{0,24},{8,0},{16,8},{24,16},{1,25},{9,1},{17,9},{25,17},{2,26},{10... | collective-permute-start | bytes 98312 | tf_op jit(solution)/shard_map/ppermute | solution.py:369
  6.9 5.5 %collective-permute-start.1 = (f32[1,8,8,128]{3,2,0,1:T(8,128)}, f32[1,8,8,128]{3,2,0,1:T(8,128)S(1)}, u32[]{:S(2)}, u32[]{:S(2)}) collective-permute-start(f32[1,8,8,128]{3,2,0,1:T(8,128)} %bitcast.117), channel_id=1, source_target_pairs={{0,16},{8,24},{16,0},{24,8},{1,17},{9,25},{17,1},{25,9},{2,18},{10... | collective-permute-start | bytes 98312 | tf_op jit(solution)/shard_map/ppermute | solution.py:369
  7.4 5.0 %collective-permute-start.2 = (f32[1,8,8,128]{3,2,0,1:T(8,128)}, f32[1,8,8,128]{3,2,0,1:T(8,128)S(1)}, u32[]{:S(2)}, u32[]{:S(2)}) collective-permute-start(f32[1,8,8,128]{3,2,0,1:T(8,128)} %bitcast.118), channel_id=1, source_target_pairs={{0,8},{8,16},{16,24},{24,0},{1,9},{9,17},{17,25},{25,1},{2,10},{10... | collective-permute-start | bytes 98312 | tf_op jit(solution)/shard_map/ppermute | solution.py:369
  12.5 1.3 %copy-start = (f32[1,8,8,128]{3,2,1,0:T(8,128)S(1)}, f32[1,8,8,128]{3,2,1,0:T(8,128)}, u32[]{:S(2)}) copy-start(f32[1,8,8,128]{3,2,1,0:T(8,128)} %get-tuple-element.16.refs_0_) | copy-start | bytes 98308
  12.5 1.3 %collective-permute-start.3 = (f32[2,4,1,8,128]{4,3,1,2,0:T(8,128)S(1)}, f32[2,4,1,8,128]{4,3,1,2,0:T(8,128)S(1)}, u32[]{:S(2)}, u32[]{:S(2)}) collective-permute-start(f32[2,4,1,8,128]{4,3,1,2,0:T(8,128)S(1)} %pad_maximum_fusion.1), channel_id=1, source_target_pairs={{1,0},{0,1},{3,2},{2,3},{5,4},{4,5},{7,6},{6,7},{9,8},{8,9},{11,10... | collective-permute-start | bytes 98312 | tf_op jit(solution)/shard_map/ppermute | solution.py:396
  13.8 9.5 %collective-permute-start.4 = (f32[4,10,8,128]{3,2,0,1:T(8,128)S(1)}, f32[4,10,8,128]{3,2,0,1:T(8,128)S(1)}, u32[]{:S(2)}, u32[]{:S(2)}) collective-permute-start(f32[4,10,8,128]{3,2,0,1:T(8,128)S(1)} %pad_maximum_fusion), channel_id=1, source_target_pairs={{8,0},{9,1},{4,2},{5,3},{12,4},{13,5},{0,6},{1,7},{24,8},{25,9},{2... | collective-permute-start | bytes 491528 | tf_op jit(solution)/shard_map/ppermute | solution.py:402
  40.9 6.1 %collective-permute-start.5 = (f32[4,10,128]{2,1,0:T(8,128)S(1)}, f32[4,10,128]{2,1,0:T(8,128)S(1)}, u32[]{:S(2)}, u32[]{:S(2)}) collective-permute-start(f32[4,10,128]{2,1,0:T(8,128)S(1)} %get-tuple-element.25), channel_id=1, source_target_pairs={{0,8},{1,9},{2,4},{3,5},{4,12},{5,13},{6,0},{7,1},{8,24},{9,25},{1... | collective-permute-start | bytes 61448 | tf_op jit(solution)/shard_map/ppermute | solution.py:413
  41.1 5.9 %copy-start.3 = (f32[8,128]{1,0:T(8,128)S(1)}, f32[8,128]{1,0:T(8,128)}, u32[]{:S(2)}) copy-start(f32[8,128]{1,0:T(8,128)} %get-tuple-element.26) | copy-start | bytes 12292
  47.0 3.7 %collective-permute-start.8 = (f32[18,128]{1,0:T(8,128)S(1)}, f32[18,128]{1,0:T(8,128)S(1)}, u32[]{:S(2)}, u32[]{:S(2)}) collective-permute-start(f32[18,128]{1,0:T(8,128)S(1)} %get-tuple-element.34), channel_id=1, source_target_pairs={{0,24},{8,0},{16,8},{24,16},{1,25},{9,1},{17,9},{25,17},{2,26},{10... | collective-permute-start | bytes 27656 | tf_op jit(solution)/shard_map/ppermute | solution.py:419
  47.2 3.7 %collective-permute-start.7 = (f32[18,128]{1,0:T(8,128)S(1)}, f32[18,128]{1,0:T(8,128)S(1)}, u32[]{:S(2)}, u32[]{:S(2)}) collective-permute-start(f32[18,128]{1,0:T(8,128)S(1)} %get-tuple-element.33), channel_id=1, source_target_pairs={{0,16},{8,24},{16,0},{24,8},{1,17},{9,25},{17,1},{25,9},{2,18},{10... | collective-permute-start | bytes 27656 | tf_op jit(solution)/shard_map/ppermute | solution.py:419
  47.6 4.6 %collective-permute-start.6 = (f32[18,128]{1,0:T(8,128)S(1)}, f32[18,128]{1,0:T(8,128)S(1)}, u32[]{:S(2)}, u32[]{:S(2)}) collective-permute-start(f32[18,128]{1,0:T(8,128)S(1)} %get-tuple-element.32), channel_id=1, source_target_pairs={{0,8},{8,16},{16,24},{24,0},{1,9},{9,17},{17,25},{25,1},{2,10},{10... | collective-permute-start | bytes 27656 | tf_op jit(solution)/shard_map/ppermute | solution.py:419
  52.3 1.2 %collective-permute-start.10 = (f32[8,128]{1,0:T(8,128)S(1)}, f32[8,128]{1,0:T(8,128)S(1)}, u32[]{:S(2)}, u32[]{:S(2)}) collective-permute-start(f32[8,128]{1,0:T(8,128)S(1)} %slice_add_fusion), channel_id=1, source_target_pairs={{0,1},{1,0},{2,3},{3,2},{4,5},{5,4},{6,7},{7,6},{8,9},{9,8},{10,11... | collective-permute-start | bytes 12296 | tf_op jit(solution)/shard_map/ppermute | solution.py:428
  52.3 8.0 %copy-start.1 = (f32[4,32,128]{2,1,0:T(8,128)S(1)}, f32[4,32,128]{2,1,0:T(8,128)}, u32[]{:S(2)}) copy-start(f32[4,32,128]{2,1,0:T(8,128)} %get-tuple-element.15.aux_ref) | copy-start | bytes 196612
  52.4 2.4 %collective-permute-start.9 = (f32[2,4,128]{2,1,0:T(4,128)S(1)}, f32[2,4,128]{2,1,0:T(4,128)S(1)}, u32[]{:S(2)}, u32[]{:S(2)}) collective-permute-start(f32[2,4,128]{2,1,0:T(4,128)S(1)} %pad_maximum_fusion.3), channel_id=1, source_target_pairs={{0,1},{1,0},{2,3},{3,2},{4,5},{5,4},{6,7},{7,6},{8,9},{9,8},{10,11... | collective-permute-start | bytes 12296 | tf_op jit(solution)/shard_map/ppermute | solution.py:436
  53.4 3.6 %collective-permute-start.11 = (f32[8,128]{1,0:T(8,128)S(1)}, f32[8,128]{1,0:T(8,128)S(1)}, u32[]{:S(2)}, u32[]{:S(2)}) collective-permute-start(f32[8,128]{1,0:T(8,128)S(1)} %add.113), channel_id=1, source_target_pairs={{0,2},{2,0},{4,6},{6,4},{1,3},{3,1},{5,7},{7,5},{8,10},{10,8},{12,... | collective-permute-start | bytes 12296 | tf_op jit(solution)/shard_map/ppermute | solution.py:428
  57.1 4.9 %collective-permute-start.12 = (f32[8,128]{1,0:T(8,128)S(1)}, f32[8,128]{1,0:T(8,128)S(1)}, u32[]{:S(2)}, u32[]{:S(2)}) collective-permute-start(f32[8,128]{1,0:T(8,128)S(1)} %add.114), channel_id=1, source_target_pairs={{0,4},{2,6},{4,0},{6,2},{1,5},{3,7},{5,1},{7,3},{8,12},{10,14},{12... | collective-permute-start | bytes 12296 | tf_op jit(solution)/shard_map/ppermute | solution.py:428
  60.7 1.2 %copy-start.2 = (s32[1,4,8,128]{3,2,1,0:T(8,128)S(1)}, s32[1,4,8,128]{3,2,1,0:T(8,128)}, u32[]{:S(2)}) copy-start(s32[1,4,8,128]{3,2,1,0:T(8,128)} %param.9) | copy-start | bytes 49156

commit v4 on v3

--- a/solution.py
+++ b/solution.py
@@ -13,7 +13,7 @@
 FIELDS = 8
 SHELL_UP = [(a, 1, c) for a in (-1, 0, 1) for c in (-1, 0, 1)]
 SHELL_ROW = [(a, 0, 1) for a in (-1, 0, 1)] + [(1, 0, 0)]
-UP_GROUP, ROW_GROUP = 3, 5
+UP_GROUP, ROW_GROUP = 3, 8
 
 
 def real_root():
@@ -214,13 +214,18 @@
         v = REACH - u
         v = v * v
         v = v * v
+        x = s * u + abc[ai, 3] * bf[3]
+        power = jnp.exp2(jnp.log2(x) * (-1.0 / 3.0))
         poly = (u + ROOT * REACH) * ((s + u) + FREE * REACH * REACH)
-        x = s * u + abc[ai, 3] * bf[3]
-        return (v * poly) * jnp.exp2(jnp.log2(x) * (-1.0 / 3.0))
-
-    def item(t, g):
+        return (v * poly) * power
+
+    def based(t, g):
+        b = listed(t, g)[0]
+        return tuple(base_s[a * (nb + 1) + b] for a in range(3))
+
+    def item(t, g, held):
         b, c = listed(t, g)
-        bases = [base_s[a * (nb + 1) + b] for a in range(3)]
+        bases = held if g == 0 else based(t, g)
         raw = [wide_ref[g, k] for k in range(5)]
         bf = [{o: (raw[k] - o * REACH if o else raw[k]) for o in (-1, 0, 1)} for k in range(3)] + [raw[3]]
         qb = raw[4]
@@ -237,16 +242,16 @@
 
     def step(t, carry):
         for g in range(group):
-            item(t, g)
+            item(t, g, carry[2:])
         for g in range(group):
             prepare(t + 1, g)
-        return extend(t + 2, *carry)
+        return extend(t + 2, *carry[:2]) + based(t + 1, 0)
 
     ahead = extend(1, *extend(0, jnp.int32(0), jnp.int32(0)))
     for g in range(group):
         prepare(0, g)
     steps = (total_chunks + (group - 1)) // group
-    lax.fori_loop(0, steps, step, ahead)
+    lax.fori_loop(0, steps, step, ahead + based(0, 0))
 
     sums = {}
 

time: 63.2 us -> 62.6 us (level)
  Pallas kernels: 32 us -> 31.3 us
    pallas_call x3, Pallas kernels: 29.3 us -> 28.6 us  [pair_call(): pl.pallas_call(lambda *refs: pair_kernel(cfg, *refs), out_shape=tuple(out...]
  transfers between devices with their start and end apart: 13 -> 13, of which waited for: 8 -> 9; matrix products, arithmetic and copies ran while one was open for 1% -> 1% of each run, Pallas kernels for 19% -> 18%
where the time goes in v4:
time: 62.6 us; the launch traced here: 62.3 us
  Pallas kernels  31.3 us (50%)
  starting transfers between devices  16.6 us (27%)
  waiting for transfers between devices  11.9 us (19%)
  between operations  0.95 us (2%)
  other arithmetic  0.76 us (1%)
  local copies, waits for them, and re-layouts  0.74 us (1%)
    pallas_call x3, Pallas kernels, pair_call(): pl.pallas_call(lambda *refs: pair_kernel(cfg, *refs), out_shape=tuple(out...  28.6 us
    ppermute x3, starting transfers between devices, body(): lax.ppermute(total, axis, [(i, i ^ 1 << bit) for i in range(count)])  5.2 us
    ppermute x3, starting transfers between devices, body(): lax.ppermute(tiles[k], 'gx', ring(nx, -k))  5.02 us
    ppermute x3, waiting for transfers between devices, body(): lax.ppermute(total, axis, [(i, i ^ 1 << bit) for i in range(count)])  3.76 us
    ppermute x3, waiting for transfers between devices, body(): lax.ppermute(tiles[k], 'gx', ring(nx, -k))  3.76 us
    ppermute x1, starting transfers between devices, body(): above = lax.ppermute(bottom, axes, towards(1, 0))  3.66 us
    ppermute x3, waiting for transfers between devices, body(): lax.ppermute(sums[k], 'gx', ring(nx, k))  3.12 us
    pallas_call x1, Pallas kernels, body(): pl.pallas_call(lambda *refs: pack_kernel(pz, tz, *refs), out_shape=(shape...  2.35 us
  transfers between devices with their start and end apart: 13, of which 9 were waited for; matrix products, arithmetic and copies ran while one was open for 1% of the time, Pallas kernels for 18%

profile of v4, /device:TPU:0, one launch (start us, length us, event | category | flops | bytes accessed | tf_op | source)
XLA Modules:
  0.0 62.3 jit_solution(3864947104097991396)
XLA Ops:
  0.6 2.4 %pack.1 = (f32[4,32,128]{2,1,0:T(8,128)}, f32[8,128]{1,0:T(8,128)}, f32[1,8,8,128]{3,2,1,0:T(8,128)}, f32[1,8,8,128]{3,2,1,0:T(8,128)}, f32[1,8,8,128]{3,2,1,0:T(8,128)}, /*index=5*/f32[1,8,8,128]{3,2,1,0:T(8,128)}) custom-call(f32[3,32,128]{2,1,0:T(8,128)} %bitcast.108, f32[6,32,128]{2,1,0:T(8,128)} %bitcast.106, s32[32,128]{1,0:T(8,128)} %bitcast.107, ...), custom_call_target="tpu_custom_call" | custom-call | tf_op jit(solution)/shard_map/pack/pallas_call | solution.py:357
  3.0 3.9 %collective-permute-start = (f32[1,8,8,128]{3,2,0,1:T(8,128)}, f32[1,8,8,128]{3,2,0,1:T(8,128)S(1)}, u32[]{:S(2)}, u32[]{:S(2)}) collective-permute-start(f32[1,8,8,128]{3,2,0,1:T(8,128)} %bitcast.116), channel_id=1, source_target_pairs={{0,24},{8,0},{16,8},{24,16},{1,25},{9,1},{17,9},{25,17},{2,26},{10... | collective-permute-start | bytes 98312 | tf_op jit(solution)/shard_map/ppermute | solution.py:374
  6.9 0.5 collective-permute-start.1
  7.4 0.6 collective-permute-start.2
  8.0 0.7 %fusion.16 = (f32[1,1,8,128]{3,2,0,1:T(8,128)S(1)}, f32[1,1,8,128]{3,2,0,1:T(8,128)S(1)}) fusion(f32[1,8,8,128]{3,2,0,1:T(8,128)} %bitcast.95), kind=kLoop, calls=%fused_computation.43 | loop fusion | bytes 16384 | tf_op jit(solution)/shard_map/slice | solution.py:398
  8.7 3.8 %collective-permute-done.2 = f32[1,8,8,128]{3,2,0,1:T(8,128)S(1)} collective-permute-done((f32[1,8,8,128]{3,2,0,1:T(8,128)}, f32[1,8,8,128]{3,2,0,1:T(8,128)S(1)}, u32[]{:S(2)}, u32[]{:S(2)}) %collective-permute-start.2) | collective-permute-done | bytes 32800 | tf_op jit(solution)/shard_map/ppermute | solution.py:374
  12.4 0.0 collective-permute-done.1
  12.4 0.0 collective-permute-done
  12.5 0.0 copy-start
  12.5 0.1 collective-permute-start.3
  12.6 1.2 %collective-permute-done.3 = f32[2,4,1,8,128]{4,3,1,2,0:T(8,128)S(1)} collective-permute-done((f32[2,4,1,8,128]{4,3,1,2,0:T(8,128)S(1)}, f32[2,4,1,8,128]{4,3,1,2,0:T(8,128)S(1)}, u32[]{:S(2)}, u32[]{:S(2)}) %collective-permute-start.3) | collective-permute-done | bytes 32800 | tf_op jit(solution)/shard_map/ppermute | solution.py:401
  13.8 0.0 copy-done
  13.8 3.7 %collective-permute-start.4 = (f32[4,10,8,128]{3,2,0,1:T(8,128)S(1)}, f32[4,10,8,128]{3,2,0,1:T(8,128)S(1)}, u32[]{:S(2)}, u32[]{:S(2)}) collective-permute-start(f32[4,10,8,128]{3,2,0,1:T(8,128)S(1)} %pad_maximum_fusion), channel_id=1, source_target_pairs={{8,0},{9,1},{4,2},{5,3},{12,4},{13,5},{0,6},{1,7},{24,8},{25,9},{2... | collective-permute-start | bytes 491528 | tf_op jit(solution)/shard_map/ppermute | solution.py:407
  17.5 5.6 %early.1 = (f32[4,10,128]{2,1,0:T(8,128)S(1)}, f32[8,128]{1,0:T(8,128)S(1)}) custom-call(f32[1,8,8,128]{3,2,1,0:T(8,128)S(1)} %copy-done, f32[1,8,8,128]{3,2,1,0:T(8,128)S(1)} %bitcast.97, f32[1,8,8,128]{3,2,1,0:T(8,128)S(1)} %bitcast.100, f32[1,8,8,128]{3,2,1,0:T(8,128)S(1)} %bitcast.103, f32[4,1,8,128]{3,2,1,0:T(8,128)S(1)} %get-tuple-element.39.refs_4_, ...), custom_call_target="tpu_custom_call" | custom-call | tf_op jit(solution)/shard_map/early/pallas_call | solution.py:310
  23.0 0.0 collective-permute-done.4
  23.1 17.5 %upper.1 = (f32[4,10,128]{2,1,0:T(8,128)S(1)}, f32[8,128]{1,0:T(8,128)S(1)}, f32[4,10,128]{2,1,0:T(8,128)S(1)}) custom-call(f32[1,8,8,128]{3,2,1,0:T(8,128)S(1)} %copy-done, f32[1,8,8,128]{3,2,1,0:T(8,128)S(1)} %bitcast.98, f32[1,8,8,128]{3,2,1,0:T(8,128)S(1)} %bitcast.101, f32[1,8,8,128]{3,2,1,0:T(8,128)S(1)} %bitcast.104, ...), custom_call_target="tpu_custom_call" | custom-call | tf_op jit(solution)/shard_map/upper/pallas_call | solution.py:310
  40.6 0.1 collective-permute-start.5
  40.8 0.0 copy-start.3
  40.8 5.5 %late.1 = (f32[4,10,128]{2,1,0:T(8,128)S(1)}, f32[8,128]{1,0:T(8,128)S(1)}) custom-call(f32[1,8,8,128]{3,2,1,0:T(8,128)S(1)} %copy-done, f32[1,8,8,128]{3,2,1,0:T(8,128)S(1)} %bitcast.99, f32[1,8,8,128]{3,2,1,0:T(8,128)S(1)} %bitcast.102, f32[1,8,8,128]{3,2,1,0:T(8,128)S(1)} %bitcast.105, f32[4,1,8,128]{3,2,1,0:T(8,128)S(1)} %get-tuple-element.39.refs_4_, ...), custom_call_target="tpu_custom_call" | custom-call | tf_op jit(solution)/shard_map/late/pallas_call | solution.py:310
  46.3 0.0 copy-done.3
  46.3 0.1 collective-permute-done.5
  46.4 0.1 collective-permute-start.8
  46.5 0.3 collective-permute-start.7
  46.8 1.7 %collective-permute-start.6 = (f32[18,128]{1,0:T(8,128)S(1)}, f32[18,128]{1,0:T(8,128)S(1)}, u32[]{:S(2)}, u32[]{:S(2)}) collective-permute-start(f32[18,128]{1,0:T(8,128)S(1)} %get-tuple-element.32), channel_id=1, source_target_pairs={{0,8},{8,16},{16,24},{24,0},{1,9},{9,17},{17,25},{25,1},{2,10},{10... | collective-permute-start | bytes 27656 | tf_op jit(solution)/shard_map/ppermute | solution.py:424
  48.5 1.7 %collective-permute-done.8 = f32[18,128]{1,0:T(8,128)S(1)} collective-permute-done((f32[18,128]{1,0:T(8,128)S(1)}, f32[18,128]{1,0:T(8,128)S(1)}, u32[]{:S(2)}, u32[]{:S(2)}) %collective-permute-start.8) | collective-permute-done | bytes 9248 | tf_op jit(solution)/shard_map/ppermute | solution.py:424
  50.1 0.1 collective-permute-done.7
  50.2 1.4 %collective-permute-done.6 = f32[18,128]{1,0:T(8,128)S(1)} collective-permute-done((f32[18,128]{1,0:T(8,128)S(1)}, f32[18,128]{1,0:T(8,128)S(1)}, u32[]{:S(2)}, u32[]{:S(2)}) %collective-permute-start.6) | collective-permute-done | bytes 9248 | tf_op jit(solution)/shard_map/ppermute | solution.py:424
  51.6 0.0 collective-permute-start.10
  51.7 0.0 copy-start.1
  51.7 0.5 collective-permute-start.9
  52.2 0.5 collective-permute-done.10
  52.8 1.5 %collective-permute-start.11 = (f32[8,128]{1,0:T(8,128)S(1)}, f32[8,128]{1,0:T(8,128)S(1)}, u32[]{:S(2)}, u32[]{:S(2)}) collective-permute-start(f32[8,128]{1,0:T(8,128)S(1)} %add.113), channel_id=1, source_target_pairs={{0,2},{2,0},{4,6},{6,4},{1,3},{3,1},{5,7},{7,5},{8,10},{10,8},{12,... | collective-permute-start | bytes 12296 | tf_op jit(solution)/shard_map/ppermute | solution.py:433
  54.3 0.0 collective-permute-done.9
  54.3 2.1 %collective-permute-done.11 = f32[8,128]{1,0:T(8,128)S(1)} collective-permute-done((f32[8,128]{1,0:T(8,128)S(1)}, f32[8,128]{1,0:T(8,128)S(1)}, u32[]{:S(2)}, u32[]{:S(2)}) %collective-permute-start.11) | collective-permute-done | bytes 4128 | tf_op jit(solution)/shard_map/ppermute | solution.py:433
  56.4 3.7 %collective-permute-start.12 = (f32[8,128]{1,0:T(8,128)S(1)}, f32[8,128]{1,0:T(8,128)S(1)}, u32[]{:S(2)}, u32[]{:S(2)}) collective-permute-start(f32[8,128]{1,0:T(8,128)S(1)} %add.114), channel_id=1, source_target_pairs={{0,4},{2,6},{4,0},{6,2},{1,5},{3,7},{5,1},{7,3},{8,12},{10,14},{12... | collective-permute-start | bytes 12296 | tf_op jit(solution)/shard_map/ppermute | solution.py:433
  60.1 0.0 copy-done.1
  60.1 0.4 unpack.1
  60.5 0.0 copy-start.2
  60.5 1.2 %collective-permute-done.12 = f32[8,128]{1,0:T(8,128)S(1)} collective-permute-done((f32[8,128]{1,0:T(8,128)S(1)}, f32[8,128]{1,0:T(8,128)S(1)}, u32[]{:S(2)}, u32[]{:S(2)}) %collective-permute-start.12) | collective-permute-done | bytes 4128 | tf_op jit(solution)/shard_map/ppermute | solution.py:433
  61.7 0.0 copy-done.2
  61.7 0.6 %multiply_bitcast_fusion = (f32[1,4,8,128]{3,2,1,0:T(8,128)}, f32[1,4,8,128]{3,2,1,0:T(8,128)}) fusion(f32[128]{0:T(128)S(1)} %bitcast.115, f32[32,128]{1,0:T(8,128)S(1)} %unpack.1, f32[4,32,128]{2,1,0:T(8,128)S(1)} %copy-done.1, s32[1,4,8,128]{3,2,1,0:T(8,128)S(1)} %copy-done.2, f32[128]{0:T(128)S(1)} %get-tuple-element.28), kind=kLoop, calls=%fused_computation.13 | loop fusion | flops 40960 | bytes 115712 | tf_op jit(solution)/shard_map/reshape | solution.py:466
  (29 shorter events, 0.2 us)
Async XLA Ops:
  3.0 9.5 %collective-permute-start = (f32[1,8,8,128]{3,2,0,1:T(8,128)}, f32[1,8,8,128]{3,2,0,1:T(8,128)S(1)}, u32[]{:S(2)}, u32[]{:S(2)}) collective-permute-start(f32[1,8,8,128]{3,2,0,1:T(8,128)} %bitcast.116), channel_id=1, source_target_pairs={{0,24},{8,0},{16,8},{24,16},{1,25},{9,1},{17,9},{25,17},{2,26},{10... | collective-permute-start | bytes 98312 | tf_op jit(solution)/shard_map/ppermute | solution.py:374
  6.9 5.5 %collective-permute-start.1 = (f32[1,8,8,128]{3,2,0,1:T(8,128)}, f32[1,8,8,128]{3,2,0,1:T(8,128)S(1)}, u32[]{:S(2)}, u32[]{:S(2)}) collective-permute-start(f32[1,8,8,128]{3,2,0,1:T(8,128)} %bitcast.117), channel_id=1, source_target_pairs={{0,16},{8,24},{16,0},{24,8},{1,17},{9,25},{17,1},{25,9},{2,18},{10... | collective-permute-start | bytes 98312 | tf_op jit(solution)/shard_map/ppermute | solution.py:374
  7.4 5.0 %collective-permute-start.2 = (f32[1,8,8,128]{3,2,0,1:T(8,128)}, f32[1,8,8,128]{3,2,0,1:T(8,128)S(1)}, u32[]{:S(2)}, u32[]{:S(2)}) collective-permute-start(f32[1,8,8,128]{3,2,0,1:T(8,128)} %bitcast.118), channel_id=1, source_target_pairs={{0,8},{8,16},{16,24},{24,0},{1,9},{9,17},{17,25},{25,1},{2,10},{10... | collective-permute-start | bytes 98312 | tf_op jit(solution)/shard_map/ppermute | solution.py:374
  12.5 1.3 %copy-start = (f32[1,8,8,128]{3,2,1,0:T(8,128)S(1)}, f32[1,8,8,128]{3,2,1,0:T(8,128)}, u32[]{:S(2)}) copy-start(f32[1,8,8,128]{3,2,1,0:T(8,128)} %get-tuple-element.16.refs_0_) | copy-start | bytes 98308
  12.5 1.3 %collective-permute-start.3 = (f32[2,4,1,8,128]{4,3,1,2,0:T(8,128)S(1)}, f32[2,4,1,8,128]{4,3,1,2,0:T(8,128)S(1)}, u32[]{:S(2)}, u32[]{:S(2)}) collective-permute-start(f32[2,4,1,8,128]{4,3,1,2,0:T(8,128)S(1)} %pad_maximum_fusion.1), channel_id=1, source_target_pairs={{1,0},{0,1},{3,2},{2,3},{5,4},{4,5},{7,6},{6,7},{9,8},{8,9},{11,10... | collective-permute-start | bytes 98312 | tf_op jit(solution)/shard_map/ppermute | solution.py:401
  13.8 9.2 %collective-permute-start.4 = (f32[4,10,8,128]{3,2,0,1:T(8,128)S(1)}, f32[4,10,8,128]{3,2,0,1:T(8,128)S(1)}, u32[]{:S(2)}, u32[]{:S(2)}) collective-permute-start(f32[4,10,8,128]{3,2,0,1:T(8,128)S(1)} %pad_maximum_fusion), channel_id=1, source_target_pairs={{8,0},{9,1},{4,2},{5,3},{12,4},{13,5},{0,6},{1,7},{24,8},{25,9},{2... | collective-permute-start | bytes 491528 | tf_op jit(solution)/shard_map/ppermute | solution.py:407
  40.6 5.8 %collective-permute-start.5 = (f32[4,10,128]{2,1,0:T(8,128)S(1)}, f32[4,10,128]{2,1,0:T(8,128)S(1)}, u32[]{:S(2)}, u32[]{:S(2)}) collective-permute-start(f32[4,10,128]{2,1,0:T(8,128)S(1)} %get-tuple-element.25), channel_id=1, source_target_pairs={{0,8},{1,9},{2,4},{3,5},{4,12},{5,13},{6,0},{7,1},{8,24},{9,25},{1... | collective-permute-start | bytes 61448 | tf_op jit(solution)/shard_map/ppermute | solution.py:418
  40.8 5.5 %copy-start.3 = (f32[8,128]{1,0:T(8,128)S(1)}, f32[8,128]{1,0:T(8,128)}, u32[]{:S(2)}) copy-start(f32[8,128]{1,0:T(8,128)} %get-tuple-element.26) | copy-start | bytes 12292
  46.4 3.7 %collective-permute-start.8 = (f32[18,128]{1,0:T(8,128)S(1)}, f32[18,128]{1,0:T(8,128)S(1)}, u32[]{:S(2)}, u32[]{:S(2)}) collective-permute-start(f32[18,128]{1,0:T(8,128)S(1)} %get-tuple-element.34), channel_id=1, source_target_pairs={{0,24},{8,0},{16,8},{24,16},{1,25},{9,1},{17,9},{25,17},{2,26},{10... | collective-permute-start | bytes 27656 | tf_op jit(solution)/shard_map/ppermute | solution.py:424
  46.5 3.8 %collective-permute-start.7 = (f32[18,128]{1,0:T(8,128)S(1)}, f32[18,128]{1,0:T(8,128)S(1)}, u32[]{:S(2)}, u32[]{:S(2)}) collective-permute-start(f32[18,128]{1,0:T(8,128)S(1)} %get-tuple-element.33), channel_id=1, source_target_pairs={{0,16},{8,24},{16,0},{24,8},{1,17},{9,25},{17,1},{25,9},{2,18},{10... | collective-permute-start | bytes 27656 | tf_op jit(solution)/shard_map/ppermute | solution.py:424
  46.8 4.8 %collective-permute-start.6 = (f32[18,128]{1,0:T(8,128)S(1)}, f32[18,128]{1,0:T(8,128)S(1)}, u32[]{:S(2)}, u32[]{:S(2)}) collective-permute-start(f32[18,128]{1,0:T(8,128)S(1)} %get-tuple-element.32), channel_id=1, source_target_pairs={{0,8},{8,16},{16,24},{24,0},{1,9},{9,17},{17,25},{25,1},{2,10},{10... | collective-permute-start | bytes 27656 | tf_op jit(solution)/shard_map/ppermute | solution.py:424
  51.6 1.2 %collective-permute-start.10 = (f32[8,128]{1,0:T(8,128)S(1)}, f32[8,128]{1,0:T(8,128)S(1)}, u32[]{:S(2)}, u32[]{:S(2)}) collective-permute-start(f32[8,128]{1,0:T(8,128)S(1)} %slice_add_fusion), channel_id=1, source_target_pairs={{0,1},{1,0},{2,3},{3,2},{4,5},{5,4},{6,7},{7,6},{8,9},{9,8},{10,11... | collective-permute-start | bytes 12296 | tf_op jit(solution)/shard_map/ppermute | solution.py:433
  51.7 8.4 %copy-start.1 = (f32[4,32,128]{2,1,0:T(8,128)S(1)}, f32[4,32,128]{2,1,0:T(8,128)}, u32[]{:S(2)}) copy-start(f32[4,32,128]{2,1,0:T(8,128)} %get-tuple-element.15.aux_ref) | copy-start | bytes 196612
  51.7 2.6 %collective-permute-start.9 = (f32[2,4,128]{2,1,0:T(4,128)S(1)}, f32[2,4,128]{2,1,0:T(4,128)S(1)}, u32[]{:S(2)}, u32[]{:S(2)}) collective-permute-start(f32[2,4,128]{2,1,0:T(4,128)S(1)} %pad_maximum_fusion.3), channel_id=1, source_target_pairs={{0,1},{1,0},{2,3},{3,2},{4,5},{5,4},{6,7},{7,6},{8,9},{9,8},{10,11... | collective-permute-start | bytes 12296 | tf_op jit(solution)/shard_map/ppermute | solution.py:441
  52.8 3.6 %collective-permute-start.11 = (f32[8,128]{1,0:T(8,128)S(1)}, f32[8,128]{1,0:T(8,128)S(1)}, u32[]{:S(2)}, u32[]{:S(2)}) collective-permute-start(f32[8,128]{1,0:T(8,128)S(1)} %add.113), channel_id=1, source_target_pairs={{0,2},{2,0},{4,6},{6,4},{1,3},{3,1},{5,7},{7,5},{8,10},{10,8},{12,... | collective-permute-start | bytes 12296 | tf_op jit(solution)/shard_map/ppermute | solution.py:433
  56.4 5.3 %collective-permute-start.12 = (f32[8,128]{1,0:T(8,128)S(1)}, f32[8,128]{1,0:T(8,128)S(1)}, u32[]{:S(2)}, u32[]{:S(2)}) collective-permute-start(f32[8,128]{1,0:T(8,128)S(1)} %add.114), channel_id=1, source_target_pairs={{0,4},{2,6},{4,0},{6,2},{1,5},{3,7},{5,1},{7,3},{8,12},{10,14},{12... | collective-permute-start | bytes 12296 | tf_op jit(solution)/shard_map/ppermute | solution.py:433
  60.5 1.2 %copy-start.2 = (s32[1,4,8,128]{3,2,1,0:T(8,128)S(1)}, s32[1,4,8,128]{3,2,1,0:T(8,128)}, u32[]{:S(2)}) copy-start(s32[1,4,8,128]{3,2,1,0:T(8,128)} %param.9) | copy-start | bytes 49156

commit v5 on v4

--- a/solution.py
+++ b/solution.py
@@ -425,12 +425,17 @@
     total = gathered[0][rows:]
     for g in gathered[1:]:
         total = total + g[rows:]
-    for axis, count in (("gz", gz), ("gy", gy)):
-        if count & (count - 1):
-            total = lax.psum(total, axis)
-        else:
-            for bit in range(count.bit_length() - 1):
-                total = total + lax.ppermute(total, axis, [(i, i ^ (1 << bit)) for i in range(count)])
+    bits = [("gz", 1 << i) for i in range((gz - 1).bit_length())] + [("gy", 1 << i) for i in range((gy - 1).bit_length())]
+    if gz & (gz - 1) or gy & (gy - 1):
+        total = lax.psum(total, ("gy", "gz"))
+        bits = []
+    while bits:
+        chosen, bits = bits[:2], bits[2:]
+        masks = [bit * (gz if axis == "gy" else 1) for axis, bit in chosen]
+        masks = masks + ([masks[0] | masks[1]] if len(masks) == 2 else [])
+        moved = [lax.ppermute(total, ("gy", "gz"), [(i, i ^ m) for i in range(gy * gz)]) for m in masks]
+        for other in moved:
+            total = total + other
     wide = jnp.zeros((ny, nz + 2, slots), F32)
     for k in range(nx):
         owner = tile_of((me - k) % nx, column, nx)

time: 62.6 us -> 61.6 us (0.984)
  waiting for transfers between devices: 11.9 us -> 10.9 us
    ppermute x3 -> x4, waiting for transfers between devices: 3.76 us -> 2.66 us  [body(): lax.ppermute(total, ('gy', 'gz'), [(i, i ^ m) for i in range(gy * gz)])]
    ppermute x3 -> x4, starting transfers between devices: 5.2 us -> 5.59 us  [body(): lax.ppermute(total, ('gy', 'gz'), [(i, i ^ m) for i in range(gy * gz)])]
  transfers between devices with their start and end apart: 13 -> 14, of which waited for: 9 -> 7; matrix products, arithmetic and copies ran while one was open for 1% -> 1% of each run, Pallas kernels for 18% -> 19%
where the time goes in v5:
time: 61.6 us; the launch traced here: 61.4 us
  Pallas kernels  31.3 us (51%)
  starting transfers between devices  16.7 us (27%)
  waiting for transfers between devices  10.9 us (18%)
  between operations  0.95 us (2%)
  local copies, waits for them, and re-layouts  0.76 us (1%)
  other arithmetic  0.74 us (1%)
    pallas_call x3, Pallas kernels, pair_call(): pl.pallas_call(lambda *refs: pair_kernel(cfg, *refs), out_shape=tuple(out...  28.6 us
    ppermute x4, starting transfers between devices, body(): lax.ppermute(total, ('gy', 'gz'), [(i, i ^ m) for i in range(gy * gz)])  5.59 us
    ppermute x3, starting transfers between devices, body(): lax.ppermute(tiles[k], 'gx', ring(nx, -k))  5.02 us
    ppermute x3, waiting for transfers between devices, body(): lax.ppermute(tiles[k], 'gx', ring(nx, -k))  3.75 us
    ppermute x1, starting transfers between devices, body(): above = lax.ppermute(bottom, axes, towards(1, 0))  3.66 us
    ppermute x3, waiting for transfers between devices, body(): lax.ppermute(sums[k], 'gx', ring(nx, k))  3.26 us
    ppermute x4, waiting for transfers between devices, body(): lax.ppermute(total, ('gy', 'gz'), [(i, i ^ m) for i in range(gy * gz)])  2.66 us
    pallas_call x1, Pallas kernels, body(): pl.pallas_call(lambda *refs: pack_kernel(pz, tz, *refs), out_shape=(shape...  2.36 us
  transfers between devices with their start and end apart: 14, of which 7 were waited for; matrix products, arithmetic and copies ran while one was open for 1% of the time, Pallas kernels for 19%

profile of v5, /device:TPU:0, one launch (start us, length us, event | category | flops | bytes accessed | tf_op | source)
XLA Modules:
  0.0 61.4 jit_solution(17947225649659882382)
XLA Ops:
  0.6 2.4 %pack.1 = (f32[4,32,128]{2,1,0:T(8,128)}, f32[8,128]{1,0:T(8,128)}, f32[1,8,8,128]{3,2,1,0:T(8,128)}, f32[1,8,8,128]{3,2,1,0:T(8,128)}, f32[1,8,8,128]{3,2,1,0:T(8,128)}, /*index=5*/f32[1,8,8,128]{3,2,1,0:T(8,128)}) custom-call(f32[3,32,128]{2,1,0:T(8,128)} %bitcast.108, f32[6,32,128]{2,1,0:T(8,128)} %bitcast.106, s32[32,128]{1,0:T(8,128)} %bitcast.107, ...), custom_call_target="tpu_custom_call" | custom-call | tf_op jit(solution)/shard_map/pack/pallas_call | solution.py:357
  3.0 3.9 %collective-permute-start = (f32[1,8,8,128]{3,2,0,1:T(8,128)}, f32[1,8,8,128]{3,2,0,1:T(8,128)S(1)}, u32[]{:S(2)}, u32[]{:S(2)}) collective-permute-start(f32[1,8,8,128]{3,2,0,1:T(8,128)} %bitcast.116), channel_id=1, source_target_pairs={{0,24},{8,0},{16,8},{24,16},{1,25},{9,1},{17,9},{25,17},{2,26},{10... | collective-permute-start | bytes 98312 | tf_op jit(solution)/shard_map/ppermute | solution.py:374
  6.9 0.5 collective-permute-start.1
  7.4 0.6 collective-permute-start.2
  8.0 0.7 %fusion.16 = (f32[1,1,8,128]{3,2,0,1:T(8,128)S(1)}, f32[1,1,8,128]{3,2,0,1:T(8,128)S(1)}) fusion(f32[1,8,8,128]{3,2,0,1:T(8,128)} %bitcast.95), kind=kLoop, calls=%fused_computation.44 | loop fusion | bytes 16384 | tf_op jit(solution)/shard_map/slice | solution.py:398
  8.7 3.7 %collective-permute-done.2 = f32[1,8,8,128]{3,2,0,1:T(8,128)S(1)} collective-permute-done((f32[1,8,8,128]{3,2,0,1:T(8,128)}, f32[1,8,8,128]{3,2,0,1:T(8,128)S(1)}, u32[]{:S(2)}, u32[]{:S(2)}) %collective-permute-start.2) | collective-permute-done | bytes 32800 | tf_op jit(solution)/shard_map/ppermute | solution.py:374
  12.4 0.0 collective-permute-done.1
  12.5 0.0 collective-permute-done
  12.5 0.0 copy-start
  12.5 0.1 collective-permute-start.3
  12.6 1.2 %collective-permute-done.3 = f32[2,4,1,8,128]{4,3,1,2,0:T(8,128)S(1)} collective-permute-done((f32[2,4,1,8,128]{4,3,1,2,0:T(8,128)S(1)}, f32[2,4,1,8,128]{4,3,1,2,0:T(8,128)S(1)}, u32[]{:S(2)}, u32[]{:S(2)}) %collective-permute-start.3) | collective-permute-done | bytes 32800 | tf_op jit(solution)/shard_map/ppermute | solution.py:401
  13.8 0.0 copy-done
  13.8 3.7 %collective-permute-start.4 = (f32[4,10,8,128]{3,2,0,1:T(8,128)S(1)}, f32[4,10,8,128]{3,2,0,1:T(8,128)S(1)}, u32[]{:S(2)}, u32[]{:S(2)}) collective-permute-start(f32[4,10,8,128]{3,2,0,1:T(8,128)S(1)} %pad_maximum_fusion), channel_id=1, source_target_pairs={{8,0},{9,1},{4,2},{5,3},{12,4},{13,5},{0,6},{1,7},{24,8},{25,9},{2... | collective-permute-start | bytes 491528 | tf_op jit(solution)/shard_map/ppermute | solution.py:407
  17.5 5.4 %early.1 = (f32[4,10,128]{2,1,0:T(8,128)S(1)}, f32[8,128]{1,0:T(8,128)S(1)}) custom-call(f32[1,8,8,128]{3,2,1,0:T(8,128)S(1)} %copy-done, f32[1,8,8,128]{3,2,1,0:T(8,128)S(1)} %bitcast.97, f32[1,8,8,128]{3,2,1,0:T(8,128)S(1)} %bitcast.100, f32[1,8,8,128]{3,2,1,0:T(8,128)S(1)} %bitcast.103, f32[4,1,8,128]{3,2,1,0:T(8,128)S(1)} %get-tuple-element.39.refs_4_, ...), custom_call_target="tpu_custom_call" | custom-call | tf_op jit(solution)/shard_map/early/pallas_call | solution.py:310
  22.8 0.0 collective-permute-done.4
  22.9 17.5 %upper.1 = (f32[4,10,128]{2,1,0:T(8,128)S(1)}, f32[8,128]{1,0:T(8,128)S(1)}, f32[4,10,128]{2,1,0:T(8,128)S(1)}) custom-call(f32[1,8,8,128]{3,2,1,0:T(8,128)S(1)} %copy-done, f32[1,8,8,128]{3,2,1,0:T(8,128)S(1)} %bitcast.98, f32[1,8,8,128]{3,2,1,0:T(8,128)S(1)} %bitcast.101, f32[1,8,8,128]{3,2,1,0:T(8,128)S(1)} %bitcast.104, ...), custom_call_target="tpu_custom_call" | custom-call | tf_op jit(solution)/shard_map/upper/pallas_call | solution.py:310
  40.4 0.1 collective-permute-start.5
  40.6 0.0 copy-start.3
  40.6 5.7 %late.1 = (f32[4,10,128]{2,1,0:T(8,128)S(1)}, f32[8,128]{1,0:T(8,128)S(1)}) custom-call(f32[1,8,8,128]{3,2,1,0:T(8,128)S(1)} %copy-done, f32[1,8,8,128]{3,2,1,0:T(8,128)S(1)} %bitcast.99, f32[1,8,8,128]{3,2,1,0:T(8,128)S(1)} %bitcast.102, f32[1,8,8,128]{3,2,1,0:T(8,128)S(1)} %bitcast.105, f32[4,1,8,128]{3,2,1,0:T(8,128)S(1)} %get-tuple-element.39.refs_4_, ...), custom_call_target="tpu_custom_call" | custom-call | tf_op jit(solution)/shard_map/late/pallas_call | solution.py:310
  46.3 0.0 copy-done.3
  46.3 0.0 collective-permute-done.5
  46.3 0.2 collective-permute-start.8
  46.5 0.6 collective-permute-start.7
  47.1 1.3 %collective-permute-start.6 = (f32[18,128]{1,0:T(8,128)S(1)}, f32[18,128]{1,0:T(8,128)S(1)}, u32[]{:S(2)}, u32[]{:S(2)}) collective-permute-start(f32[18,128]{1,0:T(8,128)S(1)} %get-tuple-element.32), channel_id=1, source_target_pairs={{0,8},{8,16},{16,24},{24,0},{1,9},{9,17},{17,25},{25,1},{2,10},{10... | collective-permute-start | bytes 27656 | tf_op jit(solution)/shard_map/ppermute | solution.py:424
  48.4 1.8 %collective-permute-done.8 = f32[18,128]{1,0:T(8,128)S(1)} collective-permute-done((f32[18,128]{1,0:T(8,128)S(1)}, f32[18,128]{1,0:T(8,128)S(1)}, u32[]{:S(2)}, u32[]{:S(2)}) %collective-permute-start.8) | collective-permute-done | bytes 9248 | tf_op jit(solution)/shard_map/ppermute | solution.py:424
  50.2 0.0 collective-permute-done.7
  50.2 1.5 %collective-permute-done.6 = f32[18,128]{1,0:T(8,128)S(1)} collective-permute-done((f32[18,128]{1,0:T(8,128)S(1)}, f32[18,128]{1,0:T(8,128)S(1)}, u32[]{:S(2)}, u32[]{:S(2)}) %collective-permute-start.6) | collective-permute-done | bytes 9248 | tf_op jit(solution)/shard_map/ppermute | solution.py:424
  51.7 0.0 collective-permute-start.12
  51.7 1.5 %collective-permute-start.11 = (f32[8,128]{1,0:T(8,128)S(1)}, f32[8,128]{1,0:T(8,128)S(1)}, u32[]{:S(2)}, u32[]{:S(2)}) collective-permute-start(f32[8,128]{1,0:T(8,128)S(1)} %slice_add_fusion), channel_id=1, source_target_pairs={{0,2},{1,3},{2,0},{3,1},{4,6},{5,7},{6,4},{7,5},{8,10},{9,11},{10,... | collective-permute-start | bytes 12296 | tf_op jit(solution)/shard_map/ppermute | solution.py:436
  53.2 0.3 collective-permute-start.10
  53.6 0.0 copy-start.1
  53.6 0.2 collective-permute-start.9
  53.9 0.9 %collective-permute-done.12 = f32[8,128]{1,0:T(8,128)S(1)} collective-permute-done((f32[8,128]{1,0:T(8,128)S(1)}, f32[8,128]{1,0:T(8,128)S(1)}, u32[]{:S(2)}, u32[]{:S(2)}) %collective-permute-start.12) | collective-permute-done | bytes 4128 | tf_op jit(solution)/shard_map/ppermute | solution.py:436
  54.8 0.6 collective-permute-done.11
  55.4 0.0 collective-permute-done.10
  55.4 3.7 %collective-permute-start.13 = (f32[8,128]{1,0:T(8,128)S(1)}, f32[8,128]{1,0:T(8,128)S(1)}, u32[]{:S(2)}, u32[]{:S(2)}) collective-permute-start(f32[8,128]{1,0:T(8,128)S(1)} %add_add_fusion), channel_id=1, source_target_pairs={{0,4},{1,5},{2,6},{3,7},{4,0},{5,1},{6,2},{7,3},{8,12},{9,13},{10,... | collective-permute-start | bytes 12296 | tf_op jit(solution)/shard_map/ppermute | solution.py:436
  59.1 0.0 collective-permute-done.9
  59.2 0.0 copy-done.1
  59.2 0.4 unpack.1
  59.6 0.0 copy-start.2
  59.6 1.1 %collective-permute-done.13 = f32[8,128]{1,0:T(8,128)S(1)} collective-permute-done((f32[8,128]{1,0:T(8,128)S(1)}, f32[8,128]{1,0:T(8,128)S(1)}, u32[]{:S(2)}, u32[]{:S(2)}) %collective-permute-start.13) | collective-permute-done | bytes 4128 | tf_op jit(solution)/shard_map/ppermute | solution.py:436
  60.7 0.0 copy-done.2
  60.7 0.6 %multiply_bitcast_fusion = (f32[1,4,8,128]{3,2,1,0:T(8,128)}, f32[1,4,8,128]{3,2,1,0:T(8,128)}) fusion(f32[128]{0:T(128)S(1)} %bitcast.115, f32[32,128]{1,0:T(8,128)S(1)} %unpack.1, f32[4,32,128]{2,1,0:T(8,128)S(1)} %copy-done.1, s32[1,4,8,128]{3,2,1,0:T(8,128)S(1)} %copy-done.2, f32[128]{0:T(128)S(1)} %get-tuple-element.28), kind=kLoop, calls=%fused_computation.13 | loop fusion | flops 40960 | bytes 115712 | tf_op jit(solution)/shard_map/reshape | solution.py:471
  (28 shorter events, 0.2 us)
Async XLA Ops:
  3.0 9.5 %collective-permute-start = (f32[1,8,8,128]{3,2,0,1:T(8,128)}, f32[1,8,8,128]{3,2,0,1:T(8,128)S(1)}, u32[]{:S(2)}, u32[]{:S(2)}) collective-permute-start(f32[1,8,8,128]{3,2,0,1:T(8,128)} %bitcast.116), channel_id=1, source_target_pairs={{0,24},{8,0},{16,8},{24,16},{1,25},{9,1},{17,9},{25,17},{2,26},{10... | collective-permute-start | bytes 98312 | tf_op jit(solution)/shard_map/ppermute | solution.py:374
  6.9 5.5 %collective-permute-start.1 = (f32[1,8,8,128]{3,2,0,1:T(8,128)}, f32[1,8,8,128]{3,2,0,1:T(8,128)S(1)}, u32[]{:S(2)}, u32[]{:S(2)}) collective-permute-start(f32[1,8,8,128]{3,2,0,1:T(8,128)} %bitcast.117), channel_id=1, source_target_pairs={{0,16},{8,24},{16,0},{24,8},{1,17},{9,25},{17,1},{25,9},{2,18},{10... | collective-permute-start | bytes 98312 | tf_op jit(solution)/shard_map/ppermute | solution.py:374
  7.4 5.0 %collective-permute-start.2 = (f32[1,8,8,128]{3,2,0,1:T(8,128)}, f32[1,8,8,128]{3,2,0,1:T(8,128)S(1)}, u32[]{:S(2)}, u32[]{:S(2)}) collective-permute-start(f32[1,8,8,128]{3,2,0,1:T(8,128)} %bitcast.118), channel_id=1, source_target_pairs={{0,8},{8,16},{16,24},{24,0},{1,9},{9,17},{17,25},{25,1},{2,10},{10... | collective-permute-start | bytes 98312 | tf_op jit(solution)/shard_map/ppermute | solution.py:374
  12.5 1.3 %copy-start = (f32[1,8,8,128]{3,2,1,0:T(8,128)S(1)}, f32[1,8,8,128]{3,2,1,0:T(8,128)}, u32[]{:S(2)}) copy-start(f32[1,8,8,128]{3,2,1,0:T(8,128)} %get-tuple-element.16.refs_0_) | copy-start | bytes 98308
  12.5 1.3 %collective-permute-start.3 = (f32[2,4,1,8,128]{4,3,1,2,0:T(8,128)S(1)}, f32[2,4,1,8,128]{4,3,1,2,0:T(8,128)S(1)}, u32[]{:S(2)}, u32[]{:S(2)}) collective-permute-start(f32[2,4,1,8,128]{4,3,1,2,0:T(8,128)S(1)} %pad_maximum_fusion.1), channel_id=1, source_target_pairs={{1,0},{0,1},{3,2},{2,3},{5,4},{4,5},{7,6},{6,7},{9,8},{8,9},{11,10... | collective-permute-start | bytes 98312 | tf_op jit(solution)/shard_map/ppermute | solution.py:401
  13.8 9.0 %collective-permute-start.4 = (f32[4,10,8,128]{3,2,0,1:T(8,128)S(1)}, f32[4,10,8,128]{3,2,0,1:T(8,128)S(1)}, u32[]{:S(2)}, u32[]{:S(2)}) collective-permute-start(f32[4,10,8,128]{3,2,0,1:T(8,128)S(1)} %pad_maximum_fusion), channel_id=1, source_target_pairs={{8,0},{9,1},{4,2},{5,3},{12,4},{13,5},{0,6},{1,7},{24,8},{25,9},{2... | collective-permute-start | bytes 491528 | tf_op jit(solution)/shard_map/ppermute | solution.py:407
  40.4 5.9 %collective-permute-start.5 = (f32[4,10,128]{2,1,0:T(8,128)S(1)}, f32[4,10,128]{2,1,0:T(8,128)S(1)}, u32[]{:S(2)}, u32[]{:S(2)}) collective-permute-start(f32[4,10,128]{2,1,0:T(8,128)S(1)} %get-tuple-element.25), channel_id=1, source_target_pairs={{0,8},{1,9},{2,4},{3,5},{4,12},{5,13},{6,0},{7,1},{8,24},{9,25},{1... | collective-permute-start | bytes 61448 | tf_op jit(solution)/shard_map/ppermute | solution.py:418
  40.6 5.7 %copy-start.3 = (f32[8,128]{1,0:T(8,128)S(1)}, f32[8,128]{1,0:T(8,128)}, u32[]{:S(2)}) copy-start(f32[8,128]{1,0:T(8,128)} %get-tuple-element.26) | copy-start | bytes 12292
  46.3 3.8 %collective-permute-start.8 = (f32[18,128]{1,0:T(8,128)S(1)}, f32[18,128]{1,0:T(8,128)S(1)}, u32[]{:S(2)}, u32[]{:S(2)}) collective-permute-start(f32[18,128]{1,0:T(8,128)S(1)} %get-tuple-element.34), channel_id=1, source_target_pairs={{0,24},{8,0},{16,8},{24,16},{1,25},{9,1},{17,9},{25,17},{2,26},{10... | collective-permute-start | bytes 27656 | tf_op jit(solution)/shard_map/ppermute | solution.py:424
  46.5 3.7 %collective-permute-start.7 = (f32[18,128]{1,0:T(8,128)S(1)}, f32[18,128]{1,0:T(8,128)S(1)}, u32[]{:S(2)}, u32[]{:S(2)}) collective-permute-start(f32[18,128]{1,0:T(8,128)S(1)} %get-tuple-element.33), channel_id=1, source_target_pairs={{0,16},{8,24},{16,0},{24,8},{1,17},{9,25},{17,1},{25,9},{2,18},{10... | collective-permute-start | bytes 27656 | tf_op jit(solution)/shard_map/ppermute | solution.py:424
  47.1 4.6 %collective-permute-start.6 = (f32[18,128]{1,0:T(8,128)S(1)}, f32[18,128]{1,0:T(8,128)S(1)}, u32[]{:S(2)}, u32[]{:S(2)}) collective-permute-start(f32[18,128]{1,0:T(8,128)S(1)} %get-tuple-element.32), channel_id=1, source_target_pairs={{0,8},{8,16},{16,24},{24,0},{1,9},{9,17},{17,25},{25,1},{2,10},{10... | collective-permute-start | bytes 27656 | tf_op jit(solution)/shard_map/ppermute | solution.py:424
  51.7 3.1 %collective-permute-start.12 = (f32[8,128]{1,0:T(8,128)S(1)}, f32[8,128]{1,0:T(8,128)S(1)}, u32[]{:S(2)}, u32[]{:S(2)}) collective-permute-start(f32[8,128]{1,0:T(8,128)S(1)} %slice_add_fusion), channel_id=1, source_target_pairs={{0,3},{1,2},{2,1},{3,0},{4,7},{5,6},{6,5},{7,4},{8,11},{9,10},{10,... | collective-permute-start | bytes 12296 | tf_op jit(solution)/shard_map/ppermute | solution.py:436
  51.7 3.7 %collective-permute-start.11 = (f32[8,128]{1,0:T(8,128)S(1)}, f32[8,128]{1,0:T(8,128)S(1)}, u32[]{:S(2)}, u32[]{:S(2)}) collective-permute-start(f32[8,128]{1,0:T(8,128)S(1)} %slice_add_fusion), channel_id=1, source_target_pairs={{0,2},{1,3},{2,0},{3,1},{4,6},{5,7},{6,4},{7,5},{8,10},{9,11},{10,... | collective-permute-start | bytes 12296 | tf_op jit(solution)/shard_map/ppermute | solution.py:436
  53.2 2.2 %collective-permute-start.10 = (f32[8,128]{1,0:T(8,128)S(1)}, f32[8,128]{1,0:T(8,128)S(1)}, u32[]{:S(2)}, u32[]{:S(2)}) collective-permute-start(f32[8,128]{1,0:T(8,128)S(1)} %slice_add_fusion), channel_id=1, source_target_pairs={{0,1},{1,0},{2,3},{3,2},{4,5},{5,4},{6,7},{7,6},{8,9},{9,8},{10,11... | collective-permute-start | bytes 12296 | tf_op jit(solution)/shard_map/ppermute | solution.py:436
  53.6 5.6 %copy-start.1 = (f32[4,32,128]{2,1,0:T(8,128)S(1)}, f32[4,32,128]{2,1,0:T(8,128)}, u32[]{:S(2)}) copy-start(f32[4,32,128]{2,1,0:T(8,128)} %get-tuple-element.15.aux_ref) | copy-start | bytes 196612
  53.6 5.5 %collective-permute-start.9 = (f32[2,4,128]{2,1,0:T(4,128)S(1)}, f32[2,4,128]{2,1,0:T(4,128)S(1)}, u32[]{:S(2)}, u32[]{:S(2)}) collective-permute-start(f32[2,4,128]{2,1,0:T(4,128)S(1)} %pad_maximum_fusion.3), channel_id=1, source_target_pairs={{0,1},{1,0},{2,3},{3,2},{4,5},{5,4},{6,7},{7,6},{8,9},{9,8},{10,11... | collective-permute-start | bytes 12296 | tf_op jit(solution)/shard_map/ppermute | solution.py:446
  55.4 5.3 %collective-permute-start.13 = (f32[8,128]{1,0:T(8,128)S(1)}, f32[8,128]{1,0:T(8,128)S(1)}, u32[]{:S(2)}, u32[]{:S(2)}) collective-permute-start(f32[8,128]{1,0:T(8,128)S(1)} %add_add_fusion), channel_id=1, source_target_pairs={{0,4},{1,5},{2,6},{3,7},{4,0},{5,1},{6,2},{7,3},{8,12},{9,13},{10,... | collective-permute-start | bytes 12296 | tf_op jit(solution)/shard_map/ppermute | solution.py:436
  59.6 1.2 %copy-start.2 = (s32[1,4,8,128]{3,2,1,0:T(8,128)S(1)}, s32[1,4,8,128]{3,2,1,0:T(8,128)}, u32[]{:S(2)}) copy-start(s32[1,4,8,128]{3,2,1,0:T(8,128)} %param.9) | copy-start | bytes 49156
